TPU v7x, 32 devices: a whole 2x2x4 slice. The times are simulated.
32 devices in a mesh: node: 16 (over z, x, core), tone: 2 (over y).
Axes of the slice: x: 2, y: 2, z: 4, core: 2. Of those that a mesh axis runs over, the one named last changes fastest.
Arguments:
- voltages: float32 [32, 32, 16384], P(None, 'tone', 'node'), may hold values from -6 to 6
- source: float32 [32, 32, 16384], P(None, 'tone', 'node'), may hold values from -6 to 6
- coupling: float32 [128, 7, 128, 128], P('node'), may hold values from -0.1875 to 0.1875
- band_code: int32 [7], replicated, may hold values from 0 to 6, each once
- active: int32 [128, 7], P('node'), may hold values 0 or 1
- cap: float32 [16384], P('node'), may hold values from 0.5 to 2
- damp: float32 [32, 32], P(None, 'tone'), may hold values from 0.5 to 4
- kind: int32 [16384], P('node'), may hold values from 0 to 3
- type_params: float32 [3, 4], replicated, may hold values from 0.3 to 2
Outputs:
- new_voltages: float32 [32, 32, 16384], P(None, 'tone', 'node')
- remaining: float32 [32, 32, 16384], P(None, 'tone', 'node')
Inputs may be any that keep to these rules, and one draw needn't show every extreme that they name: band_code holds each of 0 to 6 once, so the bands reach every block offset from -3 to 3.
All inputs are finite; a program needn't handle non-finite values. No bound on the sum of `active` on one device may be relied on, other than what follows from the above.
Results may differ from a plain program's by a relative error of at most 0.0003.
Values sent between devices are 32-bit elements; how exact they have to be, the bound alone decides.
No kernel may reach another device: no remote copies, remote signals or barrier semaphores. Data moves between devices by JAX's collectives and lax.ppermute only.
A program may use at most 128 MiB of HBM per device.

v0:
```python
import math

import jax
import jax.numpy as jnp
from jax import lax
from jax.sharding import PartitionSpec as P

K1 = 32
K2 = 32
NB = 128
HALO_B = 3
NOFF = 7
M = 4
NTYPES = 4


HIGH = lax.Precision.HIGHEST


def extended(value, sides, width):
    for axis, dim in sides:
        count, length = (lax.axis_size(axis), value.shape[dim])
        up = [(i, (i + 1) % count) for i in range(count - 1)]
        down = [(j, i) for i, j in up]
        last = lax.slice_in_dim(value, length - width, length, axis=dim)
        leading = lax.slice_in_dim(value, 0, width, axis=dim)
        before = lax.ppermute(last, axis, up)
        after = lax.ppermute(leading, axis, down)
        value = jnp.concatenate([before, value, after], axis=dim)
    return value


def hartley(count):
    grid = jnp.arange(count, dtype=jnp.int32)
    phase = grid[:, None] * grid[None, :] % count
    angle = phase.astype(jnp.float32) * (2.0 * math.pi / count)
    return (jnp.cos(angle) + jnp.sin(angle)) / math.sqrt(count)


def along_first(table, field):
    return jnp.einsum("tk,kqn->tqn", table, field, precision=HIGH)


def along_second(table, field):
    return jnp.einsum("sq,tqn->tsn", table, field, precision=HIGH)


def band_matrix(masked, band_code, nodes):
    blocks = nodes // NB
    reach = HALO_B * NB
    offsets = jnp.arange(NOFF, dtype=jnp.int32)
    select = (offsets[:, None] == band_code[None, :]).astype(jnp.float32)
    per_offset = jnp.einsum("oj,bjsc->obsc", select, masked, precision=HIGH)
    diagonal = jnp.eye(blocks, dtype=jnp.float32)
    operator = jnp.zeros((nodes + 2 * reach, nodes), dtype=jnp.float32)
    for offset in range(NOFF):
        placed = jnp.einsum("bsc,bd->bcds", per_offset[offset], diagonal).reshape(nodes, nodes)
        operator = operator.at[offset * NB : offset * NB + nodes].add(placed)
    return operator


def couple(field, operator, scale):
    reach = HALO_B * NB
    padded = extended(field, (("node", 2),), reach)
    rows = field.shape[0] * field.shape[1]
    term = jnp.dot(padded.reshape(rows, padded.shape[2]), operator, precision=HIGH)
    return scale * field + term.reshape(field.shape)


def small_solve(gram, rhs):
    lower = jnp.linalg.cholesky(gram)
    count = rhs.shape[0]
    forward = []
    for index in range(count):
        total = rhs[index]
        for other in range(index):
            total = total - lower[index, other] * forward[other]
        forward.append(total / lower[index, index])
    backward = [None] * count
    for index in reversed(range(count)):
        total = forward[index]
        for other in range(index + 1, count):
            total = total - lower[other, index] * backward[other]
        backward[index] = total / lower[index, index]
    return jnp.stack(backward)


def per_device(voltages, source, coupling, band_code, active, cap, damp, kind, type_params):
    first = hartley(K1)
    second = hartley(K2)
    onehot = (kind[None, :] == jnp.arange(NTYPES, dtype=jnp.int32)[:, None]).astype(jnp.float32)
    per_node = jnp.dot(type_params, onehot, precision=HIGH)
    masked = coupling * active[:, :, None, None].astype(jnp.float32)
    operator = band_matrix(masked, band_code, voltages.shape[2])
    scale = damp[:, :, None] * cap[None, None, :]

    def to_time(field):
        moved = lax.all_to_all(
            along_first(first, field), "tone", split_axis=0, concat_axis=1, tiled=True
        )
        return along_second(second, moved)

    def to_freq(field):
        moved = lax.all_to_all(
            along_second(second, field), "tone", split_axis=1, concat_axis=0, tiled=True
        )
        return along_first(first, moved)

    linear, amplitude, sharpness = (per_node[0], per_node[1], per_node[2])
    wave = to_time(voltages)
    bend = jnp.tanh(sharpness * wave)
    current = linear * wave + amplitude * bend
    slope = linear + amplitude * sharpness * (1.0 - bend * bend)
    start = source - couple(voltages, operator, scale) - to_freq(current)
    beta = jnp.sqrt(lax.psum(jnp.sum(start * start), ("node", "tone")))
    basis = [start / beta]
    hessen = jnp.zeros((M + 1, M), dtype=jnp.float32)
    for column in range(M):
        jacobian_field = basis[column]
        image = couple(jacobian_field, operator, scale) + to_freq(slope * to_time(jacobian_field))
        local_terms = jnp.stack([jnp.sum(vector * image) for vector in basis])
        projected = lax.psum(local_terms, ("node", "tone"))
        for index in range(len(basis)):
            image = image - projected[index] * basis[index]
        length = jnp.sqrt(lax.psum(jnp.sum(image * image), ("node", "tone")))
        hessen = hessen.at[: column + 1, column].set(projected)
        hessen = hessen.at[column + 1, column].set(length)
        basis.append(image / length)
    gram = jnp.dot(hessen.T, hessen, precision=HIGH)
    coeffs = small_solve(gram, beta * hessen[0])
    fitted = jnp.dot(hessen, coeffs, precision=HIGH)
    update = coeffs[0] * basis[0]
    for index in range(1, M):
        update = update + coeffs[index] * basis[index]
    remaining = start
    for index in range(M + 1):
        remaining = remaining - fitted[index] * basis[index]
    return (voltages + update, remaining)


def solution(mesh):
    placed = (
        P(None, "tone", "node"),
        P(None, "tone", "node"),
        P("node", None, None, None),
        P(),
        P("node", None),
        P("node"),
        P(None, "tone"),
        P("node"),
        P(),
    )
    return jax.shard_map(
        per_device,
        mesh=mesh,
        in_specs=placed,
        out_specs=(P(None, "tone", "node"), P(None, "tone", "node")),
        check_vma=False,
    )
```

profile of v0, /device:TPU:0, one launch (start us, length us, event | category | flops | bytes accessed | tf_op | source)
XLA Modules:
  0.0 942.5 jit_solution(3432726177361847667)
XLA Ops:
  0.6 4.6 fusion.72
  7.8 5.0 all-to-all-start
  21.3 4.1 fusion.16
  25.4 4.2 fusion.273
  33.9 9.7 %broadcast_multiply_fusion = (f32[8,8,128,128]{2,1,3,0:T(8,128)}, f32[8,8,128,128]{2,1,3,0:T(8,128)}, f32[8,8,128,128]{2,1,3,0:T(8,128)}, f32[8,8,128,128]{2,1,3...) fusion(f32[8,128,128]{1,2,0:T(8,128)} %copy.111, ...), kind=kLoop, calls=%fused_computation.116 | loop fusion | flops 7340032 | bytes 33030400 | tf_op jit(solution)/shard_map/bsc,bd->bcds/dot_general | solution.py:57
  46.8 6.3 scatter-add.24
  53.2 5.8 fusion.15
  59.0 5.9 fusion.14
  64.9 5.9 fusion.13
  70.8 5.7 fusion.12
  86.0 3.8 all-to-all-start.1
  89.8 7.2 fusion.11
  97.0 5.7 fusion.10
  102.7 12.3 %all-to-all-done.1 = f32[16,32,1024]{2,0,1:T(8,128)S(1)} async-done(((f32[16,32,1024]{2,0,1:T(8,128)}), f32[16,32,1024]{2,0,1:T(8,128)S(1)}, u32[]{:S(2)}, u32[]{:S(2)}) %all-to-all-start.1) | async-done | bytes 2097184 | tf_op jit(solution)/shard_map/all_to_all | solution.py:104
  117.3 17.0 %multiply_reduce_fusion.14 = (f32[]{:T(128)}, f32[32,16,1024]{2,1,0:T(8,128)S(1)}) fusion(f32[32,16,1024]{2,0,1:T(8,128)S(1)} %fusion.146, f32[32,16,1024]{2,1,0:T(8,128)S(1)} %copy-done.30, f32[1792,1024]{1,0:T(8,128)} %fusion.10, f32[32,16,384]{2,1,0:T(8,128)} %collective-permute-done.1, f32[32,16,1024]{2,1,0:T(8,128)S(1)} %copy-done.16, ...), kind=kOutput, calls=%fused_computation.111 | convolution fusion | flops 11279794176 | bytes 17307652 | tf_op jit(solution)/shard_map/dot_general | solution.py:66
  134.3 42.4 %psum.63 = f32[]{:T(128)} all-reduce(f32[]{:T(128)} %get-tuple-element.256), channel_id=1, replica_groups=mesh['node'=16,'tone'=2] {'node','tone'}, use_global_device_ids=true, to_apply=%region_1.2 | all-reduce | flops 1 | bytes 8 | tf_op jit(solution)/shard_map/psum | solution.py:115
  183.2 5.0 all-to-all-start.2
  188.2 25.1 %all-to-all-done.2 = f32[32,16,1024]{2,1,0:T(8,128)} async-done(((f32[32,16,1024]{2,1,0:T(8,128)}), f32[32,16,1024]{2,1,0:T(8,128)}, u32[]{:S(2)}, u32[]{:S(2)}) %all-to-all-start.2) | async-done | bytes 2097184 | tf_op jit(solution)/shard_map/all_to_all | solution.py:98
  222.5 4.8 all-to-all-start.3
  233.6 17.5 %all-to-all-done.3 = f32[16,32,1024]{2,0,1:T(8,128)} async-done(((f32[16,32,1024]{2,0,1:T(8,128)}), f32[16,32,1024]{2,0,1:T(8,128)}, u32[]{:S(2)}, u32[]{:S(2)}) %all-to-all-start.3) | async-done | bytes 2097184 | tf_op jit(solution)/shard_map/all_to_all | solution.py:104
  254.8 17.5 %multiply_reduce_fusion.13 = (f32[]{:T(128)}, f32[32,16,1024]{2,1,0:T(8,128)}) fusion(f32[32,16,1024]{2,1,0:T(8,128)S(1)} %get-tuple-element.257, f32[]{:T(128)S(6)} %sqrt.15, f32[32,16,1024]{2,0,1:T(8,128)S(1)} %fusion.140, f32[1792,1024]{1,0:T(8,128)} %fusion.10, f32[32,16,384]{2,1,0:T(8,128)} %collective-permute-done.3, ...), kind=kOutput, calls=%fused_computation.110 | convolution fusion | flops 11279794176 | bytes 17307656 | tf_op jit(solution)/shard_map/dot_general | solution.py:66
  272.3 38.9 %psum.64 = f32[1]{0:T(128)} all-reduce(f32[1]{0:T(128)} %bitcast.38), channel_id=1, replica_groups=mesh['node'=16,'tone'=2] {'node','tone'}, use_global_device_ids=true, to_apply=%region_3.4 | all-reduce | flops 1 | bytes 8 | tf_op jit(solution)/shard_map/psum | solution.py:122
  311.2 3.4 multiply_reduce_fusion.12
  314.6 41.2 %psum.65 = f32[]{:T(128)} all-reduce(f32[]{:T(128)} %multiply_reduce_fusion.12), channel_id=1, replica_groups=mesh['node'=16,'tone'=2] {'node','tone'}, use_global_device_ids=true, to_apply=%region_5.6 | all-reduce | flops 1 | bytes 8 | tf_op jit(solution)/shard_map/psum | solution.py:125
  363.6 27.1 %all_to_all.180 = f32[32,16,1024]{2,1,0:T(8,128)S(1)} all-to-all(f32[32,16,1024]{2,1,0:T(8,128)S(1)} %copy.125), channel_id=1, replica_groups=mesh['node'=16,'tone'=2] {'tone'}, dimensions={0} | all-to-all | bytes 4194304 | tf_op jit(solution)/shard_map/all_to_all | solution.py:98
  398.4 4.8 all-to-all-start.5
  409.3 16.6 %all-to-all-done.5 = f32[16,32,1024]{2,0,1:T(8,128)} async-done(((f32[16,32,1024]{2,0,1:T(8,128)}), f32[16,32,1024]{2,0,1:T(8,128)}, u32[]{:S(2)}, u32[]{:S(2)}) %all-to-all-start.5) | async-done | bytes 2097184 | tf_op jit(solution)/shard_map/all_to_all | solution.py:104
  429.6 17.6 %multiply_reduce_fusion.11 = (f32[]{:T(128)}, f32[]{:T(128)}, f32[32,16,1024]{2,1,0:T(8,128)}) fusion(f32[32,16,1024]{2,1,0:T(8,128)S(1)} %get-tuple-element.257, f32[]{:T(128)S(6)} %sqrt.15, f32[32,16,1024]{2,1,0:T(8,128)S(1)} %copy-done.3, f32[32,16,1024]{2,0,1:T(8,128)S(1)} %fusion.134, f32[1792,1024]{1,0:T(8,128)} %fusion.10, ...), kind=kOutput, calls=%fused_computation.107 | convolution fusion | flops 11280842752 | bytes 17307660 | tf_op jit(solution)/shard_map/dot_general | solution.py:66
  448.6 38.6 %psum.66 = f32[2]{0:T(128)S(1)} all-reduce(f32[2]{0:T(128)S(1)} %pad_maximum_fusion), channel_id=1, replica_groups=mesh['node'=16,'tone'=2] {'node','tone'}, use_global_device_ids=true, to_apply=%region_9.10 | all-reduce | flops 2 | bytes 16 | tf_op jit(solution)/shard_map/psum | solution.py:122
  487.8 6.2 multiply_reduce_fusion.9
  494.1 40.7 %psum.67 = f32[]{:T(128)} all-reduce(f32[]{:T(128)} %get-tuple-element.193), channel_id=1, replica_groups=mesh['node'=16,'tone'=2] {'node','tone'}, use_global_device_ids=true, to_apply=%region_11.12 | all-reduce | flops 1 | bytes 8 | tf_op jit(solution)/shard_map/psum | solution.py:125
  541.5 27.1 %all_to_all.181 = f32[32,16,1024]{2,1,0:T(8,128)S(1)} all-to-all(f32[32,16,1024]{2,1,0:T(8,128)S(1)} %copy.131), channel_id=1, replica_groups=mesh['node'=16,'tone'=2] {'tone'}, dimensions={0} | all-to-all | bytes 4194304 | tf_op jit(solution)/shard_map/all_to_all | solution.py:98
  576.2 4.8 all-to-all-start.7
  587.1 16.7 %all-to-all-done.7 = f32[16,32,1024]{2,0,1:T(8,128)} async-done(((f32[16,32,1024]{2,0,1:T(8,128)}), f32[16,32,1024]{2,0,1:T(8,128)}, u32[]{:S(2)}, u32[]{:S(2)}) %all-to-all-start.7) | async-done | bytes 2097184 | tf_op jit(solution)/shard_map/all_to_all | solution.py:104
  607.7 17.6 %multiply_reduce_fusion.8 = (f32[]{:T(128)}, f32[]{:T(128)}, f32[]{:T(128)}, f32[32,16,1024]{2,1,0:T(8,128)}) fusion(f32[32,16,1024]{2,1,0:T(8,128)S(1)} %get-tuple-element.257, f32[]{:T(128)S(6)} %sqrt.15, f32[32,16,1024]{2,1,0:T(8,128)S(1)} %copy-done.23, f32[32,16,1024]{2,1,0:T(8,128)S(1)} %copy-done.4, f32[32,16,1024]{2,0,1:T(8,128)S(1)} %fusion.128, ...), kind=kOutput, calls=%fused_computation.103 | convolution fusion | flops 11281891328 | bytes 19404816 | tf_op jit(solution)/shard_map/dot_general | solution.py:66
  627.3 38.9 %psum.68 = f32[3]{0:T(128)S(1)} all-reduce(f32[3]{0:T(128)S(1)} %pad_maximum_fusion.1), channel_id=1, replica_groups=mesh['node'=16,'tone'=2] {'node','tone'}, use_global_device_ids=true, to_apply=%region_16.17 | all-reduce | flops 3 | bytes 24 | tf_op jit(solution)/shard_map/psum | solution.py:122
  666.8 7.7 multiply_reduce_fusion.5
  674.5 41.0 %psum.69 = f32[]{:T(128)} all-reduce(f32[]{:T(128)} %get-tuple-element.191), channel_id=1, replica_groups=mesh['node'=16,'tone'=2] {'node','tone'}, use_global_device_ids=true, to_apply=%region_18.19 | all-reduce | flops 1 | bytes 8 | tf_op jit(solution)/shard_map/psum | solution.py:125
  723.6 5.0 all-to-all-start.8
  730.6 22.6 %all-to-all-done.8 = f32[32,16,1024]{2,1,0:T(8,128)} async-done(((f32[32,16,1024]{2,1,0:T(8,128)}), f32[32,16,1024]{2,1,0:T(8,128)}, u32[]{:S(2)}, u32[]{:S(2)}) %all-to-all-start.8) | async-done | bytes 2097184 | tf_op jit(solution)/shard_map/all_to_all | solution.py:98
  762.3 5.0 all-to-all-start.9
  781.5 9.0 all-to-all-done.9
  794.9 18.1 %multiply_reduce_fusion.4 = (f32[]{:T(128)}, f32[]{:T(128)}, f32[]{:T(128)}, f32[]{:T(128)}, f32[32,16,1024]{2,1,0:T(8,128)}) fusion(f32[32,16,1024]{2,1,0:T(8,128)S(1)} %get-tuple-element.257, f32[]{:T(128)S(6)} %sqrt.15, f32[32,16,1024]{2,1,0:T(8,128)S(1)} %copy-done.13, f32[]{:T(128)} %sqrt.18, f32[32,16,1024]{2,1,0:T(8,128)S(1)} %copy-done.24, ...), kind=kOutput, calls=%fused_computation.98 | convolution fusion | flops 11283464192 | bytes 23599128 | tf_op jit(solution)/shard_map/dot_general | solution.py:66
  817.0 38.6 %psum.70 = f32[4]{0:T(128)S(1)} all-reduce(f32[4]{0:T(128)S(1)} %pad_maximum_fusion.2), channel_id=1, replica_groups=mesh['node'=16,'tone'=2] {'node','tone'}, use_global_device_ids=true, to_apply=%region_24.25 | all-reduce | flops 4 | bytes 32 | tf_op jit(solution)/shard_map/psum | solution.py:122
  856.3 7.6 multiply_reduce_fusion
  864.0 39.6 %psum.71 = f32[]{:T(128)} all-reduce(f32[]{:T(128)} %multiply_reduce_fusion), channel_id=1, replica_groups=mesh['node'=16,'tone'=2] {'node','tone'}, use_global_device_ids=true, to_apply=%region_26.27 | all-reduce | flops 1 | bytes 8 | tf_op jit(solution)/shard_map/psum | solution.py:125
  926.7 6.5 add_add_fusion
  934.1 8.2 multiply_subtract_fusion
  (198 shorter events, 157.1 us)
Async XLA Ops:
  0.6 46.0 %copy-start = (f32[3,4]{1,0:T(4,128)S(1)}, f32[3,4]{1,0:T(4,128)}, u32[]{:S(2)}) copy-start(f32[3,4]{1,0:T(4,128)} %param.47) | copy-start | bytes 148
  7.8 5.0 copy-start.15
  7.8 68.8 %all-to-all-start = ((f32[32,16,1024]{2,1,0:T(8,128)}), f32[32,16,1024]{2,1,0:T(8,128)}, u32[]{:S(2)}, u32[]{:S(2)}) async-start(f32[32,16,1024]{2,1,0:T(8,128)} %copy.113), calls=%async_computation | async-start | bytes 4194304 | tf_op jit(solution)/shard_map/all_to_all | solution.py:98
  12.8 6.2 copy-start.32
  14.1 103.0 %collective-permute-start = (f32[32,16,384]{2,1,0:T(8,128)}, f32[32,16,384]{2,1,0:T(8,128)}, u32[]{:S(2)}, u32[]{:S(2)}) collective-permute-start(f32[32,16,384]{2,1,0:T(8,128)} %get-tuple-element.210), channel_id=1, source_target_pairs={{0,2},{2,4},{4,6},{6,8},{8,10},{10,12},{12,14},{14,16},{16,18},{18... | collective-permute-start | bytes 2359304 | tf_op jit(solution)/shard_map/ppermute | solution.py:27
  17.4 99.7 %collective-permute-start.1 = (f32[32,16,384]{2,1,0:T(8,128)}, f32[32,16,384]{2,1,0:T(8,128)}, u32[]{:S(2)}, u32[]{:S(2)}) collective-permute-start(f32[32,16,384]{2,1,0:T(8,128)} %get-tuple-element.211), channel_id=1, source_target_pairs={{2,0},{4,2},{6,4},{8,6},{10,8},{12,10},{14,12},{16,14},{18,16},{20... | collective-permute-start | bytes 2359304 | tf_op jit(solution)/shard_map/ppermute | solution.py:28
  19.0 2.4 copy-start.35
  43.6 3.0 copy-start.33
  43.6 3.1 copy-start.31
  46.8 6.3 copy-start.21
  53.2 5.8 copy-start.20
  59.0 5.9 copy-start.19
  64.9 5.9 copy-start.18
  80.4 3.1 copy-start.7
  86.0 28.9 %all-to-all-start.1 = ((f32[16,32,1024]{2,0,1:T(8,128)}), f32[16,32,1024]{2,0,1:T(8,128)S(1)}, u32[]{:S(2)}, u32[]{:S(2)}) async-start(f32[16,32,1024]{2,0,1:T(8,128)} %copy.115), calls=%async_computation.1 | async-start | bytes 4194304 | tf_op jit(solution)/shard_map/all_to_all | solution.py:104
  89.8 7.2 copy-start.17
  115.1 2.2 copy-start.30
  177.6 3.0 copy-start.27
  183.2 30.2 %all-to-all-start.2 = ((f32[32,16,1024]{2,1,0:T(8,128)}), f32[32,16,1024]{2,1,0:T(8,128)}, u32[]{:S(2)}, u32[]{:S(2)}) async-start(f32[32,16,1024]{2,1,0:T(8,128)} %copy.119), calls=%async_computation.2 | async-start | bytes 4194304 | tf_op jit(solution)/shard_map/all_to_all | solution.py:98
  222.5 28.6 %all-to-all-start.3 = ((f32[16,32,1024]{2,0,1:T(8,128)}), f32[16,32,1024]{2,0,1:T(8,128)}, u32[]{:S(2)}, u32[]{:S(2)}) async-start(f32[16,32,1024]{2,0,1:T(8,128)} %copy.121), calls=%async_computation.3 | async-start | bytes 4194304 | tf_op jit(solution)/shard_map/all_to_all | solution.py:104
  229.7 25.1 %collective-permute-start.2 = (f32[32,16,384]{2,1,0:T(8,128)}, f32[32,16,384]{2,1,0:T(8,128)}, u32[]{:S(2)}, u32[]{:S(2)}) collective-permute-start(f32[32,16,384]{2,1,0:T(8,128)} %get-tuple-element.208), channel_id=1, source_target_pairs={{0,2},{2,4},{4,6},{6,8},{8,10},{10,12},{12,14},{14,16},{16,18},{18... | collective-permute-start | bytes 2359304 | tf_op jit(solution)/shard_map/ppermute | solution.py:27
  231.9 22.9 %collective-permute-start.3 = (f32[32,16,384]{2,1,0:T(8,128)S(1)}, f32[32,16,384]{2,1,0:T(8,128)}, u32[]{:S(2)}, u32[]{:S(2)}) collective-permute-start(f32[32,16,384]{2,1,0:T(8,128)S(1)} %get-tuple-element.209), channel_id=1, source_target_pairs={{2,0},{4,2},{6,4},{8,6},{10,8},{12,10},{14,12},{16,14},{18,16},{20... | collective-permute-start | bytes 2359304 | tf_op jit(solution)/shard_map/ppermute | solution.py:28
  359.3 3.1 copy-start.2
  391.0 2.1 copy-start.9
  398.4 27.6 %all-to-all-start.5 = ((f32[16,32,1024]{2,0,1:T(8,128)}), f32[16,32,1024]{2,0,1:T(8,128)}, u32[]{:S(2)}, u32[]{:S(2)}) async-start(f32[16,32,1024]{2,0,1:T(8,128)} %copy.127), calls=%async_computation.5 | async-start | bytes 4194304 | tf_op jit(solution)/shard_map/all_to_all | solution.py:104
  405.6 24.0 %collective-permute-start.4 = (f32[32,16,384]{2,1,0:T(8,128)}, f32[32,16,384]{2,1,0:T(8,128)}, u32[]{:S(2)}, u32[]{:S(2)}) collective-permute-start(f32[32,16,384]{2,1,0:T(8,128)} %get-tuple-element.206), channel_id=1, source_target_pairs={{0,2},{2,4},{4,6},{6,8},{8,10},{10,12},{12,14},{14,16},{16,18},{18... | collective-permute-start | bytes 2359304 | tf_op jit(solution)/shard_map/ppermute | solution.py:27
  407.8 21.8 %collective-permute-start.5 = (f32[32,16,384]{2,1,0:T(8,128)S(1)}, f32[32,16,384]{2,1,0:T(8,128)}, u32[]{:S(2)}, u32[]{:S(2)}) collective-permute-start(f32[32,16,384]{2,1,0:T(8,128)S(1)} %get-tuple-element.207), channel_id=1, source_target_pairs={{2,0},{4,2},{6,4},{8,6},{10,8},{12,10},{14,12},{16,14},{18,16},{20... | collective-permute-start | bytes 2359304 | tf_op jit(solution)/shard_map/ppermute | solution.py:28
  537.2 3.1 copy-start.22
  568.9 2.1 copy-start.10
  576.2 27.5 %all-to-all-start.7 = ((f32[16,32,1024]{2,0,1:T(8,128)}), f32[16,32,1024]{2,0,1:T(8,128)}, u32[]{:S(2)}, u32[]{:S(2)}) async-start(f32[16,32,1024]{2,0,1:T(8,128)} %copy.133), calls=%async_computation.7 | async-start | bytes 4194304 | tf_op jit(solution)/shard_map/all_to_all | solution.py:104
  583.4 24.0 %collective-permute-start.6 = (f32[32,16,384]{2,1,0:T(8,128)}, f32[32,16,384]{2,1,0:T(8,128)}, u32[]{:S(2)}, u32[]{:S(2)}) collective-permute-start(f32[32,16,384]{2,1,0:T(8,128)} %get-tuple-element.204), channel_id=1, source_target_pairs={{0,2},{2,4},{4,6},{6,8},{8,10},{10,12},{12,14},{14,16},{16,18},{18... | collective-permute-start | bytes 2359304 | tf_op jit(solution)/shard_map/ppermute | solution.py:27
  585.6 21.9 %collective-permute-start.7 = (f32[32,16,384]{2,1,0:T(8,128)S(1)}, f32[32,16,384]{2,1,0:T(8,128)}, u32[]{:S(2)}, u32[]{:S(2)}) collective-permute-start(f32[32,16,384]{2,1,0:T(8,128)S(1)} %get-tuple-element.205), channel_id=1, source_target_pairs={{2,0},{4,2},{6,4},{8,6},{10,8},{12,10},{14,12},{16,14},{18,16},{20... | collective-permute-start | bytes 2359304 | tf_op jit(solution)/shard_map/ppermute | solution.py:28
  605.5 2.2 copy-start.23
  718.0 3.0 copy-start.25
  723.6 6.3 copy-start.37
  723.6 29.5 %all-to-all-start.8 = ((f32[32,16,1024]{2,1,0:T(8,128)}), f32[32,16,1024]{2,1,0:T(8,128)}, u32[]{:S(2)}, u32[]{:S(2)}) async-start(f32[32,16,1024]{2,1,0:T(8,128)} %copy.137), calls=%async_computation.8 | async-start | bytes 4194304 | tf_op jit(solution)/shard_map/all_to_all | solution.py:98
  762.3 5.0 copy-start.36
  762.3 28.2 %all-to-all-start.9 = ((f32[16,32,1024]{2,0,1:T(8,128)}), f32[16,32,1024]{2,0,1:T(8,128)}, u32[]{:S(2)}, u32[]{:S(2)}) async-start(f32[16,32,1024]{2,0,1:T(8,128)} %copy.139), calls=%async_computation.9 | async-start | bytes 4194304 | tf_op jit(solution)/shard_map/all_to_all | solution.py:104
  770.4 24.0 %collective-permute-start.8 = (f32[32,16,384]{2,1,0:T(8,128)}, f32[32,16,384]{2,1,0:T(8,128)}, u32[]{:S(2)}, u32[]{:S(2)}) collective-permute-start(f32[32,16,384]{2,1,0:T(8,128)} %get-tuple-element.202), channel_id=1, source_target_pairs={{0,2},{2,4},{4,6},{6,8},{8,10},{10,12},{12,14},{14,16},{16,18},{18... | collective-permute-start | bytes 2359304 | tf_op jit(solution)/shard_map/ppermute | solution.py:27
  772.5 21.9 %collective-permute-start.9 = (f32[32,16,384]{2,1,0:T(8,128)S(1)}, f32[32,16,384]{2,1,0:T(8,128)}, u32[]{:S(2)}, u32[]{:S(2)}) collective-permute-start(f32[32,16,384]{2,1,0:T(8,128)S(1)} %get-tuple-element.203), channel_id=1, source_target_pairs={{2,0},{4,2},{6,4},{8,6},{10,8},{12,10},{14,12},{16,14},{18,16},{20... | collective-permute-start | bytes 2359304 | tf_op jit(solution)/shard_map/ppermute | solution.py:28
  790.5 3.9 copy-start.24
  790.5 3.9 copy-start.26
  792.4 2.4 copy-start.13
  926.7 7.4 copy-start.6
  926.7 7.4 copy-start.12
  926.7 7.4 copy-start.14
  926.7 7.4 copy-start.29
  934.1 8.2 copy-start.1
  (8 other events, 16.4 us)
where the time goes:
time: 949 us; the launch traced here: 942 us
  blocking collectives  414 us (44%)
  matrix products  143 us (15%)
  waiting for transfers between devices  120 us (13%)
  other arithmetic  110 us (12%)
  local copies, waits for them, and re-layouts  77 us (8%)
  starting transfers between devices  57.6 us (6%)
  between operations  20.7 us (2%)
    psum x4, blocking collectives, per_device(): length = jnp.sqrt(lax.psum(jnp.sum(image * image), ('node', 'tone')))  163 us
    psum x4, blocking collectives, per_device(): projected = lax.psum(local_terms, ('node', 'tone'))  155 us
    dot_general x5, matrix products, couple(): jnp.dot(padded.reshape(rows, padded.shape[2]), operator, precision=HIGH)  87.9 us
    all_to_all x5, waiting for transfers between devices, to_freq(): lax.all_to_all(along_second(second, field), 'tone', split_axis=1, concat_...  72.1 us
    all_to_all x2, blocking collectives, to_time(): lax.all_to_all(along_first(first, field), 'tone', split_axis=0, concat_ax...  54.2 us
    all_to_all x3, waiting for transfers between devices, to_time(): lax.all_to_all(along_first(first, field), 'tone', split_axis=0, concat_ax...  47.7 us
    psum x1, blocking collectives, per_device(): beta = jnp.sqrt(lax.psum(jnp.sum(start * start), ('node', 'tone')))  42.4 us
    scatter-add x6, other arithmetic, band_matrix(): operator = operator.at[offset * NB:offset * NB + nodes].add(placed)  36.2 us
  transfers between devices with their start and end apart: 18, of which 7 were waited for; matrix products, arithmetic and copies ran while one was open for 13% of the time, Pallas kernels for 0%

commit v1 on v0

v1 whole, which is shorter than its diff:
```python
import functools
import math

import jax
import jax.numpy as jnp
from jax import lax
from jax.experimental import pallas as pl
from jax.experimental.pallas import tpu as pltpu
from jax.sharding import PartitionSpec as P

NB = 128
HALO_B = 3
NOFF = 7
M = 4
NTYPES = 4
AXES = ("node", "tone")
EXACT = lax.Precision.HIGHEST
F32 = jnp.float32
BF16 = jnp.bfloat16
LIMIT = 16 * 1024 * 1024
ROWS = 128


class Chain:
    def __init__(self, nodes, tones):
        self.nodes, self.tones = nodes, tones
        self.at = [0] * (nodes * tones)
        for i in range(nodes):
            for t in range(tones):
                place = (i // 2) * 2 * tones + 2 * self.turn(i, t) + i % 2
                self.at[place] = i * tones + t

    def turn(self, i, t):
        return t if (i // 2) % 2 == 0 else self.tones - 1 - t

    def device(self, group, core, turn):
        return self.at[group * 2 * self.tones + 2 * turn + core]

    def up(self, hop):
        return [(self.at[p], self.at[p + hop]) for p in range(len(self.at) - hop)]

    def down(self, hop):
        return [(b, a) for a, b in self.up(hop)]

    def node_up(self, hop):
        tones = self.tones
        return [
            (i * tones + t, (i + hop) * tones + t)
            for i in range(self.nodes - hop)
            for t in range(tones)
        ]

    def node_down(self, hop):
        return [(b, a) for a, b in self.node_up(hop)]

    def swap(self):
        tones = self.tones
        return [(i * tones + t, (i ^ 1) * tones + t) for i in range(self.nodes) for t in range(tones)]

    def shift(self, s):
        tones = self.tones
        return [
            (i * tones + t, i * tones + (t + s) % tones)
            for i in range(self.nodes)
            for t in range(tones)
        ]

    def first(self):
        pairs = []
        for g in range(self.nodes // 2):
            for a, b in (((0, 0), (1, 0)), ((0, 1), (0, 0)), ((1, 0), (1, 1)), ((1, 1), (0, 1))):
                pairs.append((self.device(g, *a), self.device(g, *b)))
        return pairs

    def second(self):
        pairs = []
        for g in range(self.nodes // 2):
            for a, b in (((0, 1), (1, 0)), ((1, 0), (0, 1))):
                pairs.append((self.device(g, *a), self.device(g, *b)))
        return pairs


def flipped(pairs):
    return [(b, a) for a, b in pairs]


def turned(tones, place, index):
    return jnp.where((place["group"] % 2) == 0, index, tones - 1 - index)


def parity_chunks(value, tones, parity, axis):
    width = value.shape[axis] // tones
    parts = [
        lax.dynamic_slice_in_dim(value, (2 * h + parity) * width, width, axis)
        for h in range(tones // 2)
    ]
    return parts[0] if len(parts) == 1 else jnp.concatenate(parts, axis=axis)


def core_swap(chain, value, core, axis):
    keep = parity_chunks(value, chain.tones, core, axis)
    give = parity_chunks(value, chain.tones, 1 - core, axis)
    got = lax.ppermute(give, AXES, chain.swap())
    return jnp.where(core == 0, keep, got), jnp.where(core == 0, got, keep)


def chunk_of(chain, value, place, axis):
    low, high = core_swap(chain, value, place["core"], axis)
    half = chain.tones // 2
    both = jnp.where(place["turn"] < half, low, high)
    width = value.shape[axis] // chain.tones
    return lax.dynamic_slice_in_dim(both, place["turn"] % half * width, width, axis)


def gather_tones(chain, field, place):
    tones, tone, core, turn = chain.tones, place["tone"], place["core"], place["turn"]
    width = field.shape[2] // tones
    rows = field.shape[0] * field.shape[1]
    field = field.reshape(rows, field.shape[2])
    if tones == 2:
        one = lax.dynamic_slice_in_dim(field, (1 - turn) * width, width, 1)
        two = lax.dynamic_slice_in_dim(field, turn * width, width, 1)
        got_one = lax.ppermute(one, AXES, chain.first())
        got_two = lax.ppermute(two, AXES, chain.second())
        same = jnp.where(core == turn, two, got_one)
        other = jnp.where(core == turn, got_one, got_two)
        return jnp.concatenate(
            [jnp.where(tone == 0, same, other), jnp.where(tone == 0, other, same)], axis=0
        )
    low, high = core_swap(chain, field, core, 1)
    chunks = jnp.concatenate([low, high], axis=1)
    out = jnp.zeros((tones * rows, width), field.dtype)
    for s in range(tones):
        target = turned(tones, place, (tone + s) % tones)
        piece = lax.dynamic_slice_in_dim(chunks, target * width, width, 1)
        if s:
            piece = lax.ppermute(piece, AXES, chain.shift(s))
        out = lax.dynamic_update_slice_in_dim(out, piece, (tone - s) % tones * rows, 0)
    return out


def scatter_tones(chain, field, place, shape):
    tones, tone, core, turn = chain.tones, place["tone"], place["core"], place["turn"]
    width = field.shape[1]
    rows = field.shape[0] // tones
    if tones == 2:
        same = lax.dynamic_slice_in_dim(field, tone * rows, rows, 0)
        other = lax.dynamic_slice_in_dim(field, (1 - tone) * rows, rows, 0)
        one = jnp.where(core == turn, other, same)
        got_one = lax.ppermute(one, AXES, flipped(chain.first()))
        got_two = lax.ppermute(other, AXES, flipped(chain.second()))
        at_turn = jnp.where(core == turn, same, got_two)
        return jnp.concatenate(
            [jnp.where(turn == 0, at_turn, got_one), jnp.where(turn == 0, got_one, at_turn)], axis=1
        ).reshape(shape)
    chunks = jnp.zeros((rows, tones * width), field.dtype)
    for s in range(tones):
        piece = lax.dynamic_slice_in_dim(field, (tone + s) % tones * rows, rows, 0)
        if s:
            piece = lax.ppermute(piece, AXES, chain.shift(s))
        slot = turned(tones, place, (tone - s) % tones)
        chunks = lax.dynamic_update_slice_in_dim(chunks, piece, slot * width, 1)
    half = tones // 2 * width
    low, high = chunks[:, :half], chunks[:, half:]
    keep = jnp.where(core == 0, low, high)
    give = jnp.where(core == 0, high, low)
    got = lax.ppermute(give, AXES, chain.swap())
    even, odd = jnp.where(core == 0, keep, got), jnp.where(core == 0, got, keep)
    parts = []
    for h in range(tones // 2):
        parts += [even[:, h * width : (h + 1) * width], odd[:, h * width : (h + 1) * width]]
    return jnp.concatenate(parts, axis=1).reshape(shape)


def edges_of(field):
    take = min(field.shape[1], HALO_B * NB)
    return field[:, field.shape[1] - take :], field[:, :take]


def halos(last, first, up, down):
    width = last.shape[1]
    reach = HALO_B * NB
    left, right = [], []
    hop, have = 1, 0
    while have < reach:
        take = min(width, reach - have)
        left.insert(0, lax.ppermute(last[:, width - take :], AXES, up(hop)))
        right.append(lax.ppermute(first[:, :take], AXES, down(hop)))
        have, hop = have + take, hop + 1
    if len(left) == 1:
        return left[0], right[0]
    return jnp.concatenate(left, axis=1), jnp.concatenate(right, axis=1)


def hartley(count):
    grid = jnp.arange(count, dtype=jnp.int32)
    phase = grid[:, None] * grid[None, :] % count
    angle = phase.astype(F32) * (2.0 * math.pi / count)
    return (jnp.cos(angle) + jnp.sin(angle)) / math.sqrt(count)


def halves(value):
    top = value.astype(BF16)
    return top, (value - top.astype(F32)).astype(BF16)


def rounded_halves(value):
    top = lax.reduce_precision(value, exponent_bits=8, mantissa_bits=7)
    return top.astype(BF16), (value - top).astype(BF16)


def two_tone_tables(k1, k2, tones):
    local, half = k2 // tones, k1 // 2
    rows = jnp.arange(half * k2 // 2, dtype=jnp.int32)
    index1 = rows // local % half
    index2 = rows // (local * half) * local + rows % local

    def spread(index, table):
        pick = (index[:, None] == jnp.arange(table.shape[0], dtype=jnp.int32)[None, :]).astype(F32)
        left = jnp.dot(pick, table, precision=EXACT)
        return lax.dot_general(left, pick, (((1,), (1,)), ((), ())), precision=EXACT)

    first, second = hartley(k1), hartley(k2)
    ones = [spread(index1, first[p::2, :half]) for p in range(2)]
    twos = [spread(index2, second[p::2, : k2 // 2]) for p in range(2)]
    forward = jnp.stack([ones[p // 2] * twos[p % 2] for p in range(4)])
    return (*rounded_halves(forward), *rounded_halves(jnp.swapaxes(forward, 1, 2)))


def dot3(a_top, a_low, b_top, b_low):
    def dot(a, b):
        return jnp.dot(a, b, preferred_element_type=F32)

    return dot(a_top, b_top) + (dot(a_top, b_low) + dot(a_low, b_top))


def lane_of(row, index):
    lanes = lax.broadcasted_iota(jnp.int32, row.shape, 1)
    return jnp.sum(jnp.where(lanes == index, row, 0.0), axis=1, keepdims=True)


def coefficients(parts):
    columns, norms = [], []
    for j, part in enumerate(parts):
        row = jnp.sum(part[...], axis=0)
        norms.append(lane_of(row, j + 2))
        squared = lane_of(row, j + 1)
        columns.append(
            ([lane_of(row, i) / norms[i] for i in range(j + 1)], squared, lax.rsqrt(squared))
        )
    return columns, norms


def orthogonal(raw, vectors, column):
    coeffs, _, scale = column
    for coeff, vector in zip(coeffs, vectors):
        raw = raw - coeff * vector
    return raw * scale


def pieces_of(k1, tones, rows):
    local = rows // (k1 * tones)
    size = k1 // 2 * local
    groups = []
    for a in range(2):
        for b in range(2):
            groups.append(
                [
                    slice(at, at + size)
                    for t in range(tones // 2)
                    for at in [((a * (tones // 2) + t) * k1 + b * (k1 // 2)) * local]
                ]
            )
    return groups


def to_samples(fields, tables, finish):
    top, low = tables[:2]
    sums = [fields[0] + fields[1], fields[2] + fields[3]]
    gaps = [fields[0] - fields[1], fields[2] - fields[3]]
    mixed = [sums[0] + sums[1], sums[0] - sums[1], gaps[0] + gaps[1], gaps[0] - gaps[1]]
    for parity in range(4):
        finish(parity, dot3(top[parity], low[parity], *halves(mixed[parity])))


def to_harmonics(samples, tables):
    top, low = tables[2:]
    parts = [dot3(top[p], low[p], *samples[p]) for p in range(4)]
    even = [parts[0] + parts[1], parts[0] - parts[1]]
    odd = [parts[2] + parts[3], parts[2] - parts[3]]
    return [even[0] + odd[0], even[0] - odd[0], even[1] + odd[1], even[1] - odd[1]]


def taken(value, groups):
    picked = [[value[here, :] for here in group] for group in groups]
    return [p[0] if len(p) == 1 else jnp.concatenate(p, axis=0) for p in picked]


def put(ref, groups, values):
    for group, value in zip(groups, values):
        size = value.shape[0] // len(group)
        for index, here in enumerate(group):
            ref[here, :] = value[index * size : (index + 1) * size, :]


def start_kernel(groups, volts, params, *refs):
    tables, (slope, back) = refs[:4], refs[4:]
    linear, amplitude, sharpness = params[0:1, :], params[1:2, :], params[2:3, :]
    samples = [None] * 4

    def finish(parity, wave):
        size = wave.shape[0]
        bend = jnp.tanh(sharpness * wave)
        here = slice(parity * size, (parity + 1) * size)
        slope[here, :] = linear + amplitude * sharpness * (1.0 - bend * bend)
        samples[parity] = halves(linear * wave + amplitude * bend)

    to_samples(taken(volts, groups), tables, finish)
    put(back, groups, to_harmonics(samples, tables))


def tone_kernel(groups, n_parts, *refs):
    parts, refs = refs[:n_parts], refs[n_parts:]
    raw, basis, refs = refs[0], refs[1 : 1 + n_parts], refs[1 + n_parts :]
    slope, tables, outs = refs[0], refs[1:5], refs[5:]
    fields = taken(raw, groups)
    if n_parts:
        columns, _ = coefficients(parts)
        vectors = [taken(b, groups) for b in basis]
        fields = [
            orthogonal(fields[p], [v[p] for v in vectors], columns[-1]) for p in range(4)
        ]
        put(outs[0], groups, fields)
    samples = [None] * 4

    def finish(parity, wave):
        size = wave.shape[0]
        samples[parity] = halves(slope[parity * size : (parity + 1) * size, :] * wave)

    to_samples(fields, tables, finish)
    put(outs[-1], groups, to_harmonics(samples, tables))


def column_block(width):
    return width // 2 if width % 256 == 0 else width


def columns_call(kernel, name, parts, fields, small, tables, outs):
    rows, width = fields[0].shape
    block = column_block(width)
    whole = pl.BlockSpec((rows, block), lambda i: (0, i))
    once = functools.partial(pl.BlockSpec, pipeline_mode=pl.Buffered(1))
    specs = [once(p.shape, lambda i: (0, 0, 0)) for p in parts]
    specs += [whole for _ in fields]
    specs += [pl.BlockSpec((s.shape[0], block), lambda i: (0, i)) for s in small]
    specs += [once(t.shape, lambda i: (0, 0, 0)) for t in tables]
    return pl.pallas_call(
        kernel,
        name=name,
        grid=(width // block,),
        in_specs=specs,
        out_specs=[whole] * outs,
        out_shape=[jax.ShapeDtypeStruct((rows, width), F32)] * outs,
        compiler_params=pltpu.CompilerParams(vmem_limit_bytes=LIMIT),
        cost_estimate=pl.CostEstimate(
            flops=3 * rows * rows * width, bytes_accessed=16 * rows * width, transcendentals=0
        ),
    )(*parts, *fields, *small, *tables)


def coupled(left, field, right, op_top, op_low, ext_top, ext_low, write):
    width = field.shape[1]
    reach = HALO_B * NB
    for value, at in ((left, 0), (field, reach), (right, reach + width)):
        here = slice(at, at + value.shape[1])
        ext_top[:, here], ext_low[:, here] = halves(value)
    step = 2 * NB if width % (2 * NB) == 0 else NB
    for at in range(0, width, step):
        rows = slice(at, at + step + 2 * reach)
        here = slice(at, at + step)
        write(here, dot3(ext_top[:, rows], ext_low[:, rows], op_top[rows, here], op_low[rows, here]))


def residual_kernel(source, volts, left, right, caps, damps, op_top, op_low, out, ext_top, ext_low):
    def write(here, value):
        scaled = damps[...] * caps[:, here] * volts[:, here]
        out[:, here] = source[:, here] - (scaled + value)

    coupled(left[...], volts[...], right[...], op_top, op_low, ext_top, ext_low, write)


def image_kernel(n_parts, more, *refs):
    parts, refs = refs[:n_parts], refs[n_parts:]
    basis, refs = refs[: n_parts + 1], refs[n_parts + 1 :]
    tones, left, right = refs[0], refs[1][...], refs[2][...]
    lefts, rights = refs[3 : 3 + n_parts], refs[3 + n_parts : 3 + 2 * n_parts]
    refs = refs[3 + 2 * n_parts :]
    caps, damps, op_top, op_low = refs[:4]
    out, stats = refs[4:6]
    refs = refs[6:]
    step = pl.program_id(0)
    if n_parts:
        columns, _ = coefficients(parts)
        left = orthogonal(left, [b[...] for b in lefts], columns[-1])
        right = orthogonal(right, [b[...] for b in rights], columns[-1])
    edges = None
    if more:
        if n_parts:
            refs[0][...] = left
            refs[1][...] = right
            refs = refs[2:]
        edges, refs = refs[:2], refs[2:]
    ext_top, ext_low, sums = refs
    field = basis[-1]

    @pl.when(step == 0)
    def _():
        sums[...] = jnp.zeros_like(sums)

    def tile_sum(value):
        value = jnp.sum(value.reshape(value.shape[0] // 8, 8, value.shape[1]), axis=0)
        total = value[:, :NB]
        for at in range(NB, value.shape[1], NB):
            total = total + value[:, at : at + NB]
        return total

    def write(here, value):
        mine = field[:, here]
        value = value + (tones[:, here] + damps[...] * caps[:, here] * mine)
        out[:, here] = value
        for i in range(n_parts + 1):
            sums[i] += tile_sum(basis[i][:, here] * value)
        sums[n_parts + 1] += tile_sum(value * value)
        sums[n_parts + 2] += tile_sum(mine * mine)

    coupled(left, field[...], right, op_top, op_low, ext_top, ext_low, write)

    if edges:
        take = edges[0].shape[1]
        edges[0][...] = out[:, out.shape[1] - take :]
        edges[1][...] = out[:, :take]

    @pl.when(step == pl.num_programs(0) - 1)
    def _():
        lanes = lax.broadcasted_iota(jnp.int32, (1, NB), 1)
        row = jnp.zeros((1, NB), F32)
        for i in range(n_parts + 3):
            total = jnp.sum(jnp.sum(sums[i], axis=0, keepdims=True), axis=1, keepdims=True)
            row = jnp.where(lanes == i, total, row)
        stats[...] = jnp.broadcast_to(row[None], stats.shape)


def rows_call(kernel, name, parts, fields, caps, damps, operator, outs, stats, scratch):
    rows, width = fields[0].shape
    block = min(rows, ROWS)
    once = functools.partial(pl.BlockSpec, pipeline_mode=pl.Buffered(1))

    def along(shape):
        return pl.BlockSpec((block, shape[1]), lambda i: (i, 0))

    specs = [once(p.shape, lambda i: (0, 0, 0)) for p in parts]
    specs += [along(f.shape) for f in fields]
    small = []
    if caps is not None:
        specs += [once(caps.shape, lambda i: (0, 0)), along(damps.shape)]
        small += [caps, damps]
    specs += [once(o.shape, lambda i: (0, 0)) for o in operator]
    shapes = [jax.ShapeDtypeStruct(o, F32) for o in outs]
    out_specs = [along(o) for o in outs]
    if stats:
        shapes.insert(1, jax.ShapeDtypeStruct((stats, 1, NB), F32))
        out_specs.insert(1, pl.BlockSpec((stats, 1, NB), lambda i: (0, 0, 0)))
    flops = 12 * rows * width * (width + HALO_B * NB) if operator else 16 * rows * width
    return pl.pallas_call(
        kernel,
        name=name,
        grid=(rows // block,),
        in_specs=specs,
        out_specs=out_specs,
        out_shape=shapes,
        scratch_shapes=scratch(block),
        compiler_params=pltpu.CompilerParams(vmem_limit_bytes=LIMIT),
        cost_estimate=pl.CostEstimate(
            flops=flops, bytes_accessed=4 * rows * width * len(fields), transcendentals=0
        ),
    )(*parts, *fields, *small, *operator)


def operator_kernel(band_code, active, coupling, top, low):
    blocks = coupling.shape[0]
    for block in range(blocks):
        cols = slice(block * NB, (block + 1) * NB)
        for row in range(blocks + 2 * HALO_B):
            here = slice(row * NB, (row + 1) * NB)
            offset = row - block
            if 0 <= offset < NOFF:
                band = 0
                for j in range(NOFF):
                    band = band + jnp.where(band_code[j] == offset, j, 0)
                value = jnp.transpose(coupling[block, band]) * active[block, band]
                top[here, cols], low[here, cols] = halves(value)
            else:
                top[here, cols] = jnp.zeros((NB, NB), BF16)
                low[here, cols] = jnp.zeros((NB, NB), BF16)


def band_operator(coupling, band_code, active):
    blocks = coupling.shape[0]
    shape = ((blocks + 2 * HALO_B) * NB, blocks * NB)
    smem = pl.BlockSpec(memory_space=pltpu.SMEM)
    vmem = pl.BlockSpec(memory_space=pltpu.VMEM)
    return pl.pallas_call(
        operator_kernel,
        name="operator",
        in_specs=[smem, smem, vmem],
        out_specs=[vmem, vmem],
        out_shape=[jax.ShapeDtypeStruct(shape, BF16)] * 2,
        compiler_params=pltpu.CompilerParams(vmem_limit_bytes=LIMIT),
        cost_estimate=pl.CostEstimate(flops=1 << 22, bytes_accessed=1 << 22, transcendentals=0),
    )(band_code, active, coupling)


def solve(gram, rhs):
    count = len(rhs)
    lower = [[None] * count for _ in range(count)]
    for i in range(count):
        for j in range(i + 1):
            total = gram[i][j]
            for k in range(j):
                total = total - lower[i][k] * lower[j][k]
            lower[i][j] = jnp.sqrt(total) if i == j else total / lower[j][j]
    forward = []
    for i in range(count):
        total = rhs[i]
        for k in range(i):
            total = total - lower[i][k] * forward[k]
        forward.append(total / lower[i][i])
    backward = [None] * count
    for i in reversed(range(count)):
        total = forward[i]
        for k in range(i + 1, count):
            total = total - lower[k][i] * backward[k]
        backward[i] = total / lower[i][i]
    return backward


def answer_of(parts):
    columns, norms = coefficients(parts)
    hessen = [[None] * M for _ in range(M + 1)]
    for j, (coeffs, squared, scale) in enumerate(columns):
        for i in range(j + 1):
            hessen[i][j] = coeffs[i]
        hessen[j + 1][j] = squared * scale
    gram = [[None] * M for _ in range(M)]
    for j in range(M):
        for i in range(j):
            total = norms[0] * hessen[0][i] * hessen[0][j]
            for k in range(1, i + 2):
                total = total + norms[k] * hessen[k][i] * hessen[k][j]
            gram[j][i] = total
        gram[j][j] = columns[j][1]
    answer = solve(gram, [norms[0] * hessen[0][j] for j in range(M)])
    fitted = []
    for i in range(M):
        first = max(i - 1, 0)
        total = hessen[i][first] * answer[first]
        for j in range(first + 1, M - 1):
            total = total + hessen[i][j] * answer[j]
        fitted.append(total)
    return answer, fitted


def update_kernel(*refs):
    parts, basis, (volts, out) = refs[:M], refs[M : 2 * M], refs[2 * M :]
    answer, _ = answer_of(parts)
    total = answer[0] * basis[0][...]
    for j in range(1, M):
        total = total + answer[j] * basis[j][...]
    out[...] = volts[...] + total


def remaining_kernel(*refs):
    parts, basis, (image, out) = refs[:M], refs[M : 2 * M], refs[2 * M :]
    answer, fitted = answer_of(parts)
    total = basis[0][...] - fitted[0] * basis[0][...]
    for i in range(1, M):
        total = total - fitted[i] * basis[i][...]
    out[...] = total - answer[M - 1] * image[...]


def make(nodes, tones):
    chain = Chain(nodes, tones)
    count = nodes * tones

    def per_device(voltages, source, coupling, band_code, active, cap, damp, kind, type_params):
        node, tone = lax.axis_index("node"), lax.axis_index("tone")
        place = {"tone": tone, "group": node // 2, "core": node % 2}
        place["turn"] = turned(tones, place, tone)
        shape = voltages.shape
        k1, k2 = shape[0], shape[1] * tones

        volts = gather_tones(chain, voltages, place)
        rows, width = volts.shape
        local = rows // tones

        onehot = (kind[None, :] == jnp.arange(NTYPES, dtype=jnp.int32)[:, None]).astype(F32)
        per_node = jnp.dot(type_params, onehot, precision=EXACT)
        per_node = jnp.concatenate(
            [per_node, cap[None, :], jnp.zeros((4, cap.shape[0]), F32)], axis=0
        )
        per_node = chunk_of(chain, per_node, place, 1)
        caps = per_node[3:4]
        damps = jnp.zeros((tones, local, 1), F32)
        for s in range(tones):
            piece = lax.ppermute(damp, AXES, chain.shift(s)) if s else damp
            piece = piece.reshape(1, local, 1)
            damps = lax.dynamic_update_slice_in_dim(damps, piece, (tone - s) % tones, 0)
        damps = damps.reshape(rows, 1)

        def ext_scratch(nodes):
            ext = nodes + 2 * HALO_B * NB
            return lambda block: [pltpu.VMEM((block, ext), BF16)] * 2

        volts_here = voltages.reshape(local, shape[2])
        left, right = halos(*edges_of(volts_here), chain.node_up, chain.node_down)
        (driven,) = rows_call(
            residual_kernel,
            "driven",
            [],
            [source.reshape(local, shape[2]), volts_here, left, right],
            cap[None, :],
            damp.reshape(local, 1),
            band_operator(coupling, band_code, active.astype(F32)),
            [(local, shape[2])],
            0,
            ext_scratch(shape[2]),
        )
        driven, volts, coupling = lax.optimization_barrier((driven, volts, coupling))
        driven = gather_tones(chain, driven.reshape(shape), place)

        mine = chunk_of(chain, coupling, place, 0)
        mine_active = chunk_of(chain, active.astype(F32), place, 0)
        operator = band_operator(mine, band_code, mine_active)
        tables = two_tone_tables(k1, k2, tones)
        groups = pieces_of(k1, tones, rows)

        slope, back = columns_call(
            functools.partial(start_kernel, groups), "start", [], [volts], [per_node], tables, 2
        )
        start = driven - back

        left, right = halos(*edges_of(start), chain.up, chain.down)
        basis, lefts, rights, parts = [], [], [], []
        image = start
        edge, reach = (rows, min(width, HALO_B * NB)), (rows, HALO_B * NB)
        for column in range(M):
            made = columns_call(
                functools.partial(tone_kernel, groups, column),
                f"tone{column}",
                parts,
                [image, *basis, slope],
                [],
                tables,
                2 if column else 1,
            )
            new, toned = made if column else (start, made[0])
            more = column + 1 < M
            made = rows_call(
                functools.partial(image_kernel, column, more),
                f"image{column}",
                parts,
                [*basis, new, toned, left, right, *lefts, *rights],
                caps,
                damps,
                operator,
                [(rows, width)] + ([reach, reach] if more and column else []) + [edge, edge] * more,
                count,
                lambda block, n=column: ext_scratch(width)(block)
                + [pltpu.VMEM((n + 3, 8, NB), F32)],
            )
            image, stats = made[:2]
            basis.append(new)
            part = lax.all_to_all(stats, AXES, 0, 0, tiled=True)
            if more:
                lefts.append(made[2] if column else left)
                rights.append(made[3] if column else right)
                last, first, part = lax.optimization_barrier((*made[-2:], part))
                left, right = halos(last, first, chain.up, chain.down)
            parts = parts + [part]

        def final(kernel, name, last):
            return rows_call(
                kernel, name, parts, [*basis, last], None, None, [], [(rows, width)], 0, lambda block: []
            )[0]

        new_volts = scatter_tones(chain, final(update_kernel, "update", volts), place, shape)
        remaining = scatter_tones(chain, final(remaining_kernel, "remaining", image), place, shape)
        return new_volts, remaining

    return per_device


def solution(mesh):
    placed = (
        P(None, "tone", "node"),
        P(None, "tone", "node"),
        P("node", None, None, None),
        P(),
        P("node", None),
        P("node"),
        P(None, "tone"),
        P("node"),
        P(),
    )
    return jax.shard_map(
        make(mesh.shape["node"], mesh.shape["tone"]),
        mesh=mesh,
        in_specs=placed,
        out_specs=(P(None, "tone", "node"), P(None, "tone", "node")),
        check_vma=False,
    )
```

time: 949 us -> 324 us (0.34)
  blocking collectives: 414 us -> 65.9 us
  matrix products: 143 us -> 3.1 us
  other arithmetic: 110 us -> 20.2 us
  Pallas kernels: 0 us -> 67.6 us
  waiting for transfers between devices: 120 us -> 57 us
  local copies, waits for them, and re-layouts: 77 us -> 32.1 us
  between operations: 20.7 us -> 1.48 us
  starting transfers between devices: 57.6 us -> 72.7 us
    psum x9 -> x0, blocking collectives: 360 us -> none  [the longest x4 163 us: per_device(): length = jnp.sqrt(lax.psum(jnp.sum(image * image), ('node', 'tone')))]
    dot_general x29 -> x9, matrix products: 143 us -> 3.1 us  [the longest x4 1.25 us: spread(): lax.dot_general(left, pick, (((1,), (1,)), ((), ())), precision=EXACT)]
    all_to_all x8 -> x1, waiting for transfers between devices: 120 us -> 7.22 us  [per_device(): part = lax.all_to_all(stats, AXES, 0, 0, tiled=True)]
    pallas_call x0 -> x14, Pallas kernels: none -> 67.6 us  [the longest x7 47 us: rows_call(): pl.pallas_call(kernel, name=name, grid=(rows // block,), in_specs=specs,...]
    ppermute x10 -> x22, waiting for transfers between devices: 0.03 us -> 49.8 us  [the longest x2 32 us: scatter_tones(): got_one = lax.ppermute(one, AXES, flipped(chain.first()))]
    scatter-add x6 -> x0, other arithmetic: 36.2 us -> none  [band_matrix(): operator = operator.at[offset * NB:offset * NB + nodes].add(placed)]
    ppermute x10 -> x22, starting transfers between devices: 19.5 us -> 54 us  [the longest x5 23.3 us: halos(): left.insert(0, lax.ppermute(last[:, width - take:], AXES, up(hop)))]
    reduce_sum x4 -> x0, other arithmetic: 25 us -> none  [per_device(): length = jnp.sqrt(lax.psum(jnp.sum(image * image), ('node', 'tone')))]
  transfers between devices with their start and end apart: 18 -> 23, of which waited for: 7 -> 7; matrix products, arithmetic and copies ran while one was open for 13% -> 10% of each run, Pallas kernels for 0% -> 9%
where the time goes in v1:
time: 324 us; the launch traced here: 320 us
  starting transfers between devices  72.7 us (22%)
  Pallas kernels  67.6 us (21%)
  blocking collectives  65.9 us (20%)
  waiting for transfers between devices  57 us (18%)
  local copies, waits for them, and re-layouts  32.1 us (10%)
  other arithmetic  20.2 us (6%)
    all_to_all x3, blocking collectives, per_device(): part = lax.all_to_all(stats, AXES, 0, 0, tiled=True)  65.9 us
    pallas_call x7, Pallas kernels, rows_call(): pl.pallas_call(kernel, name=name, grid=(rows // block,), in_specs=specs,...  47 us
    ppermute x2, waiting for transfers between devices, scatter_tones(): got_one = lax.ppermute(one, AXES, flipped(chain.first()))  32 us
    ppermute x5, starting transfers between devices, halos(): left.insert(0, lax.ppermute(last[:, width - take:], AXES, up(hop)))  23.3 us
    all_to_all x1, starting transfers between devices, per_device(): part = lax.all_to_all(stats, AXES, 0, 0, tiled=True)  18.8 us
    unnamed x93, local copies, waits for them, and re-layouts  17.3 us
    pallas_call x5, Pallas kernels, columns_call(): pl.pallas_call(kernel, name=name, grid=(width // block,), in_specs=specs,...  16.7 us
    ppermute x1, waiting for transfers between devices, per_device(): piece = lax.ppermute(damp, AXES, chain.shift(s)) if s else damp  15.1 us
  transfers between devices with their start and end apart: 23, of which 7 were waited for; matrix products, arithmetic and copies ran while one was open for 10% of the time, Pallas kernels for 9%

profile of v1, /device:TPU:0, one launch (start us, length us, event | category | flops | bytes accessed | tf_op | source)
XLA Modules:
  0.0 320.1 jit_solution(8048449167304043610)
XLA Ops:
  4.6 2.7 fusion.32
  8.6 4.0 %collective-permute-start = (f32[512,384]{1,0:T(8,128)}, f32[512,384]{1,0:T(8,128)}, u32[]{:S(2)}, u32[]{:S(2)}) collective-permute-start(f32[512,384]{1,0:T(8,128)} %get-tuple-element.105), channel_id=1, source_target_pairs={{0,2},{1,3},{2,4},{3,5},{4,6},{5,7},{6,8},{7,9},{8,10},{9,11},{10,... | collective-permute-start | bytes 2359304 | tf_op jit(solution)/shard_map/ppermute | solution.py:187
  12.5 1.5 constant_dynamic-slice_fusion.8
  15.3 1.6 collective-permute-start.3
  19.5 2.0 copy-done.14
  21.6 2.7 operator.2
  25.3 5.4 %driven.1 = f32[512,1024]{1,0:T(8,128)S(1)} custom-call(f32[512,1024]{1,0:T(8,128)S(1)} %bitcast.42, f32[512,1024]{1,0:T(8,128)S(1)} %bitcast.35, f32[512,384]{1,0:T(8,128)} %collective-permute-done.left, f32[512,384]{1,0:T(8,128)S(1)} %collective-permute-done.1.right, f32[1,1024]{1,0:T(1,128)S(1)} %bitcast.41, f32[512,1]{1,0:T(8,128)S(1)} %reshape.82.damps, ...), custom_call_target="tpu_custom_call" | custom-call | flops 8858370048 | bytes 8388608 | tf_op jit(solution)/shard_map/driven/pallas_call | solution.py:474
  30.7 1.9 broadcast_select_fusion.3
  35.3 10.0 %collective-permute-start.4 = (f32[512,512]{1,0:T(8,128)}, f32[512,512]{1,0:T(8,128)}, u32[]{:S(2)}, u32[]{:S(2)}) collective-permute-start(f32[512,512]{1,0:T(8,128)} %get-tuple-element.100), channel_id=1, source_target_pairs={{0,2},{1,0},{2,3},{3,1},{5,7},{4,5},{7,6},{6,4},{8,10},{9,8},{10,1... | collective-permute-start | bytes 3145736 | tf_op jit(solution)/shard_map/ppermute | solution.py:123
  45.3 1.6 collective-permute-start.5
  52.5 2.9 constant_dynamic-slice_fusion.2
  55.4 2.5 collective-permute-start.11
  57.9 3.0 start.1
  60.9 2.4 broadcast_select_fusion.1
  63.8 1.9 fusion.31
  67.0 14.0 %collective-permute-start.7 = (f32[1024,384]{1,0:T(8,128)}, f32[1024,384]{1,0:T(8,128)}, u32[]{:S(2)}, u32[]{:S(2)}) collective-permute-start(f32[1024,384]{1,0:T(8,128)} %get-tuple-element.99), channel_id=1, source_target_pairs={{0,2},{2,1},{1,3},{3,5},{5,7},{7,4},{4,6},{6,8},{8,10},{10,9},{9,1... | collective-permute-start | bytes 4718600 | tf_op jit(solution)/shard_map/ppermute | solution.py:187
  83.1 15.1 %collective-permute-done.9 = f32[32,16]{0,1:T(8,128)S(1)} collective-permute-done((f32[32,16]{0,1:T(8,128)S(1)}, f32[32,16]{0,1:T(8,128)S(1)}, u32[]{:S(2)}, u32[]{:S(2)}) %collective-permute-start.9) | collective-permute-done | bytes 2080 | tf_op jit(solution)/shard_map/ppermute | solution.py:615
  99.7 1.6 copy-done.9
  103.3 2.7 tone0.1.refs_1_
  106.0 1.9 select_select_fusion.coupling
  109.2 7.8 %image0.1 = (f32[1024,512]{1,0:T(8,128)S(1)}, f32[32,1,128]{2,1,0:T(1,128)S(1)}, f32[1024,384]{1,0:T(8,128)S(1)}, f32[1024,384]{1,0:T(8,128)S(1)}) custom-call(f32[1024,512]{1,0:T(8,128)S(1)} %maximum_subtract_fusion.refs_0_.refs_2_.refs_1_.refs_3_.refs_4_, f32[1024,512]{1,0:T(8,128)S(1)} %tone0.1.refs_1_, ...), custom_call_target="tpu_custom_call" | custom-call | flops 5637144576 | bytes 8388608 | tf_op jit(solution)/shard_map/image0/pallas_call | solution.py:474
  117.0 13.5 %all_to_all.20.refs_0_ = f32[32,1,128]{2,1,0:T(1,128)S(1)} all-to-all(f32[32,1,128]{2,1,0:T(1,128)S(1)} %get-tuple-element.55), channel_id=1, replica_groups=mesh['node'=16,'tone'=2] {'node','tone'}, dimensions={0} | all-to-all | bytes 32768 | tf_op jit(solution)/shard_map/all_to_all | solution.py:683
  130.6 1.8 collective-permute-start.12
  133.7 3.4 %tone1.1 = (f32[1024,512]{1,0:T(8,128)S(1)}, f32[1024,512]{1,0:T(8,128)S(1)}) custom-call(f32[32,1,128]{2,1,0:T(1,128)S(1)} %all_to_all.20.refs_0_, f32[1024,512]{1,0:T(8,128)S(1)} %get-tuple-element.57.refs_1_, f32[1024,512]{1,0:T(8,128)S(1)} %maximum_subtract_fusion.refs_0_.refs_2_.refs_1_.refs_3_.refs_4_, f32[1024,512]{1,0:T(8,128)S(1)} %copy-done.10, ...), custom_call_target="tpu_custom_call" | custom-call | flops 1610612736 | bytes 8388608 | tf_op jit(solution)/shard_map/tone1/pallas_call | solution.py:357
  137.9 8.8 %image1.1 = (f32[1024,512]{1,0:T(8,128)S(1)}, f32[32,1,128]{2,1,0:T(1,128)S(1)}, f32[1024,384]{1,0:T(8,128)S(1)}, f32[1024,384]{1,0:T(8,128)S(1)}, f32[1024,384]{1,0:T(8,128)S(1)}, /*index=5*/f32[1024,384]{1,0:T(8,128)S(1)}) custom-call(f32[32,1,128]{2,1,0:T(1,128)S(1)} %all_to_all.20.refs_0_, ...), custom_call_target="tpu_custom_call" | custom-call | flops 5637144576 | bytes 14680064 | tf_op jit(solution)/shard_map/image1/pallas_call | solution.py:474
  146.7 26.3 %all_to_all.21.refs_1_ = f32[32,1,128]{2,1,0:T(1,128)S(1)} all-to-all(f32[32,1,128]{2,1,0:T(1,128)S(1)} %get-tuple-element.64), channel_id=1, replica_groups=mesh['node'=16,'tone'=2] {'node','tone'}, dimensions={0} | all-to-all | bytes 32768 | tf_op jit(solution)/shard_map/all_to_all | solution.py:683
  173.0 1.8 collective-permute-start.14
  176.1 3.7 %tone2.1 = (f32[1024,512]{1,0:T(8,128)S(1)}, f32[1024,512]{1,0:T(8,128)S(1)}) custom-call(f32[32,1,128]{2,1,0:T(1,128)S(1)} %all_to_all.20.refs_0_, f32[32,1,128]{2,1,0:T(1,128)S(1)} %all_to_all.21.refs_1_, f32[1024,512]{1,0:T(8,128)S(1)} %get-tuple-element.66.refs_2_, f32[1024,512]{1,0:T(8,128)S(1)} %maximum_subtract_fusion.refs_0_.refs_2_.refs_1_.refs_3_.refs_4_, ...), custom_call_target="tpu_custom_call" | custom-call | flops 1610612736 | bytes 8388608 | tf_op jit(solution)/shard_map/tone2/pallas_call | solution.py:357
  180.3 9.3 %image2.1 = (f32[1024,512]{1,0:T(8,128)S(1)}, f32[32,1,128]{2,1,0:T(1,128)S(1)}, f32[1024,384]{1,0:T(8,128)S(1)}, f32[1024,384]{1,0:T(8,128)S(1)}, f32[1024,384]{1,0:T(8,128)S(1)}, /*index=5*/f32[1024,384]{1,0:T(8,128)S(1)}) custom-call(f32[32,1,128]{2,1,0:T(1,128)S(1)} %all_to_all.20.refs_0_, f32[32,1,128]{2,1,0:T(1,128)S(1)} %all_to_all.21.refs_1_, ...), custom_call_target="tpu_custom_call" | custom-call | flops 5637144576 | bytes 20971520 | tf_op jit(solution)/shard_map/image2/pallas_call | solution.py:474
  189.6 26.1 %all_to_all.22.refs_2_ = f32[32,1,128]{2,1,0:T(1,128)S(1)} all-to-all(f32[32,1,128]{2,1,0:T(1,128)S(1)} %get-tuple-element.75), channel_id=1, replica_groups=mesh['node'=16,'tone'=2] {'node','tone'}, dimensions={0} | all-to-all | bytes 32768 | tf_op jit(solution)/shard_map/all_to_all | solution.py:683
  215.7 1.8 collective-permute-start.16
  219.0 4.0 %tone3.1 = (f32[1024,512]{1,0:T(8,128)S(1)}, f32[1024,512]{1,0:T(8,128)S(1)}) custom-call(f32[32,1,128]{2,1,0:T(1,128)S(1)} %all_to_all.20.refs_0_, f32[32,1,128]{2,1,0:T(1,128)S(1)} %all_to_all.21.refs_1_, f32[32,1,128]{2,1,0:T(1,128)S(1)} %all_to_all.22.refs_2_, f32[1024,512]{1,0:T(8,128)S(1)} %get-tuple-element.77.refs_3_, ...), custom_call_target="tpu_custom_call" | custom-call | flops 1610612736 | bytes 8388608 | tf_op jit(solution)/shard_map/tone3/pallas_call | solution.py:357
  223.0 10.3 %image3.1 = (f32[1024,512]{1,0:T(8,128)S(1)}, f32[32,1,128]{2,1,0:T(1,128)}) custom-call(f32[32,1,128]{2,1,0:T(1,128)S(1)} %all_to_all.20.refs_0_, f32[32,1,128]{2,1,0:T(1,128)S(1)} %all_to_all.21.refs_1_, f32[32,1,128]{2,1,0:T(1,128)S(1)} %all_to_all.22.refs_2_, f32[1024,512]{1,0:T(8,128)S(1)} %maximum_subtract_fusion.refs_0_.refs_2_.refs_1_.refs_3_.refs_4_, ...), custom_call_target="tpu_custom_call" | custom-call | flops 5637144576 | bytes 27262976 | tf_op jit(solution)/shard_map/image3/pallas_call | solution.py:474
  234.7 18.8 %all-to-all-start.3 = ((f32[32,1,128]{2,1,0:T(1,128)}), f32[32,1,128]{2,1,0:T(1,128)S(1)}, u32[]{:S(2)}, u32[]{:S(2)}) async-start(f32[32,1,128]{2,1,0:T(1,128)} %get-tuple-element.84), calls=%async_computation.3 | async-start | bytes 32768 | tf_op jit(solution)/shard_map/all_to_all | solution.py:683
  253.5 7.2 %all-to-all-done.3.refs_3_ = f32[32,1,128]{2,1,0:T(1,128)S(1)} async-done(((f32[32,1,128]{2,1,0:T(1,128)}), f32[32,1,128]{2,1,0:T(1,128)S(1)}, u32[]{:S(2)}, u32[]{:S(2)}) %all-to-all-start.3) | async-done | bytes 16416 | tf_op jit(solution)/shard_map/all_to_all | solution.py:683
  260.7 1.6 copy-done.3
  262.3 1.6 copy-done.6
  263.9 1.6 copy-done.12
  265.5 1.6 copy-done.27
  267.1 2.5 update.1
  269.6 1.7 dynamic-slice_select_fusion.2
  272.2 1.8 collective-permute-start.18
  274.0 2.9 remaining.1
  278.5 1.8 collective-permute-start.21
  280.3 1.7 collective-permute-start.20
  282.0 12.7 %collective-permute-done.19 = f32[512,512]{1,0:T(8,128)} collective-permute-done((f32[512,512]{1,0:T(8,128)}, f32[512,512]{1,0:T(8,128)}, u32[]{:S(2)}, u32[]{:S(2)}) %collective-permute-start.19) | collective-permute-done | bytes 1048608 | tf_op jit(solution)/shard_map/ppermute | solution.py:150
  294.6 1.6 broadcast_select_fusion.11
  297.7 19.4 %collective-permute-done.21 = f32[512,512]{1,0:T(8,128)} collective-permute-done((f32[512,512]{1,0:T(8,128)}, f32[512,512]{1,0:T(8,128)}, u32[]{:S(2)}, u32[]{:S(2)}) %collective-permute-start.21) | collective-permute-done | bytes 1048608 | tf_op jit(solution)/shard_map/ppermute | solution.py:150
  (157 shorter events, 40.5 us)
Async XLA Ops:
  0.6 11.9 %copy-start.28 = (f32[32,16,1024]{2,1,0:T(8,128)S(1)}, f32[32,16,1024]{2,1,0:T(8,128)}, u32[]{:S(2)}) copy-start(f32[32,16,1024]{2,1,0:T(8,128)} %param.9) | copy-start | bytes 6291460
  4.1 47.5 %collective-permute-start.6 = (f32[8,512]{1,0:T(8,128)}, f32[8,512]{1,0:T(8,128)}, u32[]{:S(2)}, u32[]{:S(2)}) collective-permute-start(f32[8,512]{1,0:T(8,128)} %constant_dynamic-slice_fusion.5), channel_id=1, source_target_pairs={{0,2},{1,3},{2,0},{3,1},{4,6},{5,7},{6,4},{7,5},{8,10},{9,11},{10,... | collective-permute-start | bytes 49160 | tf_op jit(solution)/shard_map/ppermute | solution.py:103
  7.3 17.9 %collective-permute-start.1 = (f32[512,384]{1,0:T(8,128)}, f32[512,384]{1,0:T(8,128)S(1)}, u32[]{:S(2)}, u32[]{:S(2)}) collective-permute-start(f32[512,384]{1,0:T(8,128)} %get-tuple-element.104), channel_id=1, source_target_pairs={{2,0},{3,1},{4,2},{5,3},{6,4},{7,5},{8,6},{9,7},{10,8},{11,9},{12,... | collective-permute-start | bytes 2359304 | tf_op jit(solution)/shard_map/ppermute | solution.py:188
  8.6 16.7 %collective-permute-start = (f32[512,384]{1,0:T(8,128)}, f32[512,384]{1,0:T(8,128)}, u32[]{:S(2)}, u32[]{:S(2)}) collective-permute-start(f32[512,384]{1,0:T(8,128)} %get-tuple-element.105), channel_id=1, source_target_pairs={{0,2},{1,3},{2,4},{3,5},{4,6},{5,7},{6,8},{7,9},{8,10},{9,11},{10,... | collective-permute-start | bytes 2359304 | tf_op jit(solution)/shard_map/ppermute | solution.py:187
  12.5 5.4 %copy-start.44 = (s32[8,7]{1,0:T(8,128)S(1)}, s32[8,7]{1,0:T(8,128)}, u32[]{:S(2)}) copy-start(s32[8,7]{1,0:T(8,128)} %param.13) | copy-start | bytes 676
  12.5 5.4 %copy-start.42 = (f32[32,16]{0,1:T(8,128)S(1)}, f32[32,16]{0,1:T(8,128)}, u32[]{:S(2)}) copy-start(f32[32,16]{0,1:T(8,128)} %param.15) | copy-start | bytes 6148
  12.5 7.0 %copy-start.33 = (s32[7]{0:T(128)S(1)}, s32[7]{0:T(128)}, u32[]{:S(2)}) copy-start(s32[7]{0:T(128)} %band_code.3) | copy-start | bytes 88
  14.1 16.6 %collective-permute-start.2 = (f32[512,512]{1,0:T(8,128)}, f32[512,512]{1,0:T(8,128)}, u32[]{:S(2)}, u32[]{:S(2)}) collective-permute-start(f32[512,512]{1,0:T(8,128)} %get-tuple-element.102), channel_id=1, source_target_pairs={{0,2},{1,0},{2,3},{3,1},{5,7},{4,5},{7,6},{6,4},{8,10},{9,8},{10,1... | collective-permute-start | bytes 3145736 | tf_op jit(solution)/shard_map/ppermute | solution.py:123
  15.3 15.4 %collective-permute-start.3 = (f32[512,512]{1,0:T(8,128)}, f32[512,512]{1,0:T(8,128)}, u32[]{:S(2)}, u32[]{:S(2)}) collective-permute-start(f32[512,512]{1,0:T(8,128)} %get-tuple-element.103), channel_id=1, source_target_pairs={{1,2},{2,1},{4,7},{7,4},{9,10},{10,9},{12,15},{15,12},{17,18},{18,... | collective-permute-start | bytes 3145736 | tf_op jit(solution)/shard_map/ppermute | solution.py:124
  21.6 3.3 %copy-start.39 = (s32[256]{0:T(256)S(1)}, s32[256]{0:T(256)}, u32[]{:S(2)}) copy-start(s32[256]{0:T(256)} %copy-done.38) | copy-start | bytes 3076
  21.6 3.7 %copy-start.32 = (f32[1024]{0:T(1024)S(1)}, f32[1024]{0:T(1024)}, u32[]{:S(2)}) copy-start(f32[1024]{0:T(1024)} %param.14) | copy-start | bytes 12292
  21.6 3.7 %copy-start.34 = (f32[32,16,1024]{2,1,0:T(8,128)S(1)}, f32[32,16,1024]{2,1,0:T(8,128)}, u32[]{:S(2)}) copy-start(f32[32,16,1024]{2,1,0:T(8,128)} %param.10) | copy-start | bytes 6291460
  35.3 25.6 %collective-permute-start.4 = (f32[512,512]{1,0:T(8,128)}, f32[512,512]{1,0:T(8,128)}, u32[]{:S(2)}, u32[]{:S(2)}) collective-permute-start(f32[512,512]{1,0:T(8,128)} %get-tuple-element.100), channel_id=1, source_target_pairs={{0,2},{1,0},{2,3},{3,1},{5,7},{4,5},{7,6},{6,4},{8,10},{9,8},{10,1... | collective-permute-start | bytes 3145736 | tf_op jit(solution)/shard_map/ppermute | solution.py:123
  45.3 15.6 %collective-permute-start.5 = (f32[512,512]{1,0:T(8,128)S(1)}, f32[512,512]{1,0:T(8,128)}, u32[]{:S(2)}, u32[]{:S(2)}) collective-permute-start(f32[512,512]{1,0:T(8,128)S(1)} %get-tuple-element.101), channel_id=1, source_target_pairs={{1,2},{2,1},{4,7},{7,4},{9,10},{10,9},{12,15},{15,12},{17,18},{18,... | collective-permute-start | bytes 3145736 | tf_op jit(solution)/shard_map/ppermute | solution.py:124
  47.7 10.2 %copy-start.16 = (bf16[4,256,256]{2,1,0:T(8,128)(2,1)}, bf16[4,256,256]{2,1,0:T(8,128)(2,1)S(1)}, u32[]{:S(2)}) copy-start(bf16[4,256,256]{2,1,0:T(8,128)(2,1)S(1)} %get-tuple-element.106.refs_3_.refs_5_.refs_7_.refs_9_.refs_11_) | copy-start | bytes 1572868
  47.8 10.2 %copy-start.19 = (bf16[4,256,256]{2,1,0:T(8,128)(2,1)}, bf16[4,256,256]{2,1,0:T(8,128)(2,1)S(1)}, u32[]{:S(2)}) copy-start(bf16[4,256,256]{2,1,0:T(8,128)(2,1)S(1)} %get-tuple-element.107.refs_2_.refs_4_.refs_6_.refs_8_.refs_10_) | copy-start | bytes 1572868
  47.8 3.8 %copy-start.37 = (f32[8,1024]{1,0:T(8,128)S(1)}, f32[8,1024]{1,0:T(8,128)}, u32[]{:S(2)}) copy-start(f32[8,1024]{1,0:T(8,128)} %copy-done.36) | copy-start | bytes 98308
  51.6 6.4 %copy-start.26 = (f32[1024,512]{1,0:T(8,128)S(1)}, f32[1024,512]{1,0:T(8,128)}, u32[]{:S(2)}) copy-start(f32[1024,512]{1,0:T(8,128)} %pad_maximum_fusion.volts.refs_8_) | copy-start | bytes 6291460
  55.4 50.6 %collective-permute-start.11 = (f32[4,7,128,128]{3,2,1,0:T(8,128)}, f32[4,7,128,128]{3,2,1,0:T(8,128)}, u32[]{:S(2)}, u32[]{:S(2)}) collective-permute-start(f32[4,7,128,128]{3,2,1,0:T(8,128)} %constant_dynamic-slice_fusion.2), channel_id=1, source_target_pairs={{0,2},{1,3},{2,0},{3,1},{4,6},{5,7},{6,4},{7,5},{8,10},{9,11},{10,... | collective-permute-start | bytes 5505032 | tf_op jit(solution)/shard_map/ppermute | solution.py:103
  63.8 17.2 %copy-start.43 = (f32[32,16]{0,1:T(8,128)S(1)}, f32[32,16]{0,1:T(8,128)}, u32[]{:S(2)}) copy-start(f32[32,16]{0,1:T(8,128)} %param.15) | copy-start | bytes 6148
  63.8 17.9 %copy-start.35 = (f32[32,16]{1,0:T(8,128)S(1)}, f32[32,16]{1,0:T(8,128)}, u32[]{:S(2)}) copy-start(f32[32,16]{1,0:T(8,128)} %copy.30) | copy-start | bytes 6148
  65.7 43.4 %collective-permute-start.8 = (f32[1024,384]{1,0:T(8,128)}, f32[1024,384]{1,0:T(8,128)}, u32[]{:S(2)}, u32[]{:S(2)}) collective-permute-start(f32[1024,384]{1,0:T(8,128)} %get-tuple-element.98), channel_id=1, source_target_pairs={{2,0},{1,2},{3,1},{5,3},{7,5},{4,7},{6,4},{8,6},{10,8},{9,10},{11,... | collective-permute-start | bytes 4718600 | tf_op jit(solution)/shard_map/ppermute | solution.py:188
  67.0 42.1 %collective-permute-start.7 = (f32[1024,384]{1,0:T(8,128)}, f32[1024,384]{1,0:T(8,128)}, u32[]{:S(2)}, u32[]{:S(2)}) collective-permute-start(f32[1024,384]{1,0:T(8,128)} %get-tuple-element.99), channel_id=1, source_target_pairs={{0,2},{2,1},{1,3},{3,5},{5,7},{7,4},{4,6},{6,8},{8,10},{10,9},{9,1... | collective-permute-start | bytes 4718600 | tf_op jit(solution)/shard_map/ppermute | solution.py:187
  81.0 17.3 %collective-permute-start.9 = (f32[32,16]{0,1:T(8,128)S(1)}, f32[32,16]{0,1:T(8,128)S(1)}, u32[]{:S(2)}, u32[]{:S(2)}) collective-permute-start(f32[32,16]{0,1:T(8,128)S(1)} %copy-done.43), channel_id=1, source_target_pairs={{0,1},{1,0},{2,3},{3,2},{4,5},{5,4},{6,7},{7,6},{8,9},{9,8},{10,11... | collective-permute-start | bytes 6152 | tf_op jit(solution)/shard_map/ppermute | solution.py:615
  81.5 1.6 collective-permute-start.10
  109.1 24.5 %copy-start.10 = (f32[1024,512]{1,0:T(8,128)S(1)}, f32[1024,512]{1,0:T(8,128)}, u32[]{:S(2)}) copy-start(f32[1024,512]{1,0:T(8,128)} %copy-done.8) | copy-start | bytes 6291460
  109.2 24.5 %copy-start.18 = (bf16[4,256,256]{2,1,0:T(8,128)(2,1)S(1)}, bf16[4,256,256]{2,1,0:T(8,128)(2,1)}, u32[]{:S(2)}) copy-start(bf16[4,256,256]{2,1,0:T(8,128)(2,1)} %copy-done.16) | copy-start | bytes 1572868
  109.2 24.5 %copy-start.21 = (bf16[4,256,256]{2,1,0:T(8,128)(2,1)S(1)}, bf16[4,256,256]{2,1,0:T(8,128)(2,1)}, u32[]{:S(2)}) copy-start(bf16[4,256,256]{2,1,0:T(8,128)(2,1)} %copy-done.19) | copy-start | bytes 1572868
  130.6 6.6 %collective-permute-start.12 = (f32[1024,384]{1,0:T(8,128)S(1)}, f32[1024,384]{1,0:T(8,128)S(1)}, u32[]{:S(2)}, u32[]{:S(2)}) collective-permute-start(f32[1024,384]{1,0:T(8,128)S(1)} %get-tuple-element.60), channel_id=1, source_target_pairs={{0,2},{2,1},{1,3},{3,5},{5,7},{7,4},{4,6},{6,8},{8,10},{10,9},{9,1... | collective-permute-start | bytes 4718600 | tf_op jit(solution)/shard_map/ppermute | solution.py:187
  132.4 5.5 %collective-permute-start.13 = (f32[1024,384]{1,0:T(8,128)S(1)}, f32[1024,384]{1,0:T(8,128)S(1)}, u32[]{:S(2)}, u32[]{:S(2)}) collective-permute-start(f32[1024,384]{1,0:T(8,128)S(1)} %get-tuple-element.61), channel_id=1, source_target_pairs={{2,0},{1,2},{3,1},{5,3},{7,5},{4,7},{6,4},{8,6},{10,8},{9,10},{11,... | collective-permute-start | bytes 4718600 | tf_op jit(solution)/shard_map/ppermute | solution.py:188
  137.1 85.9 %copy-start.2 = (f32[1024,512]{1,0:T(8,128)}, f32[1024,512]{1,0:T(8,128)S(1)}, u32[]{:S(2)}) copy-start(f32[1024,512]{1,0:T(8,128)S(1)} %get-tuple-element.58.refs_2_.refs_4_.refs_3_.refs_5_) | copy-start | bytes 6291460
  173.0 6.8 %collective-permute-start.14 = (f32[1024,384]{1,0:T(8,128)S(1)}, f32[1024,384]{1,0:T(8,128)S(1)}, u32[]{:S(2)}, u32[]{:S(2)}) collective-permute-start(f32[1024,384]{1,0:T(8,128)S(1)} %get-tuple-element.69), channel_id=1, source_target_pairs={{0,2},{2,1},{1,3},{3,5},{5,7},{7,4},{4,6},{6,8},{8,10},{10,9},{9,1... | collective-permute-start | bytes 4718600 | tf_op jit(solution)/shard_map/ppermute | solution.py:187
  174.8 5.5 %collective-permute-start.15 = (f32[1024,384]{1,0:T(8,128)S(1)}, f32[1024,384]{1,0:T(8,128)S(1)}, u32[]{:S(2)}, u32[]{:S(2)}) collective-permute-start(f32[1024,384]{1,0:T(8,128)S(1)} %get-tuple-element.70), channel_id=1, source_target_pairs={{2,0},{1,2},{3,1},{5,3},{7,5},{4,7},{6,4},{8,6},{10,8},{9,10},{11,... | collective-permute-start | bytes 4718600 | tf_op jit(solution)/shard_map/ppermute | solution.py:188
  179.8 43.3 %copy-start.5 = (f32[1024,512]{1,0:T(8,128)}, f32[1024,512]{1,0:T(8,128)S(1)}, u32[]{:S(2)}) copy-start(f32[1024,512]{1,0:T(8,128)S(1)} %get-tuple-element.67.refs_4_.refs_6_.refs_5_) | copy-start | bytes 6291460
  215.7 7.3 %collective-permute-start.16 = (f32[1024,384]{1,0:T(8,128)S(1)}, f32[1024,384]{1,0:T(8,128)S(1)}, u32[]{:S(2)}, u32[]{:S(2)}) collective-permute-start(f32[1024,384]{1,0:T(8,128)S(1)} %get-tuple-element.80), channel_id=1, source_target_pairs={{0,2},{2,1},{1,3},{3,5},{5,7},{7,4},{4,6},{6,8},{8,10},{10,9},{9,1... | collective-permute-start | bytes 4718600 | tf_op jit(solution)/shard_map/ppermute | solution.py:187
  217.5 5.5 %collective-permute-start.17 = (f32[1024,384]{1,0:T(8,128)S(1)}, f32[1024,384]{1,0:T(8,128)S(1)}, u32[]{:S(2)}, u32[]{:S(2)}) collective-permute-start(f32[1024,384]{1,0:T(8,128)S(1)} %get-tuple-element.81), channel_id=1, source_target_pairs={{2,0},{1,2},{3,1},{5,3},{7,5},{4,7},{6,4},{8,6},{10,8},{9,10},{11,... | collective-permute-start | bytes 4718600 | tf_op jit(solution)/shard_map/ppermute | solution.py:188
  223.0 10.4 %copy-start.11 = (f32[1024,512]{1,0:T(8,128)}, f32[1024,512]{1,0:T(8,128)S(1)}, u32[]{:S(2)}) copy-start(f32[1024,512]{1,0:T(8,128)S(1)} %get-tuple-element.78.refs_6_.refs_7_) | copy-start | bytes 6291460
  234.7 26.0 %all-to-all-start.3 = ((f32[32,1,128]{2,1,0:T(1,128)}), f32[32,1,128]{2,1,0:T(1,128)S(1)}, u32[]{:S(2)}, u32[]{:S(2)}) async-start(f32[32,1,128]{2,1,0:T(1,128)} %get-tuple-element.84), calls=%async_computation.3 | async-start | bytes 32768 | tf_op jit(solution)/shard_map/all_to_all | solution.py:683
  267.1 6.9 %copy-start.13 = (f32[1024,512]{1,0:T(8,128)S(1)}, f32[1024,512]{1,0:T(8,128)}, u32[]{:S(2)}) copy-start(f32[1024,512]{1,0:T(8,128)} %copy-done.11) | copy-start | bytes 6291460
  267.1 6.9 %copy-start.31 = (f32[1024,512]{1,0:T(8,128)S(1)}, f32[1024,512]{1,0:T(8,128)}, u32[]{:S(2)}) copy-start(f32[1024,512]{1,0:T(8,128)} %copy-done.30) | copy-start | bytes 6291460
  269.6 4.4 %copy-start.4 = (f32[1024,512]{1,0:T(8,128)S(1)}, f32[1024,512]{1,0:T(8,128)}, u32[]{:S(2)}) copy-start(f32[1024,512]{1,0:T(8,128)} %copy-done.2) | copy-start | bytes 6291460
  269.6 4.4 %copy-start.7 = (f32[1024,512]{1,0:T(8,128)S(1)}, f32[1024,512]{1,0:T(8,128)}, u32[]{:S(2)}) copy-start(f32[1024,512]{1,0:T(8,128)} %copy-done.5) | copy-start | bytes 6291460
  271.7 22.9 %collective-permute-start.19 = (f32[512,512]{1,0:T(8,128)}, f32[512,512]{1,0:T(8,128)}, u32[]{:S(2)}, u32[]{:S(2)}) collective-permute-start(f32[512,512]{1,0:T(8,128)} %get-tuple-element.88), channel_id=1, source_target_pairs={{2,0},{0,1},{3,2},{1,3},{7,5},{5,4},{6,7},{4,6},{10,8},{8,9},{11,1... | collective-permute-start | bytes 3145736 | tf_op jit(solution)/shard_map/ppermute | solution.py:150
  272.2 22.4 %collective-permute-start.18 = (f32[512,512]{1,0:T(8,128)}, f32[512,512]{1,0:T(8,128)}, u32[]{:S(2)}, u32[]{:S(2)}) collective-permute-start(f32[512,512]{1,0:T(8,128)} %get-tuple-element.89), channel_id=1, source_target_pairs={{2,1},{1,2},{7,4},{4,7},{10,9},{9,10},{15,12},{12,15},{18,17},{17,... | collective-permute-start | bytes 3145736 | tf_op jit(solution)/shard_map/ppermute | solution.py:151
  276.8 17.8 %copy-start.25 = (f32[1024,512]{1,0:T(8,128)S(1)}, f32[1024,512]{1,0:T(8,128)}, u32[]{:S(2)}) copy-start(f32[1024,512]{1,0:T(8,128)} %copy-done.24) | copy-start | bytes 6291460
  278.5 38.6 %collective-permute-start.21 = (f32[512,512]{1,0:T(8,128)}, f32[512,512]{1,0:T(8,128)}, u32[]{:S(2)}, u32[]{:S(2)}) collective-permute-start(f32[512,512]{1,0:T(8,128)} %get-tuple-element.86), channel_id=1, source_target_pairs={{2,0},{0,1},{3,2},{1,3},{7,5},{5,4},{6,7},{4,6},{10,8},{8,9},{11,1... | collective-permute-start | bytes 3145736 | tf_op jit(solution)/shard_map/ppermute | solution.py:150
  280.3 36.8 %collective-permute-start.20 = (f32[512,512]{1,0:T(8,128)S(1)}, f32[512,512]{1,0:T(8,128)}, u32[]{:S(2)}, u32[]{:S(2)}) collective-permute-start(f32[512,512]{1,0:T(8,128)S(1)} %get-tuple-element.87), channel_id=1, source_target_pairs={{2,1},{1,2},{7,4},{4,7},{10,9},{9,10},{15,12},{12,15},{18,17},{17,... | collective-permute-start | bytes 3145736 | tf_op jit(solution)/shard_map/ppermute | solution.py:151
  296.2 20.9 %copy-start.23 = (f32[1024,512]{1,0:T(8,128)S(1)}, f32[1024,512]{1,0:T(8,128)}, u32[]{:S(2)}) copy-start(f32[1024,512]{1,0:T(8,128)} %copy-done.22) | copy-start | bytes 6291460
  (20 other events, 32.5 us)

commit v2 on v1

--- a/solution.py
+++ b/solution.py
@@ -345,7 +345,7 @@
     return width // 2 if width % 256 == 0 else width
 
 
-def columns_call(kernel, name, parts, fields, small, tables, outs):
+def columns_call(kernel, parts, fields, small, tables, outs):
     rows, width = fields[0].shape
     block = column_block(width)
     whole = pl.BlockSpec((rows, block), lambda i: (0, i))
@@ -356,7 +356,6 @@
     specs += [once(t.shape, lambda i: (0, 0, 0)) for t in tables]
     return pl.pallas_call(
         kernel,
-        name=name,
         grid=(width // block,),
         in_specs=specs,
         out_specs=[whole] * outs,
@@ -450,7 +449,7 @@
         stats[...] = jnp.broadcast_to(row[None], stats.shape)
 
 
-def rows_call(kernel, name, parts, fields, caps, damps, operator, outs, stats, scratch):
+def rows_call(kernel, parts, fields, caps, damps, operator, outs, stats, scratch):
     rows, width = fields[0].shape
     block = min(rows, ROWS)
     once = functools.partial(pl.BlockSpec, pipeline_mode=pl.Buffered(1))
@@ -473,7 +472,6 @@
     flops = 12 * rows * width * (width + HALO_B * NB) if operator else 16 * rows * width
     return pl.pallas_call(
         kernel,
-        name=name,
         grid=(rows // block,),
         in_specs=specs,
         out_specs=out_specs,
@@ -570,22 +568,17 @@
     return answer, fitted
 
 
-def update_kernel(*refs):
-    parts, basis, (volts, out) = refs[:M], refs[M : 2 * M], refs[2 * M :]
-    answer, _ = answer_of(parts)
+def final_kernel(*refs):
+    parts, basis, (volts, image, updated, remaining) = refs[:M], refs[M : 2 * M], refs[2 * M :]
+    answer, fitted = answer_of(parts)
     total = answer[0] * basis[0][...]
+    rest = basis[0][...] - fitted[0] * basis[0][...]
     for j in range(1, M):
-        total = total + answer[j] * basis[j][...]
-    out[...] = volts[...] + total
-
-
-def remaining_kernel(*refs):
-    parts, basis, (image, out) = refs[:M], refs[M : 2 * M], refs[2 * M :]
-    answer, fitted = answer_of(parts)
-    total = basis[0][...] - fitted[0] * basis[0][...]
-    for i in range(1, M):
-        total = total - fitted[i] * basis[i][...]
-    out[...] = total - answer[M - 1] * image[...]
+        vector = basis[j][...]
+        total = total + answer[j] * vector
+        rest = rest - fitted[j] * vector
+    updated[...] = volts[...] + total
+    remaining[...] = rest - answer[M - 1] * image[...]
 
 
 def make(nodes, tones):
@@ -609,7 +602,6 @@
             [per_node, cap[None, :], jnp.zeros((4, cap.shape[0]), F32)], axis=0
         )
         per_node = chunk_of(chain, per_node, place, 1)
-        caps = per_node[3:4]
         damps = jnp.zeros((tones, local, 1), F32)
         for s in range(tones):
             piece = lax.ppermute(damp, AXES, chain.shift(s)) if s else damp
@@ -625,7 +617,6 @@
         left, right = halos(*edges_of(volts_here), chain.node_up, chain.node_down)
         (driven,) = rows_call(
             residual_kernel,
-            "driven",
             [],
             [source.reshape(local, shape[2]), volts_here, left, right],
             cap[None, :],
@@ -635,17 +626,20 @@
             0,
             ext_scratch(shape[2]),
         )
-        driven, volts, coupling = lax.optimization_barrier((driven, volts, coupling))
-        driven = gather_tones(chain, driven.reshape(shape), place)
-
         mine = chunk_of(chain, coupling, place, 0)
         mine_active = chunk_of(chain, active.astype(F32), place, 0)
+        driven, damps, mine, mine_active, per_node = lax.optimization_barrier(
+            (driven, damps, mine, mine_active, per_node)
+        )
+        caps = per_node[3:4]
+        driven = gather_tones(chain, driven.reshape(shape), place)
+
         operator = band_operator(mine, band_code, mine_active)
         tables = two_tone_tables(k1, k2, tones)
         groups = pieces_of(k1, tones, rows)
 
         slope, back = columns_call(
-            functools.partial(start_kernel, groups), "start", [], [volts], [per_node], tables, 2
+            functools.partial(start_kernel, groups), [], [volts], [per_node], tables, 2
         )
         start = driven - back
 
@@ -656,7 +650,6 @@
         for column in range(M):
             made = columns_call(
                 functools.partial(tone_kernel, groups, column),
-                f"tone{column}",
                 parts,
                 [image, *basis, slope],
                 [],
@@ -667,7 +660,6 @@
             more = column + 1 < M
             made = rows_call(
                 functools.partial(image_kernel, column, more),
-                f"image{column}",
                 parts,
                 [*basis, new, toned, left, right, *lefts, *rights],
                 caps,
@@ -680,21 +672,26 @@
             )
             image, stats = made[:2]
             basis.append(new)
-            part = lax.all_to_all(stats, AXES, 0, 0, tiled=True)
             if more:
                 lefts.append(made[2] if column else left)
                 rights.append(made[3] if column else right)
-                last, first, part = lax.optimization_barrier((*made[-2:], part))
-                left, right = halos(last, first, chain.up, chain.down)
+                left, right = halos(*made[-2:], chain.up, chain.down)
+            part = lax.all_to_all(stats, AXES, 0, 0, tiled=True)
             parts = parts + [part]
 
-        def final(kernel, name, last):
-            return rows_call(
-                kernel, name, parts, [*basis, last], None, None, [], [(rows, width)], 0, lambda block: []
-            )[0]
-
-        new_volts = scatter_tones(chain, final(update_kernel, "update", volts), place, shape)
-        remaining = scatter_tones(chain, final(remaining_kernel, "remaining", image), place, shape)
+        new_volts, remaining = rows_call(
+            final_kernel,
+            parts,
+            [*basis, volts, image],
+            None,
+            None,
+            [],
+            [(rows, width)] * 2,
+            0,
+            lambda block: [],
+        )
+        new_volts = scatter_tones(chain, new_volts, place, shape)
+        remaining = scatter_tones(chain, remaining, place, shape)
         return new_volts, remaining
 
     return per_device
@@ -712,8 +709,10 @@
         P("node"),
         P(),
     )
+    body = make(mesh.shape["node"], mesh.shape["tone"])
+
     return jax.shard_map(
-        make(mesh.shape["node"], mesh.shape["tone"]),
+        body,
         mesh=mesh,
         in_specs=placed,
         out_specs=(P(None, "tone", "node"), P(None, "tone", "node")),

time: 324 us -> 313 us (0.966)
  starting transfers between devices: 72.7 us -> 58.8 us
  blocking collectives: 65.9 us -> 72.4 us
  waiting for transfers between devices: 57 us -> 50.7 us
  local copies, waits for them, and re-layouts: 32.1 us -> 37.4 us
    all_to_all x1, starting transfers between devices: 18.8 us -> 2.77 us  [per_device(): part = lax.all_to_all(stats, AXES, 0, 0, tiled=True)]
    ppermute x1, waiting for transfers between devices: 15.1 us -> 0.01 us  [per_device(): piece = lax.ppermute(damp, AXES, chain.shift(s)) if s else damp]
    ppermute x5, starting transfers between devices: 23.3 us -> 34.7 us  [halos(): left.insert(0, lax.ppermute(last[:, width - take:], AXES, up(hop)))]
    ppermute x2, starting transfers between devices: 11.3 us -> 2.11 us  [gather_tones(): got_one = lax.ppermute(one, AXES, chain.first())]
    ppermute x2, waiting for transfers between devices: 0.01 us -> 7.58 us  [gather_tones(): got_one = lax.ppermute(one, AXES, chain.first())]
    unnamed x93 -> x76, local copies, waits for them, and re-layouts: 17.3 us -> 24.1 us
    all_to_all x3, blocking collectives: 65.9 us -> 72.4 us  [per_device(): part = lax.all_to_all(stats, AXES, 0, 0, tiled=True)]
    ppermute x2, waiting for transfers between devices: 32 us -> 35.5 us  [scatter_tones(): got_one = lax.ppermute(one, AXES, flipped(chain.first()))]
  transfers between devices with their start and end apart: 23 -> 23, of which waited for: 7 -> 5; matrix products, arithmetic and copies ran while one was open for 10% -> 8% of each run, Pallas kernels for 9% -> 9%
where the time goes in v2:
time: 313 us; the launch traced here: 309 us
  blocking collectives  72.4 us (23%)
  Pallas kernels  67.5 us (22%)
  starting transfers between devices  58.8 us (19%)
  waiting for transfers between devices  50.7 us (16%)
  local copies, waits for them, and re-layouts  37.4 us (12%)
  other arithmetic  18.6 us (6%)
    all_to_all x3, blocking collectives, per_device(): part = lax.all_to_all(stats, AXES, 0, 0, tiled=True)  72.4 us
    pallas_call x6, Pallas kernels, rows_call(): pl.pallas_call(kernel, grid=(rows // block,), in_specs=specs, out_specs=o...  46.7 us
    ppermute x2, waiting for transfers between devices, scatter_tones(): got_one = lax.ppermute(one, AXES, flipped(chain.first()))  35.5 us
    ppermute x5, starting transfers between devices, halos(): left.insert(0, lax.ppermute(last[:, width - take:], AXES, up(hop)))  34.7 us
    unnamed x76, local copies, waits for them, and re-layouts  24.1 us
    pallas_call x5, Pallas kernels, columns_call(): pl.pallas_call(kernel, grid=(width // block,), in_specs=specs, out_specs=...  17 us
    ppermute x2, waiting for transfers between devices, gather_tones(): got_one = lax.ppermute(one, AXES, chain.first())  7.58 us
    all_to_all x1, waiting for transfers between devices, per_device(): part = lax.all_to_all(stats, AXES, 0, 0, tiled=True)  7.22 us
  transfers between devices with their start and end apart: 23, of which 5 were waited for; matrix products, arithmetic and copies ran while one was open for 8% of the time, Pallas kernels for 9%

profile of v2, /device:TPU:0, one launch (start us, length us, event | category | flops | bytes accessed | tf_op | source)
XLA Modules:
  0.0 309.2 jit_solution(6231107568412205799)
XLA Ops:
  1.9 2.6 collective-permute-start.2
  4.4 2.6 fusion.32
  8.5 3.9 %collective-permute-start = (f32[512,384]{1,0:T(8,128)}, f32[512,384]{1,0:T(8,128)}, u32[]{:S(2)}, u32[]{:S(2)}) collective-permute-start(f32[512,384]{1,0:T(8,128)} %get-tuple-element.93), channel_id=1, source_target_pairs={{0,2},{1,3},{2,4},{3,5},{4,6},{5,7},{6,8},{7,9},{8,10},{9,11},{10,... | collective-permute-start | bytes 2359304 | tf_op jit(solution)/shard_map/ppermute | solution.py:187
  12.4 2.9 constant_dynamic-slice_fusion.9
  18.0 2.0 copy-done.9
  20.1 2.7 operator.2
  22.7 1.8 copy-done.30
  24.6 1.8 copy-done.32
  29.9 1.6 collective-permute-start.9
  31.5 2.0 copy-done.31
  33.6 2.0 copy-done.33
  35.6 1.6 copy-done.34
  37.2 5.7 %shard_map.104 = f32[512,1024]{1,0:T(8,128)S(1)} custom-call(f32[512,1024]{1,0:T(8,128)S(1)} %bitcast.38, f32[512,1024]{1,0:T(8,128)S(1)} %bitcast.35, f32[512,384]{1,0:T(8,128)} %collective-permute-done.left, f32[512,384]{1,0:T(8,128)} %collective-permute-done.1.right, f32[1,1024]{1,0:T(1,128)S(1)} %bitcast.37, f32[512,1]{1,0:T(8,128)S(1)} %reshape.82.damps, ...), custom_call_target="tpu_custom_call" | custom-call | flops 8858370048 | bytes 8388608 | tf_op jit(solution)/shard_map/pallas_call | solution.py:473
  43.0 3.1 select_select_fusion.coupling
  48.7 1.6 collective-permute-start.7
  53.3 2.3 broadcast_select_fusion.1
  55.8 3.0 shard_map.105
  58.8 7.6 %collective-permute-done.6 = f32[512,512]{1,0:T(8,128)} collective-permute-done((f32[512,512]{1,0:T(8,128)}, f32[512,512]{1,0:T(8,128)}, u32[]{:S(2)}, u32[]{:S(2)}) %collective-permute-start.6) | collective-permute-done | bytes 1048608 | tf_op jit(solution)/shard_map/ppermute | solution.py:123
  66.4 1.6 broadcast_select_fusion.3
  68.5 2.0 fusion.31
  71.8 15.1 %collective-permute-start.10 = (f32[1024,384]{1,0:T(8,128)}, f32[1024,384]{1,0:T(8,128)}, u32[]{:S(2)}, u32[]{:S(2)}) collective-permute-start(f32[1024,384]{1,0:T(8,128)} %get-tuple-element.89), channel_id=1, source_target_pairs={{0,2},{2,1},{1,3},{3,5},{5,7},{7,4},{4,6},{6,8},{8,10},{10,9},{9,1... | collective-permute-start | bytes 4718600 | tf_op jit(solution)/shard_map/ppermute | solution.py:187
  92.2 2.7 shard_map.106.refs_1_
  95.0 7.8 %shard_map.107 = (f32[1024,512]{1,0:T(8,128)S(1)}, f32[32,1,128]{2,1,0:T(1,128)S(1)}, f32[1024,384]{1,0:T(8,128)S(1)}, f32[1024,384]{1,0:T(8,128)S(1)}) custom-call(f32[1024,512]{1,0:T(8,128)S(1)} %maximum_subtract_fusion.refs_0_.refs_2_.refs_1_.refs_3_.refs_4_, f32[1024,512]{1,0:T(8,128)S(1)} %shard_map.106.refs_1_, ...), custom_call_target="tpu_custom_call" | custom-call | flops 5637144576 | bytes 8388608 | tf_op jit(solution)/shard_map/pallas_call | solution.py:473
  102.8 12.1 %collective-permute-start.12 = (f32[1024,384]{1,0:T(8,128)S(1)}, f32[1024,384]{1,0:T(8,128)S(1)}, u32[]{:S(2)}, u32[]{:S(2)}) collective-permute-start(f32[1024,384]{1,0:T(8,128)S(1)} %get-tuple-element.54), channel_id=1, source_target_pairs={{0,2},{2,1},{1,3},{3,5},{5,7},{7,4},{4,6},{6,8},{8,10},{10,9},{9,1... | collective-permute-start | bytes 4718600 | tf_op jit(solution)/shard_map/ppermute | solution.py:187
  116.2 26.5 %all_to_all.20.refs_0_ = f32[32,1,128]{2,1,0:T(1,128)S(1)} all-to-all(f32[32,1,128]{2,1,0:T(1,128)S(1)} %get-tuple-element.50), channel_id=1, replica_groups=mesh['node'=16,'tone'=2] {'node','tone'}, dimensions={0} | all-to-all | bytes 32768 | tf_op jit(solution)/shard_map/all_to_all | solution.py:679
  142.7 3.5 %shard_map.108 = (f32[1024,512]{1,0:T(8,128)S(1)}, f32[1024,512]{1,0:T(8,128)S(1)}) custom-call(f32[32,1,128]{2,1,0:T(1,128)S(1)} %all_to_all.20.refs_0_, f32[1024,512]{1,0:T(8,128)S(1)} %get-tuple-element.51.refs_1_, f32[1024,512]{1,0:T(8,128)S(1)} %maximum_subtract_fusion.refs_0_.refs_2_.refs_1_.refs_3_.refs_4_, f32[1024,512]{1,0:T(8,128)S(1)} %copy-done.6, ...), custom_call_target="tpu_custom_call" | custom-call | flops 1610612736 | bytes 8388608 | tf_op jit(solution)/shard_map/pallas_call | solution.py:357
  146.2 9.1 %shard_map.109 = (f32[1024,512]{1,0:T(8,128)S(1)}, f32[32,1,128]{2,1,0:T(1,128)S(1)}, f32[1024,384]{1,0:T(8,128)S(1)}, f32[1024,384]{1,0:T(8,128)S(1)}, f32[1024...) custom-call(f32[32,1,128]{2,1,0:T(1,128)S(1)} %all_to_all.20.refs_0_, ...), custom_call_target="tpu_custom_call" | custom-call | flops 5637144576 | bytes 14680064 | tf_op jit(solution)/shard_map/pallas_call | solution.py:473
  155.3 1.8 collective-permute-start.14
  158.4 23.4 %all_to_all.21.refs_1_ = f32[32,1,128]{2,1,0:T(1,128)S(1)} all-to-all(f32[32,1,128]{2,1,0:T(1,128)S(1)} %get-tuple-element.56), channel_id=1, replica_groups=mesh['node'=16,'tone'=2] {'node','tone'}, dimensions={0} | all-to-all | bytes 32768 | tf_op jit(solution)/shard_map/all_to_all | solution.py:679
  181.7 3.8 %shard_map.110 = (f32[1024,512]{1,0:T(8,128)S(1)}, f32[1024,512]{1,0:T(8,128)S(1)}) custom-call(f32[32,1,128]{2,1,0:T(1,128)S(1)} %all_to_all.20.refs_0_, f32[32,1,128]{2,1,0:T(1,128)S(1)} %all_to_all.21.refs_1_, f32[1024,512]{1,0:T(8,128)S(1)} %get-tuple-element.57.refs_2_, f32[1024,512]{1,0:T(8,128)S(1)} %maximum_subtract_fusion.refs_0_.refs_2_.refs_1_.refs_3_.refs_4_, ...), custom_call_target="tpu_custom_call" | custom-call | flops 1610612736 | bytes 8388608 | tf_op jit(solution)/shard_map/pallas_call | solution.py:357
  185.5 9.5 %shard_map.111 = (f32[1024,512]{1,0:T(8,128)S(1)}, f32[32,1,128]{2,1,0:T(1,128)S(1)}, f32[1024,384]{1,0:T(8,128)S(1)}, f32[1024,384]{1,0:T(8,128)S(1)}, f32[1024...) custom-call(f32[32,1,128]{2,1,0:T(1,128)S(1)} %all_to_all.20.refs_0_, f32[32,1,128]{2,1,0:T(1,128)S(1)} %all_to_all.21.refs_1_, ...), custom_call_target="tpu_custom_call" | custom-call | flops 5637144576 | bytes 20971520 | tf_op jit(solution)/shard_map/pallas_call | solution.py:473
  195.1 1.8 collective-permute-start.16
  198.2 22.6 %all_to_all.22.refs_2_ = f32[32,1,128]{2,1,0:T(1,128)S(1)} all-to-all(f32[32,1,128]{2,1,0:T(1,128)S(1)} %get-tuple-element.64), channel_id=1, replica_groups=mesh['node'=16,'tone'=2] {'node','tone'}, dimensions={0} | all-to-all | bytes 32768 | tf_op jit(solution)/shard_map/all_to_all | solution.py:679
  220.8 4.0 %shard_map.112 = (f32[1024,512]{1,0:T(8,128)S(1)}, f32[1024,512]{1,0:T(8,128)S(1)}) custom-call(f32[32,1,128]{2,1,0:T(1,128)S(1)} %all_to_all.20.refs_0_, f32[32,1,128]{2,1,0:T(1,128)S(1)} %all_to_all.21.refs_1_, f32[32,1,128]{2,1,0:T(1,128)S(1)} %all_to_all.22.refs_2_, f32[1024,512]{1,0:T(8,128)S(1)} %get-tuple-element.65.refs_3_, ...), custom_call_target="tpu_custom_call" | custom-call | flops 1610612736 | bytes 8388608 | tf_op jit(solution)/shard_map/pallas_call | solution.py:357
  224.9 10.3 %shard_map.113 = (f32[1024,512]{1,0:T(8,128)S(1)}, f32[32,1,128]{2,1,0:T(1,128)}) custom-call(f32[32,1,128]{2,1,0:T(1,128)S(1)} %all_to_all.20.refs_0_, f32[32,1,128]{2,1,0:T(1,128)S(1)} %all_to_all.21.refs_1_, f32[32,1,128]{2,1,0:T(1,128)S(1)} %all_to_all.22.refs_2_, f32[1024,512]{1,0:T(8,128)S(1)} %maximum_subtract_fusion.refs_0_.refs_2_.refs_1_.refs_3_.refs_4_, ...), custom_call_target="tpu_custom_call" | custom-call | flops 5637144576 | bytes 27262976 | tf_op jit(solution)/shard_map/pallas_call | solution.py:473
  236.5 2.8 all-to-all-start.3
  239.3 7.2 %all-to-all-done.3.refs_3_ = f32[32,1,128]{2,1,0:T(1,128)S(1)} async-done(((f32[32,1,128]{2,1,0:T(1,128)}), f32[32,1,128]{2,1,0:T(1,128)S(1)}, u32[]{:S(2)}, u32[]{:S(2)}) %all-to-all-start.3) | async-done | bytes 16416 | tf_op jit(solution)/shard_map/all_to_all | solution.py:679
  246.5 1.6 copy-done.3
  248.1 1.6 copy-done.8
  249.7 1.6 copy-done.16
  254.5 4.3 %shard_map.114 = (f32[1024,512]{1,0:T(8,128)S(1)}, f32[1024,512]{1,0:T(8,128)S(1)}) custom-call(f32[32,1,128]{2,1,0:T(1,128)S(1)} %all_to_all.20.refs_0_, f32[32,1,128]{2,1,0:T(1,128)S(1)} %all_to_all.21.refs_1_, f32[32,1,128]{2,1,0:T(1,128)S(1)} %all_to_all.22.refs_2_, f32[32,1,128]{2,1,0:T(1,128)S(1)} %all-to-all-done.3.refs_3_, ...), custom_call_target="tpu_custom_call" | custom-call | flops 8388608 | bytes 12582912 | tf_op jit(solution)/shard_map/pallas_call | solution.py:473
  258.8 1.8 dynamic-slice_select_fusion.2
  261.2 1.7 collective-permute-start.18
  264.2 1.9 collective-permute-start.21
  266.0 1.6 collective-permute-start.20
  267.7 16.1 %collective-permute-done.19 = f32[512,512]{1,0:T(8,128)} collective-permute-done((f32[512,512]{1,0:T(8,128)}, f32[512,512]{1,0:T(8,128)}, u32[]{:S(2)}, u32[]{:S(2)}) %collective-permute-start.19) | collective-permute-done | bytes 1048608 | tf_op jit(solution)/shard_map/ppermute | solution.py:150
  283.8 1.6 broadcast_select_fusion.11
  286.8 19.4 %collective-permute-done.21 = f32[512,512]{1,0:T(8,128)} collective-permute-done((f32[512,512]{1,0:T(8,128)}, f32[512,512]{1,0:T(8,128)}, u32[]{:S(2)}, u32[]{:S(2)}) %collective-permute-start.21) | collective-permute-done | bytes 1048608 | tf_op jit(solution)/shard_map/ppermute | solution.py:150
  (140 shorter events, 36.4 us)
Async XLA Ops:
  0.6 25.8 %copy-start = (f32[3,4]{1,0:T(4,128)S(1)}, f32[3,4]{1,0:T(4,128)}, u32[]{:S(2)}) copy-start(f32[3,4]{1,0:T(4,128)} %param.17) | copy-start | bytes 148
  1.4 27.2 %collective-permute-start.4 = (f32[4,7]{1,0:T(4,128)S(1)}, f32[4,7]{1,0:T(4,128)S(1)}, u32[]{:S(2)}, u32[]{:S(2)}) collective-permute-start(f32[4,7]{1,0:T(4,128)S(1)} %constant_dynamic-slice_fusion.7), channel_id=1, source_target_pairs={{0,2},{1,3},{2,0},{3,1},{4,6},{5,7},{6,4},{7,5},{8,10},{9,11},{10,... | collective-permute-start | bytes 344 | tf_op jit(solution)/shard_map/ppermute | solution.py:103
  1.9 26.9 %collective-permute-start.2 = (f32[32,16]{0,1:T(8,128)}, f32[32,16]{0,1:T(8,128)S(1)}, u32[]{:S(2)}, u32[]{:S(2)}) collective-permute-start(f32[32,16]{0,1:T(8,128)} %param.15), channel_id=1, source_target_pairs={{0,1},{1,0},{2,3},{3,2},{4,5},{5,4},{6,7},{7,6},{8,9},{9,8},{10,11... | collective-permute-start | bytes 6152 | tf_op jit(solution)/shard_map/ppermute | solution.py:607
  7.1 8.8 %copy-start.35 = (f32[32,16]{0,1:T(8,128)S(1)}, f32[32,16]{0,1:T(8,128)}, u32[]{:S(2)}) copy-start(f32[32,16]{0,1:T(8,128)} %param.15) | copy-start | bytes 6148
  7.1 24.5 %collective-permute-start.1 = (f32[512,384]{1,0:T(8,128)}, f32[512,384]{1,0:T(8,128)}, u32[]{:S(2)}, u32[]{:S(2)}) collective-permute-start(f32[512,384]{1,0:T(8,128)} %get-tuple-element.92), channel_id=1, source_target_pairs={{2,0},{3,1},{4,2},{5,3},{6,4},{7,5},{8,6},{9,7},{10,8},{11,9},{12,... | collective-permute-start | bytes 2359304 | tf_op jit(solution)/shard_map/ppermute | solution.py:188
  8.5 9.5 %copy-start.29 = (s32[7]{0:T(128)S(1)}, s32[7]{0:T(128)}, u32[]{:S(2)}) copy-start(s32[7]{0:T(128)} %band_code.3) | copy-start | bytes 88
  8.5 23.0 %collective-permute-start = (f32[512,384]{1,0:T(8,128)}, f32[512,384]{1,0:T(8,128)}, u32[]{:S(2)}, u32[]{:S(2)}) collective-permute-start(f32[512,384]{1,0:T(8,128)} %get-tuple-element.93), channel_id=1, source_target_pairs={{0,2},{1,3},{2,4},{3,5},{4,6},{5,7},{6,8},{7,9},{8,10},{9,11},{10,... | collective-permute-start | bytes 2359304 | tf_op jit(solution)/shard_map/ppermute | solution.py:187
  15.3 27.6 %collective-permute-start.3 = (f32[4,7,128,128]{3,2,1,0:T(8,128)}, f32[4,7,128,128]{3,2,1,0:T(8,128)}, u32[]{:S(2)}, u32[]{:S(2)}) collective-permute-start(f32[4,7,128,128]{3,2,1,0:T(8,128)} %constant_dynamic-slice_fusion.9), channel_id=1, source_target_pairs={{0,2},{1,3},{2,0},{3,1},{4,6},{5,7},{6,4},{7,5},{8,10},{9,11},{10,... | collective-permute-start | bytes 5505032 | tf_op jit(solution)/shard_map/ppermute | solution.py:103
  17.7 8.8 %copy-start.36 = (s32[1024]{0:T(1024)S(1)}, s32[1024]{0:T(1024)}, u32[]{:S(2)}) copy-start(s32[1024]{0:T(1024)} %param.16) | copy-start | bytes 12292
  18.0 2.0 copy-start.9
  20.1 6.5 %copy-start.20 = (f32[32,16,1024]{2,1,0:T(8,128)S(1)}, f32[32,16,1024]{2,1,0:T(8,128)}, u32[]{:S(2)}) copy-start(f32[32,16,1024]{2,1,0:T(8,128)} %param.9) | copy-start | bytes 6291460
  22.7 1.8 copy-start.30
  24.6 1.8 copy-start.32
  28.6 1.2 collective-permute-start.5
  28.7 24.6 %collective-permute-start.8 = (f32[512,512]{1,0:T(8,128)}, f32[512,512]{1,0:T(8,128)}, u32[]{:S(2)}, u32[]{:S(2)}) collective-permute-start(f32[512,512]{1,0:T(8,128)} %get-tuple-element.94), channel_id=1, source_target_pairs={{0,2},{1,0},{2,3},{3,1},{5,7},{4,5},{7,6},{6,4},{8,10},{9,8},{10,1... | collective-permute-start | bytes 3145736 | tf_op jit(solution)/shard_map/ppermute | solution.py:123
  29.9 23.5 %collective-permute-start.9 = (f32[512,512]{1,0:T(8,128)}, f32[512,512]{1,0:T(8,128)}, u32[]{:S(2)}, u32[]{:S(2)}) collective-permute-start(f32[512,512]{1,0:T(8,128)} %get-tuple-element.95), channel_id=1, source_target_pairs={{1,2},{2,1},{4,7},{7,4},{9,10},{10,9},{12,15},{15,12},{17,18},{18,... | collective-permute-start | bytes 3145736 | tf_op jit(solution)/shard_map/ppermute | solution.py:124
  31.5 2.0 copy-start.31
  33.6 2.0 copy-start.33
  37.2 5.8 %copy-start.10 = (f32[8,7,128,128]{3,2,1,0:T(8,128)S(1)}, f32[8,7,128,128]{3,2,1,0:T(8,128)}, u32[]{:S(2)}) copy-start(f32[8,7,128,128]{3,2,1,0:T(8,128)} %coupling.1) | copy-start | bytes 11010052
  47.2 19.2 %collective-permute-start.6 = (f32[512,512]{1,0:T(8,128)}, f32[512,512]{1,0:T(8,128)}, u32[]{:S(2)}, u32[]{:S(2)}) collective-permute-start(f32[512,512]{1,0:T(8,128)} %get-tuple-element.90), channel_id=1, source_target_pairs={{0,2},{1,0},{2,3},{3,1},{5,7},{4,5},{7,6},{6,4},{8,10},{9,8},{10,1... | collective-permute-start | bytes 3145736 | tf_op jit(solution)/shard_map/ppermute | solution.py:123
  48.7 17.6 %collective-permute-start.7 = (f32[512,512]{1,0:T(8,128)S(1)}, f32[512,512]{1,0:T(8,128)}, u32[]{:S(2)}, u32[]{:S(2)}) collective-permute-start(f32[512,512]{1,0:T(8,128)S(1)} %get-tuple-element.91), channel_id=1, source_target_pairs={{1,2},{2,1},{4,7},{7,4},{9,10},{10,9},{12,15},{15,12},{17,18},{18,... | collective-permute-start | bytes 3145736 | tf_op jit(solution)/shard_map/ppermute | solution.py:124
  53.3 2.5 copy-start.11
  53.3 2.5 copy-start.13
  55.8 3.0 copy-start.17
  58.8 9.2 %copy-start.4 = (f32[1024,512]{1,0:T(8,128)}, f32[1024,512]{1,0:T(8,128)S(1)}, u32[]{:S(2)}) copy-start(f32[1024,512]{1,0:T(8,128)S(1)} %get-tuple-element.44.refs_1_.refs_3_.refs_5_.refs_7_) | copy-start | bytes 6291460
  70.5 24.5 %collective-permute-start.11 = (f32[1024,384]{1,0:T(8,128)}, f32[1024,384]{1,0:T(8,128)}, u32[]{:S(2)}, u32[]{:S(2)}) collective-permute-start(f32[1024,384]{1,0:T(8,128)} %get-tuple-element.88), channel_id=1, source_target_pairs={{2,0},{1,2},{3,1},{5,3},{7,5},{4,7},{6,4},{8,6},{10,8},{9,10},{11,... | collective-permute-start | bytes 4718600 | tf_op jit(solution)/shard_map/ppermute | solution.py:188
  71.8 23.2 %collective-permute-start.10 = (f32[1024,384]{1,0:T(8,128)}, f32[1024,384]{1,0:T(8,128)}, u32[]{:S(2)}, u32[]{:S(2)}) collective-permute-start(f32[1024,384]{1,0:T(8,128)} %get-tuple-element.89), channel_id=1, source_target_pairs={{0,2},{2,1},{1,3},{3,5},{5,7},{7,4},{4,6},{6,8},{8,10},{10,9},{9,1... | collective-permute-start | bytes 4718600 | tf_op jit(solution)/shard_map/ppermute | solution.py:187
  90.6 1.6 copy-start.5
  92.2 2.8 copy-start.21
  95.0 47.7 %copy-start.6 = (f32[1024,512]{1,0:T(8,128)S(1)}, f32[1024,512]{1,0:T(8,128)}, u32[]{:S(2)}) copy-start(f32[1024,512]{1,0:T(8,128)} %copy-done.4) | copy-start | bytes 6291460
  102.8 43.4 %collective-permute-start.12 = (f32[1024,384]{1,0:T(8,128)S(1)}, f32[1024,384]{1,0:T(8,128)S(1)}, u32[]{:S(2)}, u32[]{:S(2)}) collective-permute-start(f32[1024,384]{1,0:T(8,128)S(1)} %get-tuple-element.54), channel_id=1, source_target_pairs={{0,2},{2,1},{1,3},{3,5},{5,7},{7,4},{4,6},{6,8},{8,10},{10,9},{9,1... | collective-permute-start | bytes 4718600 | tf_op jit(solution)/shard_map/ppermute | solution.py:187
  114.9 31.3 %collective-permute-start.13 = (f32[1024,384]{1,0:T(8,128)S(1)}, f32[1024,384]{1,0:T(8,128)S(1)}, u32[]{:S(2)}, u32[]{:S(2)}) collective-permute-start(f32[1024,384]{1,0:T(8,128)S(1)} %get-tuple-element.55), channel_id=1, source_target_pairs={{2,0},{1,2},{3,1},{5,3},{7,5},{4,7},{6,4},{8,6},{10,8},{9,10},{11,... | collective-permute-start | bytes 4718600 | tf_op jit(solution)/shard_map/ppermute | solution.py:188
  146.1 78.7 %copy-start.2 = (f32[1024,512]{1,0:T(8,128)}, f32[1024,512]{1,0:T(8,128)S(1)}, u32[]{:S(2)}) copy-start(f32[1024,512]{1,0:T(8,128)S(1)} %get-tuple-element.52.refs_2_.refs_4_.refs_3_.refs_5_) | copy-start | bytes 6291460
  155.3 30.3 %collective-permute-start.14 = (f32[1024,384]{1,0:T(8,128)S(1)}, f32[1024,384]{1,0:T(8,128)S(1)}, u32[]{:S(2)}, u32[]{:S(2)}) collective-permute-start(f32[1024,384]{1,0:T(8,128)S(1)} %get-tuple-element.60), channel_id=1, source_target_pairs={{0,2},{2,1},{1,3},{3,5},{5,7},{7,4},{4,6},{6,8},{8,10},{10,9},{9,1... | collective-permute-start | bytes 4718600 | tf_op jit(solution)/shard_map/ppermute | solution.py:187
  157.1 28.5 %collective-permute-start.15 = (f32[1024,384]{1,0:T(8,128)S(1)}, f32[1024,384]{1,0:T(8,128)S(1)}, u32[]{:S(2)}, u32[]{:S(2)}) collective-permute-start(f32[1024,384]{1,0:T(8,128)S(1)} %get-tuple-element.61), channel_id=1, source_target_pairs={{2,0},{1,2},{3,1},{5,3},{7,5},{4,7},{6,4},{8,6},{10,8},{9,10},{11,... | collective-permute-start | bytes 4718600 | tf_op jit(solution)/shard_map/ppermute | solution.py:188
  185.5 39.3 %copy-start.7 = (f32[1024,512]{1,0:T(8,128)}, f32[1024,512]{1,0:T(8,128)S(1)}, u32[]{:S(2)}) copy-start(f32[1024,512]{1,0:T(8,128)S(1)} %get-tuple-element.58.refs_4_.refs_6_.refs_5_) | copy-start | bytes 6291460
  195.1 29.8 %collective-permute-start.16 = (f32[1024,384]{1,0:T(8,128)S(1)}, f32[1024,384]{1,0:T(8,128)S(1)}, u32[]{:S(2)}, u32[]{:S(2)}) collective-permute-start(f32[1024,384]{1,0:T(8,128)S(1)} %get-tuple-element.68), channel_id=1, source_target_pairs={{0,2},{2,1},{1,3},{3,5},{5,7},{7,4},{4,6},{6,8},{8,10},{10,9},{9,1... | collective-permute-start | bytes 4718600 | tf_op jit(solution)/shard_map/ppermute | solution.py:187
  196.9 27.9 %collective-permute-start.17 = (f32[1024,384]{1,0:T(8,128)S(1)}, f32[1024,384]{1,0:T(8,128)S(1)}, u32[]{:S(2)}, u32[]{:S(2)}) collective-permute-start(f32[1024,384]{1,0:T(8,128)S(1)} %get-tuple-element.69), channel_id=1, source_target_pairs={{2,0},{1,2},{3,1},{5,3},{7,5},{4,7},{6,4},{8,6},{10,8},{9,10},{11,... | collective-permute-start | bytes 4718600 | tf_op jit(solution)/shard_map/ppermute | solution.py:188
  224.8 10.3 %copy-start.15 = (f32[1024,512]{1,0:T(8,128)}, f32[1024,512]{1,0:T(8,128)S(1)}, u32[]{:S(2)}) copy-start(f32[1024,512]{1,0:T(8,128)S(1)} %get-tuple-element.66.refs_6_.refs_7_) | copy-start | bytes 6291460
  236.5 10.0 %all-to-all-start.3 = ((f32[32,1,128]{2,1,0:T(1,128)}), f32[32,1,128]{2,1,0:T(1,128)S(1)}, u32[]{:S(2)}, u32[]{:S(2)}) async-start(f32[32,1,128]{2,1,0:T(1,128)} %get-tuple-element.72), calls=%async_computation.3 | async-start | bytes 32768 | tf_op jit(solution)/shard_map/all_to_all | solution.py:679
  258.7 2.0 copy-start.24
  258.7 4.2 %copy-start.22 = (f32[1024,512]{1,0:T(8,128)}, f32[1024,512]{1,0:T(8,128)S(1)}, u32[]{:S(2)}) copy-start(f32[1024,512]{1,0:T(8,128)S(1)} %get-tuple-element.75) | copy-start | bytes 6291460
  260.7 23.1 %collective-permute-start.19 = (f32[512,512]{1,0:T(8,128)}, f32[512,512]{1,0:T(8,128)}, u32[]{:S(2)}, u32[]{:S(2)}) collective-permute-start(f32[512,512]{1,0:T(8,128)} %get-tuple-element.78), channel_id=1, source_target_pairs={{2,0},{0,1},{3,2},{1,3},{7,5},{5,4},{6,7},{4,6},{10,8},{8,9},{11,1... | collective-permute-start | bytes 3145736 | tf_op jit(solution)/shard_map/ppermute | solution.py:150
  261.2 22.6 %collective-permute-start.18 = (f32[512,512]{1,0:T(8,128)}, f32[512,512]{1,0:T(8,128)}, u32[]{:S(2)}, u32[]{:S(2)}) collective-permute-start(f32[512,512]{1,0:T(8,128)} %get-tuple-element.79), channel_id=1, source_target_pairs={{2,1},{1,2},{7,4},{4,7},{10,9},{9,10},{15,12},{12,15},{18,17},{17,... | collective-permute-start | bytes 3145736 | tf_op jit(solution)/shard_map/ppermute | solution.py:151
  262.9 20.8 %copy-start.25 = (f32[1024,512]{1,0:T(8,128)S(1)}, f32[1024,512]{1,0:T(8,128)}, u32[]{:S(2)}) copy-start(f32[1024,512]{1,0:T(8,128)} %copy-done.24) | copy-start | bytes 6291460
  264.2 42.0 %collective-permute-start.21 = (f32[512,512]{1,0:T(8,128)}, f32[512,512]{1,0:T(8,128)}, u32[]{:S(2)}, u32[]{:S(2)}) collective-permute-start(f32[512,512]{1,0:T(8,128)} %get-tuple-element.76), channel_id=1, source_target_pairs={{2,0},{0,1},{3,2},{1,3},{7,5},{5,4},{6,7},{4,6},{10,8},{8,9},{11,1... | collective-permute-start | bytes 3145736 | tf_op jit(solution)/shard_map/ppermute | solution.py:150
  266.0 40.2 %collective-permute-start.20 = (f32[512,512]{1,0:T(8,128)S(1)}, f32[512,512]{1,0:T(8,128)}, u32[]{:S(2)}, u32[]{:S(2)}) collective-permute-start(f32[512,512]{1,0:T(8,128)S(1)} %get-tuple-element.77), channel_id=1, source_target_pairs={{2,1},{1,2},{7,4},{4,7},{10,9},{9,10},{15,12},{12,15},{18,17},{17,... | collective-permute-start | bytes 3145736 | tf_op jit(solution)/shard_map/ppermute | solution.py:151
  285.4 20.9 %copy-start.23 = (f32[1024,512]{1,0:T(8,128)S(1)}, f32[1024,512]{1,0:T(8,128)}, u32[]{:S(2)}) copy-start(f32[1024,512]{1,0:T(8,128)} %copy-done.22) | copy-start | bytes 6291460
  (12 other events, 17.9 us)

commit v3 on v2

--- a/solution.py
+++ b/solution.py
@@ -18,7 +18,9 @@
 F32 = jnp.float32
 BF16 = jnp.bfloat16
 LIMIT = 16 * 1024 * 1024
-ROWS = 128
+LIMIT_START = 60 * 1024 * 1024
+LIMIT_END = 60 * 1024 * 1024
+ROWS = 256
 
 
 class Chain:
@@ -367,25 +369,27 @@
     )(*parts, *fields, *small, *tables)
 
 
-def coupled(left, field, right, op_top, op_low, ext_top, ext_low, write):
-    width = field.shape[1]
+def coupled(left, field, right, op_top, op_low, ext, write):
+    block, width = field.shape
     reach = HALO_B * NB
     for value, at in ((left, 0), (field, reach), (right, reach + width)):
         here = slice(at, at + value.shape[1])
-        ext_top[:, here], ext_low[:, here] = halves(value)
+        ext[:block, here], ext[block:, here] = halves(value)
     step = 2 * NB if width % (2 * NB) == 0 else NB
     for at in range(0, width, step):
         rows = slice(at, at + step + 2 * reach)
         here = slice(at, at + step)
-        write(here, dot3(ext_top[:, rows], ext_low[:, rows], op_top[rows, here], op_low[rows, here]))
-
-
-def residual_kernel(source, volts, left, right, caps, damps, op_top, op_low, out, ext_top, ext_low):
+        both = jnp.dot(ext[:, rows], op_top[rows, here], preferred_element_type=F32)
+        rest = jnp.dot(ext[:block, rows], op_low[rows, here], preferred_element_type=F32)
+        write(here, both[:block] + (both[block:] + rest))
+
+
+def residual_kernel(source, volts, left, right, caps, damps, op_top, op_low, out, ext):
     def write(here, value):
         scaled = damps[...] * caps[:, here] * volts[:, here]
         out[:, here] = source[:, here] - (scaled + value)
 
-    coupled(left[...], volts[...], right[...], op_top, op_low, ext_top, ext_low, write)
+    coupled(left[...], volts[...], right[...], op_top, op_low, ext, write)
 
 
 def image_kernel(n_parts, more, *refs):
@@ -409,7 +413,7 @@
             refs[1][...] = right
             refs = refs[2:]
         edges, refs = refs[:2], refs[2:]
-    ext_top, ext_low, sums = refs
+    ext, sums = refs
     field = basis[-1]
 
     @pl.when(step == 0)
@@ -432,7 +436,7 @@
         sums[n_parts + 1] += tile_sum(value * value)
         sums[n_parts + 2] += tile_sum(mine * mine)
 
-    coupled(left, field[...], right, op_top, op_low, ext_top, ext_low, write)
+    coupled(left, field[...], right, op_top, op_low, ext, write)
 
     if edges:
         take = edges[0].shape[1]
@@ -449,7 +453,7 @@
         stats[...] = jnp.broadcast_to(row[None], stats.shape)
 
 
-def rows_call(kernel, parts, fields, caps, damps, operator, outs, stats, scratch):
+def rows_call(kernel, parts, fields, caps, damps, operator, outs, stats, scratch, limit=LIMIT):
     rows, width = fields[0].shape
     block = min(rows, ROWS)
     once = functools.partial(pl.BlockSpec, pipeline_mode=pl.Buffered(1))
@@ -477,7 +481,7 @@
         out_specs=out_specs,
         out_shape=shapes,
         scratch_shapes=scratch(block),
-        compiler_params=pltpu.CompilerParams(vmem_limit_bytes=LIMIT),
+        compiler_params=pltpu.CompilerParams(vmem_limit_bytes=limit),
         cost_estimate=pl.CostEstimate(
             flops=flops, bytes_accessed=4 * rows * width * len(fields), transcendentals=0
         ),
@@ -611,7 +615,7 @@
 
         def ext_scratch(nodes):
             ext = nodes + 2 * HALO_B * NB
-            return lambda block: [pltpu.VMEM((block, ext), BF16)] * 2
+            return lambda block: [pltpu.VMEM((2 * block, ext), BF16)]
 
         volts_here = voltages.reshape(local, shape[2])
         left, right = halos(*edges_of(volts_here), chain.node_up, chain.node_down)
@@ -625,11 +629,12 @@
             [(local, shape[2])],
             0,
             ext_scratch(shape[2]),
+            LIMIT_START,
         )
         mine = chunk_of(chain, coupling, place, 0)
         mine_active = chunk_of(chain, active.astype(F32), place, 0)
-        driven, damps, mine, mine_active, per_node = lax.optimization_barrier(
-            (driven, damps, mine, mine_active, per_node)
+        driven, damps, mine_active, per_node = lax.optimization_barrier(
+            (driven, damps, mine_active, per_node)
         )
         caps = per_node[3:4]
         driven = gather_tones(chain, driven.reshape(shape), place)
@@ -689,6 +694,7 @@
             [(rows, width)] * 2,
             0,
             lambda block: [],
+            LIMIT_END,
         )
         new_volts = scatter_tones(chain, new_volts, place, shape)
         remaining = scatter_tones(chain, remaining, place, shape)

time: 313 us -> 306 us (0.978)
  local copies, waits for them, and re-layouts: 37.4 us -> 20.5 us
    unnamed x76 -> x60, local copies, waits for them, and re-layouts: 24.1 us -> 6.3 us
    ppermute x2, waiting for transfers between devices: 7.58 us -> 11.2 us  [gather_tones(): got_one = lax.ppermute(one, AXES, chain.first())]
  transfers between devices with their start and end apart: 23 -> 23, of which waited for: 5 -> 4; matrix products, arithmetic and copies ran while one was open for 8% -> 11% of each run, Pallas kernels for 9% -> 10%
where the time goes in v3:
time: 306 us; the launch traced here: 303 us
  blocking collectives  72.1 us (24%)
  Pallas kernels  70.1 us (23%)
  starting transfers between devices  59.6 us (19%)
  waiting for transfers between devices  53.7 us (18%)
  other arithmetic  20.6 us (7%)
  local copies, waits for them, and re-layouts  20.5 us (7%)
  matrix products  5.08 us (2%)
    all_to_all x3, blocking collectives, per_device(): part = lax.all_to_all(stats, AXES, 0, 0, tiled=True)  72.1 us
    pallas_call x6, Pallas kernels, rows_call(): pl.pallas_call(kernel, grid=(rows // block,), in_specs=specs, out_specs=o...  49.5 us
    ppermute x2, waiting for transfers between devices, scatter_tones(): got_one = lax.ppermute(one, AXES, flipped(chain.first()))  35.2 us
    ppermute x5, starting transfers between devices, halos(): left.insert(0, lax.ppermute(last[:, width - take:], AXES, up(hop)))  35 us
    pallas_call x5, Pallas kernels, columns_call(): pl.pallas_call(kernel, grid=(width // block,), in_specs=specs, out_specs=...  16.8 us
    ppermute x2, waiting for transfers between devices, gather_tones(): got_one = lax.ppermute(one, AXES, chain.first())  11.2 us
    all_to_all x1, waiting for transfers between devices, per_device(): part = lax.all_to_all(stats, AXES, 0, 0, tiled=True)  7.21 us
    ppermute x5, starting transfers between devices, halos(): right.append(lax.ppermute(first[:, :take], AXES, down(hop)))  6.44 us
  transfers between devices with their start and end apart: 23, of which 4 were waited for; matrix products, arithmetic and copies ran while one was open for 11% of the time, Pallas kernels for 10%

profile of v3, /device:TPU:0, one launch (start us, length us, event | category | flops | bytes accessed | tf_op | source)
XLA Modules:
  0.0 303.0 jit_solution(10824416118938853418)
XLA Ops:
  1.9 2.6 collective-permute-start.2
  6.3 2.8 fusion.32
  10.4 3.9 %collective-permute-start = (f32[512,384]{1,0:T(8,128)}, f32[512,384]{1,0:T(8,128)}, u32[]{:S(2)}, u32[]{:S(2)}) collective-permute-start(f32[512,384]{1,0:T(8,128)} %get-tuple-element.91), channel_id=1, source_target_pairs={{0,2},{1,3},{2,4},{3,5},{4,6},{5,7},{6,8},{7,9},{8,10},{9,11},{10,... | collective-permute-start | bytes 2359304 | tf_op jit(solution)/shard_map/ppermute | solution.py:189
  21.5 2.7 operator.2
  24.2 1.8 copy-done.20
  26.0 1.4 constant_dynamic-slice_fusion.2
  30.0 1.6 collective-permute-start.8
  31.7 9.1 %shard_map.104 = f32[512,1024]{1,0:T(8,128)} custom-call(f32[512,1024]{1,0:T(8,128)} %bitcast.44, f32[512,1024]{1,0:T(8,128)} %bitcast.34, f32[512,384]{1,0:T(8,128)} %collective-permute-done.left, f32[512,384]{1,0:T(8,128)} %collective-permute-done.1.right, f32[1,1024]{1,0:T(1,128)} %bitcast.43, f32[512,1]{1,0:T(8,128)} %reshape.82.damps, ...), custom_call_target="tpu_custom_call" | custom-call | flops 8858370048 | bytes 8388608 | tf_op jit(solution)/shard_map/pallas_call | solution.py:477
  40.8 3.1 %constant_dynamic-slice_fusion.5 = (f32[512,512]{1,0:T(8,128)}, f32[512,512]{1,0:T(8,128)}) fusion(f32[512,1024]{1,0:T(8,128)} %shard_map.104, s32[]{:T(128)S(6)} %select_n.297, s32[]{:T(128)S(6)} %select_n.296), kind=kLoop, calls=%fused_computation.70 | loop fusion | bytes 4194312 | tf_op jit(solution)/shard_map/dynamic_slice | solution.py:123
  43.9 2.4 collective-permute-start.5
  46.3 1.7 collective-permute-start.6
  51.0 1.8 broadcast_select_fusion.1
  53.1 3.0 shard_map.105
  56.1 11.2 %collective-permute-done.5 = f32[512,512]{1,0:T(8,128)} collective-permute-done((f32[512,512]{1,0:T(8,128)}, f32[512,512]{1,0:T(8,128)}, u32[]{:S(2)}, u32[]{:S(2)}) %collective-permute-start.5) | collective-permute-done | bytes 1048608 | tf_op jit(solution)/shard_map/ppermute | solution.py:125
  67.3 1.9 broadcast_select_fusion.3
  69.7 2.0 fusion.31
  73.0 14.8 %collective-permute-start.9 = (f32[1024,384]{1,0:T(8,128)}, f32[1024,384]{1,0:T(8,128)}, u32[]{:S(2)}, u32[]{:S(2)}) collective-permute-start(f32[1024,384]{1,0:T(8,128)} %get-tuple-element.87), channel_id=1, source_target_pairs={{0,2},{2,1},{1,3},{3,5},{5,7},{7,4},{4,6},{6,8},{8,10},{10,9},{9,1... | collective-permute-start | bytes 4718600 | tf_op jit(solution)/shard_map/ppermute | solution.py:189
  88.8 2.5 select_select_fusion.coupling
  92.6 2.7 shard_map.106.refs_1_
  95.3 6.1 %shard_map.107 = (f32[1024,512]{1,0:T(8,128)S(1)}, f32[32,1,128]{2,1,0:T(1,128)S(1)}, f32[1024,384]{1,0:T(8,128)S(1)}, f32[1024,384]{1,0:T(8,128)S(1)}) custom-call(f32[1024,512]{1,0:T(8,128)S(1)} %maximum_subtract_fusion.refs_0_.refs_2_.refs_1_.refs_3_.refs_4_, f32[1024,512]{1,0:T(8,128)S(1)} %shard_map.106.refs_1_, ...), custom_call_target="tpu_custom_call" | custom-call | flops 5637144576 | bytes 8388608 | tf_op jit(solution)/shard_map/pallas_call | solution.py:477
  101.4 12.7 %collective-permute-start.12 = (f32[1024,384]{1,0:T(8,128)S(1)}, f32[1024,384]{1,0:T(8,128)S(1)}, u32[]{:S(2)}, u32[]{:S(2)}) collective-permute-start(f32[1024,384]{1,0:T(8,128)S(1)} %get-tuple-element.52), channel_id=1, source_target_pairs={{0,2},{2,1},{1,3},{3,5},{5,7},{7,4},{4,6},{6,8},{8,10},{10,9},{9,1... | collective-permute-start | bytes 4718600 | tf_op jit(solution)/shard_map/ppermute | solution.py:189
  114.1 1.3 collective-permute-start.13
  115.4 26.0 %all_to_all.20.refs_0_ = f32[32,1,128]{2,1,0:T(1,128)S(1)} all-to-all(f32[32,1,128]{2,1,0:T(1,128)S(1)} %get-tuple-element.48), channel_id=1, replica_groups=mesh['node'=16,'tone'=2] {'node','tone'}, dimensions={0} | all-to-all | bytes 32768 | tf_op jit(solution)/shard_map/all_to_all | solution.py:684
  141.4 3.4 %shard_map.108 = (f32[1024,512]{1,0:T(8,128)S(1)}, f32[1024,512]{1,0:T(8,128)S(1)}) custom-call(f32[32,1,128]{2,1,0:T(1,128)S(1)} %all_to_all.20.refs_0_, f32[1024,512]{1,0:T(8,128)S(1)} %get-tuple-element.49.refs_1_, f32[1024,512]{1,0:T(8,128)S(1)} %maximum_subtract_fusion.refs_0_.refs_2_.refs_1_.refs_3_.refs_4_, f32[1024,512]{1,0:T(8,128)S(1)} %copy-done.5, ...), custom_call_target="tpu_custom_call" | custom-call | flops 1610612736 | bytes 8388608 | tf_op jit(solution)/shard_map/pallas_call | solution.py:359
  144.9 7.8 %shard_map.109 = (f32[1024,512]{1,0:T(8,128)S(1)}, f32[32,1,128]{2,1,0:T(1,128)S(1)}, f32[1024,384]{1,0:T(8,128)S(1)}, f32[1024,384]{1,0:T(8,128)S(1)}, f32[1024...) custom-call(f32[32,1,128]{2,1,0:T(1,128)S(1)} %all_to_all.20.refs_0_, ...), custom_call_target="tpu_custom_call" | custom-call | flops 5637144576 | bytes 14680064 | tf_op jit(solution)/shard_map/pallas_call | solution.py:477
  152.7 1.8 collective-permute-start.14
  154.5 1.3 collective-permute-start.15
  155.8 23.4 %all_to_all.21.refs_1_ = f32[32,1,128]{2,1,0:T(1,128)S(1)} all-to-all(f32[32,1,128]{2,1,0:T(1,128)S(1)} %get-tuple-element.54), channel_id=1, replica_groups=mesh['node'=16,'tone'=2] {'node','tone'}, dimensions={0} | all-to-all | bytes 32768 | tf_op jit(solution)/shard_map/all_to_all | solution.py:684
  179.2 3.7 %shard_map.110 = (f32[1024,512]{1,0:T(8,128)S(1)}, f32[1024,512]{1,0:T(8,128)S(1)}) custom-call(f32[32,1,128]{2,1,0:T(1,128)S(1)} %all_to_all.20.refs_0_, f32[32,1,128]{2,1,0:T(1,128)S(1)} %all_to_all.21.refs_1_, f32[1024,512]{1,0:T(8,128)S(1)} %get-tuple-element.55.refs_2_, f32[1024,512]{1,0:T(8,128)S(1)} %maximum_subtract_fusion.refs_0_.refs_2_.refs_1_.refs_3_.refs_4_, ...), custom_call_target="tpu_custom_call" | custom-call | flops 1610612736 | bytes 8388608 | tf_op jit(solution)/shard_map/pallas_call | solution.py:359
  182.9 8.5 %shard_map.111 = (f32[1024,512]{1,0:T(8,128)S(1)}, f32[32,1,128]{2,1,0:T(1,128)S(1)}, f32[1024,384]{1,0:T(8,128)S(1)}, f32[1024,384]{1,0:T(8,128)S(1)}, f32[1024...) custom-call(f32[32,1,128]{2,1,0:T(1,128)S(1)} %all_to_all.20.refs_0_, f32[32,1,128]{2,1,0:T(1,128)S(1)} %all_to_all.21.refs_1_, ...), custom_call_target="tpu_custom_call" | custom-call | flops 5637144576 | bytes 20971520 | tf_op jit(solution)/shard_map/pallas_call | solution.py:477
  191.4 1.8 collective-permute-start.16
  194.6 22.7 %all_to_all.22.refs_2_ = f32[32,1,128]{2,1,0:T(1,128)S(1)} all-to-all(f32[32,1,128]{2,1,0:T(1,128)S(1)} %get-tuple-element.62), channel_id=1, replica_groups=mesh['node'=16,'tone'=2] {'node','tone'}, dimensions={0} | all-to-all | bytes 32768 | tf_op jit(solution)/shard_map/all_to_all | solution.py:684
  217.3 4.0 %shard_map.112 = (f32[1024,512]{1,0:T(8,128)S(1)}, f32[1024,512]{1,0:T(8,128)S(1)}) custom-call(f32[32,1,128]{2,1,0:T(1,128)S(1)} %all_to_all.20.refs_0_, f32[32,1,128]{2,1,0:T(1,128)S(1)} %all_to_all.21.refs_1_, f32[32,1,128]{2,1,0:T(1,128)S(1)} %all_to_all.22.refs_2_, f32[1024,512]{1,0:T(8,128)S(1)} %get-tuple-element.63.refs_3_, ...), custom_call_target="tpu_custom_call" | custom-call | flops 1610612736 | bytes 8388608 | tf_op jit(solution)/shard_map/pallas_call | solution.py:359
  221.3 9.5 %shard_map.113 = (f32[1024,512]{1,0:T(8,128)S(1)}, f32[32,1,128]{2,1,0:T(1,128)}) custom-call(f32[32,1,128]{2,1,0:T(1,128)S(1)} %all_to_all.20.refs_0_, f32[32,1,128]{2,1,0:T(1,128)S(1)} %all_to_all.21.refs_1_, f32[32,1,128]{2,1,0:T(1,128)S(1)} %all_to_all.22.refs_2_, f32[1024,512]{1,0:T(8,128)S(1)} %maximum_subtract_fusion.refs_0_.refs_2_.refs_1_.refs_3_.refs_4_, ...), custom_call_target="tpu_custom_call" | custom-call | flops 5637144576 | bytes 27262976 | tf_op jit(solution)/shard_map/pallas_call | solution.py:477
  230.8 1.4 copy-done.15
  232.2 2.6 all-to-all-start.3
  234.8 7.2 %all-to-all-done.3.refs_3_ = f32[32,1,128]{2,1,0:T(1,128)S(1)} async-done(((f32[32,1,128]{2,1,0:T(1,128)}), f32[32,1,128]{2,1,0:T(1,128)S(1)}, u32[]{:S(2)}, u32[]{:S(2)}) %all-to-all-start.3) | async-done | bytes 16416 | tf_op jit(solution)/shard_map/all_to_all | solution.py:684
  242.6 8.4 %shard_map.114 = (f32[1024,512]{1,0:T(8,128)}, f32[1024,512]{1,0:T(8,128)}) custom-call(f32[32,1,128]{2,1,0:T(1,128)} %copy-done.16, f32[32,1,128]{2,1,0:T(1,128)} %copy-done.17, f32[32,1,128]{2,1,0:T(1,128)} %copy-done.18, f32[32,1,128]{2,1,0:T(1,128)} %copy-done.27, f32[1024,512]{1,0:T(8,128)} %copy-done.2, f32[1024,512]{1,0:T(8,128)} %copy-done.3, ...), custom_call_target="tpu_custom_call" | custom-call | flops 8388608 | bytes 12582912 | tf_op jit(solution)/shard_map/pallas_call | solution.py:477
  251.1 3.3 %dynamic-slice_select_fusion.2 = (f32[512,512]{1,0:T(8,128)}, f32[512,512]{1,0:T(8,128)}) fusion(f32[1024,512]{1,0:T(8,128)} %get-tuple-element.72, s32[]{:T(128)S(6)} %select_n.317, pred[]{:T(512)S(6)} %eq.138, s32[]{:T(128)S(6)} %select_n.318), kind=kLoop, calls=%fused_computation.15 | loop fusion | flops 262144 | bytes 4194313 | tf_op jit(solution)/shard_map/jit(_where)/select_n | solution.py:151
  254.8 1.6 collective-permute-start.18
  257.7 1.9 collective-permute-start.21
  259.6 1.7 collective-permute-start.20
  261.3 16.1 %collective-permute-done.19 = f32[512,512]{1,0:T(8,128)} collective-permute-done((f32[512,512]{1,0:T(8,128)}, f32[512,512]{1,0:T(8,128)}, u32[]{:S(2)}, u32[]{:S(2)}) %collective-permute-start.19) | collective-permute-done | bytes 1048608 | tf_op jit(solution)/shard_map/ppermute | solution.py:152
  277.4 1.9 broadcast_select_fusion.11
  279.3 1.5 pad_maximum_fusion.1
  280.8 19.1 %collective-permute-done.21 = f32[512,512]{1,0:T(8,128)} collective-permute-done((f32[512,512]{1,0:T(8,128)}, f32[512,512]{1,0:T(8,128)}, u32[]{:S(2)}, u32[]{:S(2)}) %collective-permute-start.21) | collective-permute-done | bytes 1048608 | tf_op jit(solution)/shard_map/ppermute | solution.py:152
  299.9 1.6 broadcast_select_fusion.9
  301.5 1.5 pad_maximum_fusion.2
  (124 shorter events, 25.0 us)
Async XLA Ops:
  0.6 3.9 %copy-start = (f32[3,4]{1,0:T(4,128)S(1)}, f32[3,4]{1,0:T(4,128)}, u32[]{:S(2)}) copy-start(f32[3,4]{1,0:T(4,128)} %param.17) | copy-start | bytes 148
  0.6 13.7 %copy-start.28 = (f32[32,16]{0,1:T(8,128)S(1)}, f32[32,16]{0,1:T(8,128)}, u32[]{:S(2)}) copy-start(f32[32,16]{0,1:T(8,128)} %param.15) | copy-start | bytes 6148
  1.4 27.4 %collective-permute-start.3 = (f32[4,7]{1,0:T(4,128)S(1)}, f32[4,7]{1,0:T(4,128)S(1)}, u32[]{:S(2)}, u32[]{:S(2)}) collective-permute-start(f32[4,7]{1,0:T(4,128)S(1)} %constant_dynamic-slice_fusion.8), channel_id=1, source_target_pairs={{0,2},{1,3},{2,0},{3,1},{4,6},{5,7},{6,4},{7,5},{8,10},{9,11},{10,... | collective-permute-start | bytes 344 | tf_op jit(solution)/shard_map/ppermute | solution.py:105
  1.9 27.8 %collective-permute-start.2 = (f32[32,16]{0,1:T(8,128)}, f32[32,16]{0,1:T(8,128)S(1)}, u32[]{:S(2)}, u32[]{:S(2)}) collective-permute-start(f32[32,16]{0,1:T(8,128)} %param.15), channel_id=1, source_target_pairs={{0,1},{1,0},{2,3},{3,2},{4,5},{5,4},{6,7},{7,6},{8,9},{9,8},{10,11... | collective-permute-start | bytes 6152 | tf_op jit(solution)/shard_map/ppermute | solution.py:611
  6.1 23.9 %collective-permute-start.4 = (f32[8,512]{1,0:T(8,128)S(1)}, f32[8,512]{1,0:T(8,128)S(1)}, u32[]{:S(2)}, u32[]{:S(2)}) collective-permute-start(f32[8,512]{1,0:T(8,128)S(1)} %constant_dynamic-slice_fusion.7), channel_id=1, source_target_pairs={{0,2},{1,3},{2,0},{3,1},{4,6},{5,7},{6,4},{7,5},{8,10},{9,11},{10,... | collective-permute-start | bytes 49160 | tf_op jit(solution)/shard_map/ppermute | solution.py:105
  6.3 12.8 %copy-start.22 = (f32[32,16,1024]{2,1,0:T(8,128)S(1)}, f32[32,16,1024]{2,1,0:T(8,128)}, u32[]{:S(2)}) copy-start(f32[32,16,1024]{2,1,0:T(8,128)} %param.9) | copy-start | bytes 6291460
  9.1 22.6 %collective-permute-start.1 = (f32[512,384]{1,0:T(8,128)}, f32[512,384]{1,0:T(8,128)}, u32[]{:S(2)}, u32[]{:S(2)}) collective-permute-start(f32[512,384]{1,0:T(8,128)} %get-tuple-element.90), channel_id=1, source_target_pairs={{2,0},{3,1},{4,2},{5,3},{6,4},{7,5},{8,6},{9,7},{10,8},{11,9},{12,... | collective-permute-start | bytes 2359304 | tf_op jit(solution)/shard_map/ppermute | solution.py:190
  10.4 21.3 %collective-permute-start = (f32[512,384]{1,0:T(8,128)}, f32[512,384]{1,0:T(8,128)}, u32[]{:S(2)}, u32[]{:S(2)}) collective-permute-start(f32[512,384]{1,0:T(8,128)} %get-tuple-element.91), channel_id=1, source_target_pairs={{0,2},{1,3},{2,4},{3,5},{4,6},{5,7},{6,8},{7,9},{8,10},{9,11},{10,... | collective-permute-start | bytes 2359304 | tf_op jit(solution)/shard_map/ppermute | solution.py:189
  19.1 2.4 copy-start.7
  19.1 2.4 copy-start.19
  24.2 1.8 copy-start.20
  26.0 2.4 copy-start.21
  26.0 2.4 copy-start.26
  28.8 60.0 %collective-permute-start.11 = (f32[4,7,128,128]{3,2,1,0:T(8,128)}, f32[4,7,128,128]{3,2,1,0:T(8,128)}, u32[]{:S(2)}, u32[]{:S(2)}) collective-permute-start(f32[4,7,128,128]{3,2,1,0:T(8,128)} %constant_dynamic-slice_fusion.2), channel_id=1, source_target_pairs={{0,2},{1,3},{2,0},{3,1},{4,6},{5,7},{6,4},{7,5},{8,10},{9,11},{10,... | collective-permute-start | bytes 5505032 | tf_op jit(solution)/shard_map/ppermute | solution.py:105
  29.7 21.3 %collective-permute-start.7 = (f32[512,512]{1,0:T(8,128)}, f32[512,512]{1,0:T(8,128)}, u32[]{:S(2)}, u32[]{:S(2)}) collective-permute-start(f32[512,512]{1,0:T(8,128)} %get-tuple-element.92), channel_id=1, source_target_pairs={{0,2},{1,0},{2,3},{3,1},{5,7},{4,5},{7,6},{6,4},{8,10},{9,8},{10,1... | collective-permute-start | bytes 3145736 | tf_op jit(solution)/shard_map/ppermute | solution.py:125
  30.0 21.0 %collective-permute-start.8 = (f32[512,512]{1,0:T(8,128)S(1)}, f32[512,512]{1,0:T(8,128)}, u32[]{:S(2)}, u32[]{:S(2)}) collective-permute-start(f32[512,512]{1,0:T(8,128)S(1)} %get-tuple-element.93), channel_id=1, source_target_pairs={{1,2},{2,1},{4,7},{7,4},{9,10},{10,9},{12,15},{15,12},{17,18},{18,... | collective-permute-start | bytes 3145736 | tf_op jit(solution)/shard_map/ppermute | solution.py:126
  40.8 7.2 %copy-start.24 = (f32[256,256]{0,1:T(8,128)S(1)}, f32[256,256]{0,1:T(8,128)}, u32[]{:S(2)}) copy-start(f32[256,256]{0,1:T(8,128)} %fusion.2) | copy-start | bytes 786436
  40.8 7.2 %copy-start.25 = (f32[256,16]{1,0:T(8,128)S(1)}, f32[256,16]{1,0:T(8,128)}, u32[]{:S(2)}) copy-start(f32[256,16]{1,0:T(8,128)} %fusion.9) | copy-start | bytes 49156
  43.9 23.4 %collective-permute-start.5 = (f32[512,512]{1,0:T(8,128)}, f32[512,512]{1,0:T(8,128)}, u32[]{:S(2)}, u32[]{:S(2)}) collective-permute-start(f32[512,512]{1,0:T(8,128)} %get-tuple-element.88), channel_id=1, source_target_pairs={{0,2},{1,0},{2,3},{3,1},{5,7},{4,5},{7,6},{6,4},{8,10},{9,8},{10,1... | collective-permute-start | bytes 3145736 | tf_op jit(solution)/shard_map/ppermute | solution.py:125
  46.3 21.0 %collective-permute-start.6 = (f32[512,512]{1,0:T(8,128)}, f32[512,512]{1,0:T(8,128)}, u32[]{:S(2)}, u32[]{:S(2)}) collective-permute-start(f32[512,512]{1,0:T(8,128)} %get-tuple-element.89), channel_id=1, source_target_pairs={{1,2},{2,1},{4,7},{7,4},{9,10},{10,9},{12,15},{15,12},{17,18},{18,... | collective-permute-start | bytes 3145736 | tf_op jit(solution)/shard_map/ppermute | solution.py:126
  50.9 2.2 copy-start.8
  50.9 2.2 copy-start.10
  53.1 3.0 copy-start.13
  56.1 13.1 %copy-start.4 = (f32[1024,512]{1,0:T(8,128)}, f32[1024,512]{1,0:T(8,128)S(1)}, u32[]{:S(2)}) copy-start(f32[1024,512]{1,0:T(8,128)S(1)} %get-tuple-element.43.refs_1_.refs_3_.refs_5_.refs_7_) | copy-start | bytes 6291460
  69.7 151.5 %copy-start.2 = (f32[1024,512]{1,0:T(8,128)}, f32[1024,512]{1,0:T(8,128)S(1)}, u32[]{:S(2)}) copy-start(f32[1024,512]{1,0:T(8,128)S(1)} %maximum_subtract_fusion.refs_0_.refs_2_.refs_1_.refs_3_.refs_4_) | copy-start | bytes 6291460
  71.7 23.6 %collective-permute-start.10 = (f32[1024,384]{1,0:T(8,128)}, f32[1024,384]{1,0:T(8,128)}, u32[]{:S(2)}, u32[]{:S(2)}) collective-permute-start(f32[1024,384]{1,0:T(8,128)} %get-tuple-element.86), channel_id=1, source_target_pairs={{2,0},{1,2},{3,1},{5,3},{7,5},{4,7},{6,4},{8,6},{10,8},{9,10},{11,... | collective-permute-start | bytes 4718600 | tf_op jit(solution)/shard_map/ppermute | solution.py:190
  73.0 22.3 %collective-permute-start.9 = (f32[1024,384]{1,0:T(8,128)}, f32[1024,384]{1,0:T(8,128)}, u32[]{:S(2)}, u32[]{:S(2)}) collective-permute-start(f32[1024,384]{1,0:T(8,128)} %get-tuple-element.87), channel_id=1, source_target_pairs={{0,2},{2,1},{1,3},{3,5},{5,7},{7,4},{4,6},{6,8},{8,10},{10,9},{9,1... | collective-permute-start | bytes 4718600 | tf_op jit(solution)/shard_map/ppermute | solution.py:189
  88.8 3.7 %copy-start.5 = (f32[1024,512]{1,0:T(8,128)S(1)}, f32[1024,512]{1,0:T(8,128)}, u32[]{:S(2)}) copy-start(f32[1024,512]{1,0:T(8,128)} %copy-done.4) | copy-start | bytes 6291460
  92.6 2.7 copy-start.14
  101.4 43.4 %collective-permute-start.12 = (f32[1024,384]{1,0:T(8,128)S(1)}, f32[1024,384]{1,0:T(8,128)S(1)}, u32[]{:S(2)}, u32[]{:S(2)}) collective-permute-start(f32[1024,384]{1,0:T(8,128)S(1)} %get-tuple-element.52), channel_id=1, source_target_pairs={{0,2},{2,1},{1,3},{3,5},{5,7},{7,4},{4,6},{6,8},{8,10},{10,9},{9,1... | collective-permute-start | bytes 4718600 | tf_op jit(solution)/shard_map/ppermute | solution.py:189
  114.1 30.8 %collective-permute-start.13 = (f32[1024,384]{1,0:T(8,128)S(1)}, f32[1024,384]{1,0:T(8,128)S(1)}, u32[]{:S(2)}, u32[]{:S(2)}) collective-permute-start(f32[1024,384]{1,0:T(8,128)S(1)} %get-tuple-element.53), channel_id=1, source_target_pairs={{2,0},{1,2},{3,1},{5,3},{7,5},{4,7},{6,4},{8,6},{10,8},{9,10},{11,... | collective-permute-start | bytes 4718600 | tf_op jit(solution)/shard_map/ppermute | solution.py:190
  141.4 79.9 %copy-start.16 = (f32[32,1,128]{2,1,0:T(1,128)}, f32[32,1,128]{2,1,0:T(1,128)S(1)}, u32[]{:S(2)}) copy-start(f32[32,1,128]{2,1,0:T(1,128)S(1)} %all_to_all.20.refs_0_) | copy-start | bytes 49156
  144.9 76.4 %copy-start.3 = (f32[1024,512]{1,0:T(8,128)}, f32[1024,512]{1,0:T(8,128)S(1)}, u32[]{:S(2)}) copy-start(f32[1024,512]{1,0:T(8,128)S(1)} %get-tuple-element.50.refs_2_.refs_4_.refs_3_.refs_5_) | copy-start | bytes 6291460
  152.7 30.2 %collective-permute-start.14 = (f32[1024,384]{1,0:T(8,128)S(1)}, f32[1024,384]{1,0:T(8,128)S(1)}, u32[]{:S(2)}, u32[]{:S(2)}) collective-permute-start(f32[1024,384]{1,0:T(8,128)S(1)} %get-tuple-element.58), channel_id=1, source_target_pairs={{0,2},{2,1},{1,3},{3,5},{5,7},{7,4},{4,6},{6,8},{8,10},{10,9},{9,1... | collective-permute-start | bytes 4718600 | tf_op jit(solution)/shard_map/ppermute | solution.py:189
  154.5 28.4 %collective-permute-start.15 = (f32[1024,384]{1,0:T(8,128)S(1)}, f32[1024,384]{1,0:T(8,128)S(1)}, u32[]{:S(2)}, u32[]{:S(2)}) collective-permute-start(f32[1024,384]{1,0:T(8,128)S(1)} %get-tuple-element.59), channel_id=1, source_target_pairs={{2,0},{1,2},{3,1},{5,3},{7,5},{4,7},{6,4},{8,6},{10,8},{9,10},{11,... | collective-permute-start | bytes 4718600 | tf_op jit(solution)/shard_map/ppermute | solution.py:190
  179.2 42.2 %copy-start.17 = (f32[32,1,128]{2,1,0:T(1,128)}, f32[32,1,128]{2,1,0:T(1,128)S(1)}, u32[]{:S(2)}) copy-start(f32[32,1,128]{2,1,0:T(1,128)S(1)} %all_to_all.21.refs_1_) | copy-start | bytes 49156
  182.9 38.4 %copy-start.6 = (f32[1024,512]{1,0:T(8,128)}, f32[1024,512]{1,0:T(8,128)S(1)}, u32[]{:S(2)}) copy-start(f32[1024,512]{1,0:T(8,128)S(1)} %get-tuple-element.56.refs_4_.refs_6_.refs_5_) | copy-start | bytes 6291460
  191.4 29.8 %collective-permute-start.16 = (f32[1024,384]{1,0:T(8,128)S(1)}, f32[1024,384]{1,0:T(8,128)S(1)}, u32[]{:S(2)}, u32[]{:S(2)}) collective-permute-start(f32[1024,384]{1,0:T(8,128)S(1)} %get-tuple-element.66), channel_id=1, source_target_pairs={{0,2},{2,1},{1,3},{3,5},{5,7},{7,4},{4,6},{6,8},{8,10},{10,9},{9,1... | collective-permute-start | bytes 4718600 | tf_op jit(solution)/shard_map/ppermute | solution.py:189
  193.3 28.0 %collective-permute-start.17 = (f32[1024,384]{1,0:T(8,128)S(1)}, f32[1024,384]{1,0:T(8,128)S(1)}, u32[]{:S(2)}, u32[]{:S(2)}) collective-permute-start(f32[1024,384]{1,0:T(8,128)S(1)} %get-tuple-element.67), channel_id=1, source_target_pairs={{2,0},{1,2},{3,1},{5,3},{7,5},{4,7},{6,4},{8,6},{10,8},{9,10},{11,... | collective-permute-start | bytes 4718600 | tf_op jit(solution)/shard_map/ppermute | solution.py:190
  217.3 4.1 %copy-start.18 = (f32[32,1,128]{2,1,0:T(1,128)}, f32[32,1,128]{2,1,0:T(1,128)S(1)}, u32[]{:S(2)}) copy-start(f32[32,1,128]{2,1,0:T(1,128)S(1)} %all_to_all.22.refs_2_) | copy-start | bytes 49156
  221.2 9.6 %copy-start.12 = (f32[1024,512]{1,0:T(8,128)}, f32[1024,512]{1,0:T(8,128)S(1)}, u32[]{:S(2)}) copy-start(f32[1024,512]{1,0:T(8,128)S(1)} %get-tuple-element.64.refs_6_.refs_7_) | copy-start | bytes 6291460
  232.2 9.8 %all-to-all-start.3 = ((f32[32,1,128]{2,1,0:T(1,128)}), f32[32,1,128]{2,1,0:T(1,128)S(1)}, u32[]{:S(2)}, u32[]{:S(2)}) async-start(f32[32,1,128]{2,1,0:T(1,128)} %get-tuple-element.70), calls=%async_computation.3 | async-start | bytes 32768 | tf_op jit(solution)/shard_map/all_to_all | solution.py:684
  251.1 5.4 %copy-start.23 = (f32[1024,512]{1,0:T(8,128)S(1)}, f32[1024,512]{1,0:T(8,128)}, u32[]{:S(2)}) copy-start(f32[1024,512]{1,0:T(8,128)} %get-tuple-element.73) | copy-start | bytes 6291460
  254.3 23.1 %collective-permute-start.19 = (f32[512,512]{1,0:T(8,128)}, f32[512,512]{1,0:T(8,128)}, u32[]{:S(2)}, u32[]{:S(2)}) collective-permute-start(f32[512,512]{1,0:T(8,128)} %get-tuple-element.76), channel_id=1, source_target_pairs={{2,0},{0,1},{3,2},{1,3},{7,5},{5,4},{6,7},{4,6},{10,8},{8,9},{11,1... | collective-permute-start | bytes 3145736 | tf_op jit(solution)/shard_map/ppermute | solution.py:152
  254.8 22.6 %collective-permute-start.18 = (f32[512,512]{1,0:T(8,128)}, f32[512,512]{1,0:T(8,128)}, u32[]{:S(2)}, u32[]{:S(2)}) collective-permute-start(f32[512,512]{1,0:T(8,128)} %get-tuple-element.77), channel_id=1, source_target_pairs={{2,1},{1,2},{7,4},{4,7},{10,9},{9,10},{15,12},{12,15},{18,17},{17,... | collective-permute-start | bytes 3145736 | tf_op jit(solution)/shard_map/ppermute | solution.py:153
  257.7 42.1 %collective-permute-start.21 = (f32[512,512]{1,0:T(8,128)}, f32[512,512]{1,0:T(8,128)}, u32[]{:S(2)}, u32[]{:S(2)}) collective-permute-start(f32[512,512]{1,0:T(8,128)} %get-tuple-element.74), channel_id=1, source_target_pairs={{2,0},{0,1},{3,2},{1,3},{7,5},{5,4},{6,7},{4,6},{10,8},{8,9},{11,1... | collective-permute-start | bytes 3145736 | tf_op jit(solution)/shard_map/ppermute | solution.py:152
  259.6 40.2 %collective-permute-start.20 = (f32[512,512]{1,0:T(8,128)S(1)}, f32[512,512]{1,0:T(8,128)}, u32[]{:S(2)}, u32[]{:S(2)}) collective-permute-start(f32[512,512]{1,0:T(8,128)S(1)} %get-tuple-element.75), channel_id=1, source_target_pairs={{2,1},{1,2},{7,4},{4,7},{10,9},{9,10},{15,12},{12,15},{18,17},{17,... | collective-permute-start | bytes 3145736 | tf_op jit(solution)/shard_map/ppermute | solution.py:153
  301.5 1.5 copy-start.1
  (4 other events, 4.5 us)

commit v4 on v3

--- a/solution.py
+++ b/solution.py
@@ -152,8 +152,10 @@
         got_one = lax.ppermute(one, AXES, flipped(chain.first()))
         got_two = lax.ppermute(other, AXES, flipped(chain.second()))
         at_turn = jnp.where(core == turn, same, got_two)
-        return jnp.concatenate(
-            [jnp.where(turn == 0, at_turn, got_one), jnp.where(turn == 0, got_one, at_turn)], axis=1
+        return jnp.where(
+            turn == 0,
+            jnp.concatenate([at_turn, got_one], axis=1),
+            jnp.concatenate([got_one, at_turn], axis=1),
         ).reshape(shape)
     chunks = jnp.zeros((rows, tones * width), field.dtype)
     for s in range(tones):
@@ -455,7 +457,7 @@
 
 def rows_call(kernel, parts, fields, caps, damps, operator, outs, stats, scratch, limit=LIMIT):
     rows, width = fields[0].shape
-    block = min(rows, ROWS)
+    block = min(rows, ROWS if operator else ROWS // 2)
     once = functools.partial(pl.BlockSpec, pipeline_mode=pl.Buffered(1))
 
     def along(shape):

time: 306 us -> 311 us (1.016)
    select_n x2 -> x4, other arithmetic: 3.5 us -> 8.51 us  [the longest x2 6.84 us: scatter_tones(): jnp.where(turn == 0, jnp.concatenate([at_turn, got_one], axis=1), jnp.con...]
where the time goes in v4:
time: 311 us; the launch traced here: 307 us
  blocking collectives  72.1 us (23%)
  Pallas kernels  71.1 us (23%)
  starting transfers between devices  60.1 us (19%)
  waiting for transfers between devices  54 us (17%)
  other arithmetic  22.7 us (7%)
  local copies, waits for them, and re-layouts  20.5 us (7%)
  matrix products  5.09 us (2%)
    all_to_all x3, blocking collectives, per_device(): part = lax.all_to_all(stats, AXES, 0, 0, tiled=True)  72.1 us
    pallas_call x6, Pallas kernels, rows_call(): pl.pallas_call(kernel, grid=(rows // block,), in_specs=specs, out_specs=o...  50.5 us
    ppermute x2, waiting for transfers between devices, scatter_tones(): got_one = lax.ppermute(one, AXES, flipped(chain.first()))  35.5 us
    ppermute x5, starting transfers between devices, halos(): left.insert(0, lax.ppermute(last[:, width - take:], AXES, up(hop)))  35 us
    pallas_call x5, Pallas kernels, columns_call(): pl.pallas_call(kernel, grid=(width // block,), in_specs=specs, out_specs=...  16.8 us
    ppermute x2, waiting for transfers between devices, gather_tones(): got_one = lax.ppermute(one, AXES, chain.first())  11.2 us
    all_to_all x1, waiting for transfers between devices, per_device(): part = lax.all_to_all(stats, AXES, 0, 0, tiled=True)  7.21 us
    select_n x2, other arithmetic, scatter_tones(): jnp.where(turn == 0, jnp.concatenate([at_turn, got_one], axis=1), jnp.con...  6.84 us
  transfers between devices with their start and end apart: 23, of which 4 were waited for; matrix products, arithmetic and copies ran while one was open for 11% of the time, Pallas kernels for 10%

profile of v4, /device:TPU:0, one launch (start us, length us, event | category | flops | bytes accessed | tf_op | source)
XLA Modules:
  0.0 306.9 jit_solution(2890819371570124833)
XLA Ops:
  1.9 2.6 collective-permute-start.2
  6.3 2.8 fusion.32
  10.4 3.9 %collective-permute-start = (f32[512,384]{1,0:T(8,128)}, f32[512,384]{1,0:T(8,128)}, u32[]{:S(2)}, u32[]{:S(2)}) collective-permute-start(f32[512,384]{1,0:T(8,128)} %get-tuple-element.87), channel_id=1, source_target_pairs={{0,2},{1,3},{2,4},{3,5},{4,6},{5,7},{6,8},{7,9},{8,10},{9,11},{10,... | collective-permute-start | bytes 2359304 | tf_op jit(solution)/shard_map/ppermute | solution.py:191
  21.5 2.7 operator.2
  24.2 1.8 copy-done.20
  26.0 1.4 constant_dynamic-slice_fusion.2
  30.0 1.6 collective-permute-start.8
  31.7 9.1 %shard_map.104 = f32[512,1024]{1,0:T(8,128)} custom-call(f32[512,1024]{1,0:T(8,128)} %bitcast.46, f32[512,1024]{1,0:T(8,128)} %bitcast.36, f32[512,384]{1,0:T(8,128)} %collective-permute-done.left, f32[512,384]{1,0:T(8,128)} %collective-permute-done.1.right, f32[1,1024]{1,0:T(1,128)} %bitcast.45, f32[512,1]{1,0:T(8,128)} %reshape.84.damps, ...), custom_call_target="tpu_custom_call" | custom-call | flops 8858370048 | bytes 8388608 | tf_op jit(solution)/shard_map/pallas_call | solution.py:479
  40.8 3.1 %constant_dynamic-slice_fusion.5 = (f32[512,512]{1,0:T(8,128)}, f32[512,512]{1,0:T(8,128)}) fusion(f32[512,1024]{1,0:T(8,128)} %shard_map.104, s32[]{:T(128)S(6)} %select_n.293, s32[]{:T(128)S(6)} %select_n.292), kind=kLoop, calls=%fused_computation.66 | loop fusion | bytes 4194312 | tf_op jit(solution)/shard_map/dynamic_slice | solution.py:123
  43.9 2.4 collective-permute-start.5
  46.3 1.7 collective-permute-start.6
  51.0 1.8 broadcast_select_fusion.1
  53.1 3.0 shard_map.105
  56.1 11.2 %collective-permute-done.5 = f32[512,512]{1,0:T(8,128)} collective-permute-done((f32[512,512]{1,0:T(8,128)}, f32[512,512]{1,0:T(8,128)}, u32[]{:S(2)}, u32[]{:S(2)}) %collective-permute-start.5) | collective-permute-done | bytes 1048608 | tf_op jit(solution)/shard_map/ppermute | solution.py:125
  67.3 1.9 broadcast_select_fusion.3
  69.8 2.0 fusion.31
  73.0 14.7 %collective-permute-start.9 = (f32[1024,384]{1,0:T(8,128)}, f32[1024,384]{1,0:T(8,128)}, u32[]{:S(2)}, u32[]{:S(2)}) collective-permute-start(f32[1024,384]{1,0:T(8,128)} %get-tuple-element.83), channel_id=1, source_target_pairs={{0,2},{2,1},{1,3},{3,5},{5,7},{7,4},{4,6},{6,8},{8,10},{10,9},{9,1... | collective-permute-start | bytes 4718600 | tf_op jit(solution)/shard_map/ppermute | solution.py:191
  88.8 2.5 select_select_fusion.coupling
  92.6 2.7 shard_map.106.refs_1_
  95.3 6.1 %shard_map.107 = (f32[1024,512]{1,0:T(8,128)S(1)}, f32[32,1,128]{2,1,0:T(1,128)S(1)}, f32[1024,384]{1,0:T(8,128)S(1)}, f32[1024,384]{1,0:T(8,128)S(1)}) custom-call(f32[1024,512]{1,0:T(8,128)S(1)} %maximum_subtract_fusion.refs_0_.refs_2_.refs_1_.refs_3_.refs_4_, f32[1024,512]{1,0:T(8,128)S(1)} %shard_map.106.refs_1_, ...), custom_call_target="tpu_custom_call" | custom-call | flops 5637144576 | bytes 8388608 | tf_op jit(solution)/shard_map/pallas_call | solution.py:479
  101.4 12.7 %collective-permute-start.12 = (f32[1024,384]{1,0:T(8,128)S(1)}, f32[1024,384]{1,0:T(8,128)S(1)}, u32[]{:S(2)}, u32[]{:S(2)}) collective-permute-start(f32[1024,384]{1,0:T(8,128)S(1)} %get-tuple-element.52), channel_id=1, source_target_pairs={{0,2},{2,1},{1,3},{3,5},{5,7},{7,4},{4,6},{6,8},{8,10},{10,9},{9,1... | collective-permute-start | bytes 4718600 | tf_op jit(solution)/shard_map/ppermute | solution.py:191
  114.1 1.3 collective-permute-start.13
  115.4 26.0 %all_to_all.20.refs_0_ = f32[32,1,128]{2,1,0:T(1,128)S(1)} all-to-all(f32[32,1,128]{2,1,0:T(1,128)S(1)} %get-tuple-element.48), channel_id=1, replica_groups=mesh['node'=16,'tone'=2] {'node','tone'}, dimensions={0} | all-to-all | bytes 32768 | tf_op jit(solution)/shard_map/all_to_all | solution.py:686
  141.4 3.4 %shard_map.108 = (f32[1024,512]{1,0:T(8,128)S(1)}, f32[1024,512]{1,0:T(8,128)S(1)}) custom-call(f32[32,1,128]{2,1,0:T(1,128)S(1)} %all_to_all.20.refs_0_, f32[1024,512]{1,0:T(8,128)S(1)} %get-tuple-element.49.refs_1_, f32[1024,512]{1,0:T(8,128)S(1)} %maximum_subtract_fusion.refs_0_.refs_2_.refs_1_.refs_3_.refs_4_, f32[1024,512]{1,0:T(8,128)S(1)} %copy-done.5, ...), custom_call_target="tpu_custom_call" | custom-call | flops 1610612736 | bytes 8388608 | tf_op jit(solution)/shard_map/pallas_call | solution.py:361
  144.9 7.8 %shard_map.109 = (f32[1024,512]{1,0:T(8,128)S(1)}, f32[32,1,128]{2,1,0:T(1,128)S(1)}, f32[1024,384]{1,0:T(8,128)S(1)}, f32[1024,384]{1,0:T(8,128)S(1)}, f32[1024...) custom-call(f32[32,1,128]{2,1,0:T(1,128)S(1)} %all_to_all.20.refs_0_, ...), custom_call_target="tpu_custom_call" | custom-call | flops 5637144576 | bytes 14680064 | tf_op jit(solution)/shard_map/pallas_call | solution.py:479
  152.7 1.8 collective-permute-start.14
  154.5 1.3 collective-permute-start.15
  155.8 23.4 %all_to_all.21.refs_1_ = f32[32,1,128]{2,1,0:T(1,128)S(1)} all-to-all(f32[32,1,128]{2,1,0:T(1,128)S(1)} %get-tuple-element.54), channel_id=1, replica_groups=mesh['node'=16,'tone'=2] {'node','tone'}, dimensions={0} | all-to-all | bytes 32768 | tf_op jit(solution)/shard_map/all_to_all | solution.py:686
  179.2 3.7 %shard_map.110 = (f32[1024,512]{1,0:T(8,128)S(1)}, f32[1024,512]{1,0:T(8,128)S(1)}) custom-call(f32[32,1,128]{2,1,0:T(1,128)S(1)} %all_to_all.20.refs_0_, f32[32,1,128]{2,1,0:T(1,128)S(1)} %all_to_all.21.refs_1_, f32[1024,512]{1,0:T(8,128)S(1)} %get-tuple-element.55.refs_2_, f32[1024,512]{1,0:T(8,128)S(1)} %maximum_subtract_fusion.refs_0_.refs_2_.refs_1_.refs_3_.refs_4_, ...), custom_call_target="tpu_custom_call" | custom-call | flops 1610612736 | bytes 8388608 | tf_op jit(solution)/shard_map/pallas_call | solution.py:361
  182.9 8.5 %shard_map.111 = (f32[1024,512]{1,0:T(8,128)S(1)}, f32[32,1,128]{2,1,0:T(1,128)S(1)}, f32[1024,384]{1,0:T(8,128)S(1)}, f32[1024,384]{1,0:T(8,128)S(1)}, f32[1024...) custom-call(f32[32,1,128]{2,1,0:T(1,128)S(1)} %all_to_all.20.refs_0_, f32[32,1,128]{2,1,0:T(1,128)S(1)} %all_to_all.21.refs_1_, ...), custom_call_target="tpu_custom_call" | custom-call | flops 5637144576 | bytes 20971520 | tf_op jit(solution)/shard_map/pallas_call | solution.py:479
  191.4 1.8 collective-permute-start.16
  193.3 1.3 collective-permute-start.17
  194.6 22.7 %all_to_all.22.refs_2_ = f32[32,1,128]{2,1,0:T(1,128)S(1)} all-to-all(f32[32,1,128]{2,1,0:T(1,128)S(1)} %get-tuple-element.62), channel_id=1, replica_groups=mesh['node'=16,'tone'=2] {'node','tone'}, dimensions={0} | all-to-all | bytes 32768 | tf_op jit(solution)/shard_map/all_to_all | solution.py:686
  217.3 4.0 %shard_map.112 = (f32[1024,512]{1,0:T(8,128)S(1)}, f32[1024,512]{1,0:T(8,128)S(1)}) custom-call(f32[32,1,128]{2,1,0:T(1,128)S(1)} %all_to_all.20.refs_0_, f32[32,1,128]{2,1,0:T(1,128)S(1)} %all_to_all.21.refs_1_, f32[32,1,128]{2,1,0:T(1,128)S(1)} %all_to_all.22.refs_2_, f32[1024,512]{1,0:T(8,128)S(1)} %get-tuple-element.63.refs_3_, ...), custom_call_target="tpu_custom_call" | custom-call | flops 1610612736 | bytes 8388608 | tf_op jit(solution)/shard_map/pallas_call | solution.py:361
  221.4 9.5 %shard_map.113 = (f32[1024,512]{1,0:T(8,128)S(1)}, f32[32,1,128]{2,1,0:T(1,128)}) custom-call(f32[32,1,128]{2,1,0:T(1,128)S(1)} %all_to_all.20.refs_0_, f32[32,1,128]{2,1,0:T(1,128)S(1)} %all_to_all.21.refs_1_, f32[32,1,128]{2,1,0:T(1,128)S(1)} %all_to_all.22.refs_2_, f32[1024,512]{1,0:T(8,128)S(1)} %maximum_subtract_fusion.refs_0_.refs_2_.refs_1_.refs_3_.refs_4_, ...), custom_call_target="tpu_custom_call" | custom-call | flops 5637144576 | bytes 27262976 | tf_op jit(solution)/shard_map/pallas_call | solution.py:479
  230.8 1.4 copy-done.15
  232.2 2.6 all-to-all-start.3
  234.8 7.2 %all-to-all-done.3.refs_3_ = f32[32,1,128]{2,1,0:T(1,128)S(1)} async-done(((f32[32,1,128]{2,1,0:T(1,128)}), f32[32,1,128]{2,1,0:T(1,128)S(1)}, u32[]{:S(2)}, u32[]{:S(2)}) %all-to-all-start.3) | async-done | bytes 16416 | tf_op jit(solution)/shard_map/all_to_all | solution.py:686
  242.7 9.5 %shard_map.114 = (f32[1024,512]{1,0:T(8,128)}, f32[1024,512]{1,0:T(8,128)}) custom-call(f32[32,1,128]{2,1,0:T(1,128)} %copy-done.16, f32[32,1,128]{2,1,0:T(1,128)} %copy-done.17, f32[32,1,128]{2,1,0:T(1,128)} %copy-done.18, f32[32,1,128]{2,1,0:T(1,128)} %copy-done.27, f32[1024,512]{1,0:T(8,128)} %copy-done.2, f32[1024,512]{1,0:T(8,128)} %copy-done.3, ...), custom_call_target="tpu_custom_call" | custom-call | flops 8388608 | bytes 12582912 | tf_op jit(solution)/shard_map/pallas_call | solution.py:479
  252.1 3.3 %dynamic-slice_select_fusion.2 = (f32[512,512]{1,0:T(8,128)}, f32[512,512]{1,0:T(8,128)}) fusion(f32[1024,512]{1,0:T(8,128)} %get-tuple-element.72, s32[]{:T(128)S(6)} %select_n.313, pred[]{:T(512)S(6)} %eq.136, s32[]{:T(128)S(6)} %select_n.314), kind=kLoop, calls=%fused_computation.15 | loop fusion | flops 262144 | bytes 4194313 | tf_op jit(solution)/shard_map/jit(_where)/select_n | solution.py:151
  255.4 1.6 collective-permute-start.18
  257.0 1.7 collective-permute-start.19
  260.0 1.7 collective-permute-start.20
  262.9 1.4 dynamic-slice_select_fusion.3
  264.3 18.3 %collective-permute-done.19 = f32[512,512]{1,0:T(8,128)} collective-permute-done((f32[512,512]{1,0:T(8,128)}, f32[512,512]{1,0:T(8,128)}, u32[]{:S(2)}, u32[]{:S(2)}) %collective-permute-start.19) | collective-permute-done | bytes 1048608 | tf_op jit(solution)/shard_map/ppermute | solution.py:152
  282.7 3.4 %maximum_select_fusion = f32[32,16,1024]{2,1,0:T(8,128)} fusion(f32[32,16,512]{2,1,0:T(8,128)} %bitcast.12, f32[32,16,512]{2,1,0:T(8,128)S(1)} %bitcast.39, pred[]{:T(512)S(6)} %eq.135), kind=kLoop, calls=%fused_computation.2 | loop fusion | flops 1572864 | bytes 4194305 | tf_op jit(solution)/shard_map/jit(_where)/select_n | solution.py:155
  286.3 17.1 %collective-permute-done.21 = f32[512,512]{1,0:T(8,128)} collective-permute-done((f32[512,512]{1,0:T(8,128)S(1)}, f32[512,512]{1,0:T(8,128)}, u32[]{:S(2)}, u32[]{:S(2)}) %collective-permute-start.21) | collective-permute-done | bytes 1048608 | tf_op jit(solution)/shard_map/ppermute | solution.py:152
  303.4 3.4 %maximum_select_fusion.1 = f32[32,16,1024]{2,1,0:T(8,128)} fusion(f32[32,16,512]{2,1,0:T(8,128)} %bitcast.14, f32[32,16,512]{2,1,0:T(8,128)S(1)} %bitcast.38, pred[]{:T(512)S(6)} %eq.135), kind=kLoop, calls=%fused_computation.3 | loop fusion | flops 1572864 | bytes 4194305 | tf_op jit(solution)/shard_map/jit(_where)/select_n | solution.py:155
  (124 shorter events, 24.7 us)
Async XLA Ops:
  0.6 3.9 %copy-start = (f32[3,4]{1,0:T(4,128)S(1)}, f32[3,4]{1,0:T(4,128)}, u32[]{:S(2)}) copy-start(f32[3,4]{1,0:T(4,128)} %param.17) | copy-start | bytes 148
  0.6 13.6 %copy-start.28 = (f32[32,16]{0,1:T(8,128)S(1)}, f32[32,16]{0,1:T(8,128)}, u32[]{:S(2)}) copy-start(f32[32,16]{0,1:T(8,128)} %param.15) | copy-start | bytes 6148
  1.4 27.4 %collective-permute-start.3 = (f32[4,7]{1,0:T(4,128)S(1)}, f32[4,7]{1,0:T(4,128)S(1)}, u32[]{:S(2)}, u32[]{:S(2)}) collective-permute-start(f32[4,7]{1,0:T(4,128)S(1)} %constant_dynamic-slice_fusion.8), channel_id=1, source_target_pairs={{0,2},{1,3},{2,0},{3,1},{4,6},{5,7},{6,4},{7,5},{8,10},{9,11},{10,... | collective-permute-start | bytes 344 | tf_op jit(solution)/shard_map/ppermute | solution.py:105
  1.9 27.8 %collective-permute-start.2 = (f32[32,16]{0,1:T(8,128)}, f32[32,16]{0,1:T(8,128)S(1)}, u32[]{:S(2)}, u32[]{:S(2)}) collective-permute-start(f32[32,16]{0,1:T(8,128)} %param.15), channel_id=1, source_target_pairs={{0,1},{1,0},{2,3},{3,2},{4,5},{5,4},{6,7},{7,6},{8,9},{9,8},{10,11... | collective-permute-start | bytes 6152 | tf_op jit(solution)/shard_map/ppermute | solution.py:613
  6.1 23.9 %collective-permute-start.4 = (f32[8,512]{1,0:T(8,128)S(1)}, f32[8,512]{1,0:T(8,128)S(1)}, u32[]{:S(2)}, u32[]{:S(2)}) collective-permute-start(f32[8,512]{1,0:T(8,128)S(1)} %constant_dynamic-slice_fusion.7), channel_id=1, source_target_pairs={{0,2},{1,3},{2,0},{3,1},{4,6},{5,7},{6,4},{7,5},{8,10},{9,11},{10,... | collective-permute-start | bytes 49160 | tf_op jit(solution)/shard_map/ppermute | solution.py:105
  6.3 12.8 %copy-start.22 = (f32[32,16,1024]{2,1,0:T(8,128)S(1)}, f32[32,16,1024]{2,1,0:T(8,128)}, u32[]{:S(2)}) copy-start(f32[32,16,1024]{2,1,0:T(8,128)} %param.9) | copy-start | bytes 6291460
  9.1 22.6 %collective-permute-start.1 = (f32[512,384]{1,0:T(8,128)}, f32[512,384]{1,0:T(8,128)}, u32[]{:S(2)}, u32[]{:S(2)}) collective-permute-start(f32[512,384]{1,0:T(8,128)} %get-tuple-element.86), channel_id=1, source_target_pairs={{2,0},{3,1},{4,2},{5,3},{6,4},{7,5},{8,6},{9,7},{10,8},{11,9},{12,... | collective-permute-start | bytes 2359304 | tf_op jit(solution)/shard_map/ppermute | solution.py:192
  10.4 21.3 %collective-permute-start = (f32[512,384]{1,0:T(8,128)}, f32[512,384]{1,0:T(8,128)}, u32[]{:S(2)}, u32[]{:S(2)}) collective-permute-start(f32[512,384]{1,0:T(8,128)} %get-tuple-element.87), channel_id=1, source_target_pairs={{0,2},{1,3},{2,4},{3,5},{4,6},{5,7},{6,8},{7,9},{8,10},{9,11},{10,... | collective-permute-start | bytes 2359304 | tf_op jit(solution)/shard_map/ppermute | solution.py:191
  19.1 2.4 copy-start.7
  19.1 2.4 copy-start.19
  24.2 1.8 copy-start.20
  26.0 2.4 copy-start.21
  26.0 2.4 copy-start.26
  28.8 60.0 %collective-permute-start.11 = (f32[4,7,128,128]{3,2,1,0:T(8,128)}, f32[4,7,128,128]{3,2,1,0:T(8,128)}, u32[]{:S(2)}, u32[]{:S(2)}) collective-permute-start(f32[4,7,128,128]{3,2,1,0:T(8,128)} %constant_dynamic-slice_fusion.2), channel_id=1, source_target_pairs={{0,2},{1,3},{2,0},{3,1},{4,6},{5,7},{6,4},{7,5},{8,10},{9,11},{10,... | collective-permute-start | bytes 5505032 | tf_op jit(solution)/shard_map/ppermute | solution.py:105
  29.7 21.2 %collective-permute-start.7 = (f32[512,512]{1,0:T(8,128)}, f32[512,512]{1,0:T(8,128)}, u32[]{:S(2)}, u32[]{:S(2)}) collective-permute-start(f32[512,512]{1,0:T(8,128)} %get-tuple-element.88), channel_id=1, source_target_pairs={{0,2},{1,0},{2,3},{3,1},{5,7},{4,5},{7,6},{6,4},{8,10},{9,8},{10,1... | collective-permute-start | bytes 3145736 | tf_op jit(solution)/shard_map/ppermute | solution.py:125
  30.0 20.9 %collective-permute-start.8 = (f32[512,512]{1,0:T(8,128)S(1)}, f32[512,512]{1,0:T(8,128)}, u32[]{:S(2)}, u32[]{:S(2)}) collective-permute-start(f32[512,512]{1,0:T(8,128)S(1)} %get-tuple-element.89), channel_id=1, source_target_pairs={{1,2},{2,1},{4,7},{7,4},{9,10},{10,9},{12,15},{15,12},{17,18},{18,... | collective-permute-start | bytes 3145736 | tf_op jit(solution)/shard_map/ppermute | solution.py:126
  40.8 7.2 %copy-start.24 = (f32[256,256]{0,1:T(8,128)S(1)}, f32[256,256]{0,1:T(8,128)}, u32[]{:S(2)}) copy-start(f32[256,256]{0,1:T(8,128)} %fusion.2) | copy-start | bytes 786436
  40.8 7.2 %copy-start.25 = (f32[256,16]{1,0:T(8,128)S(1)}, f32[256,16]{1,0:T(8,128)}, u32[]{:S(2)}) copy-start(f32[256,16]{1,0:T(8,128)} %fusion.9) | copy-start | bytes 49156
  43.9 23.4 %collective-permute-start.5 = (f32[512,512]{1,0:T(8,128)}, f32[512,512]{1,0:T(8,128)}, u32[]{:S(2)}, u32[]{:S(2)}) collective-permute-start(f32[512,512]{1,0:T(8,128)} %get-tuple-element.84), channel_id=1, source_target_pairs={{0,2},{1,0},{2,3},{3,1},{5,7},{4,5},{7,6},{6,4},{8,10},{9,8},{10,1... | collective-permute-start | bytes 3145736 | tf_op jit(solution)/shard_map/ppermute | solution.py:125
  46.3 21.0 %collective-permute-start.6 = (f32[512,512]{1,0:T(8,128)}, f32[512,512]{1,0:T(8,128)}, u32[]{:S(2)}, u32[]{:S(2)}) collective-permute-start(f32[512,512]{1,0:T(8,128)} %get-tuple-element.85), channel_id=1, source_target_pairs={{1,2},{2,1},{4,7},{7,4},{9,10},{10,9},{12,15},{15,12},{17,18},{18,... | collective-permute-start | bytes 3145736 | tf_op jit(solution)/shard_map/ppermute | solution.py:126
  50.9 2.2 copy-start.8
  50.9 2.2 copy-start.10
  53.1 3.0 copy-start.13
  56.1 13.2 %copy-start.4 = (f32[1024,512]{1,0:T(8,128)}, f32[1024,512]{1,0:T(8,128)S(1)}, u32[]{:S(2)}) copy-start(f32[1024,512]{1,0:T(8,128)S(1)} %get-tuple-element.43.refs_1_.refs_3_.refs_5_.refs_7_) | copy-start | bytes 6291460
  69.8 151.5 %copy-start.2 = (f32[1024,512]{1,0:T(8,128)}, f32[1024,512]{1,0:T(8,128)S(1)}, u32[]{:S(2)}) copy-start(f32[1024,512]{1,0:T(8,128)S(1)} %maximum_subtract_fusion.refs_0_.refs_2_.refs_1_.refs_3_.refs_4_) | copy-start | bytes 6291460
  71.8 23.5 %collective-permute-start.10 = (f32[1024,384]{1,0:T(8,128)}, f32[1024,384]{1,0:T(8,128)}, u32[]{:S(2)}, u32[]{:S(2)}) collective-permute-start(f32[1024,384]{1,0:T(8,128)} %get-tuple-element.82), channel_id=1, source_target_pairs={{2,0},{1,2},{3,1},{5,3},{7,5},{4,7},{6,4},{8,6},{10,8},{9,10},{11,... | collective-permute-start | bytes 4718600 | tf_op jit(solution)/shard_map/ppermute | solution.py:192
  73.0 22.3 %collective-permute-start.9 = (f32[1024,384]{1,0:T(8,128)}, f32[1024,384]{1,0:T(8,128)}, u32[]{:S(2)}, u32[]{:S(2)}) collective-permute-start(f32[1024,384]{1,0:T(8,128)} %get-tuple-element.83), channel_id=1, source_target_pairs={{0,2},{2,1},{1,3},{3,5},{5,7},{7,4},{4,6},{6,8},{8,10},{10,9},{9,1... | collective-permute-start | bytes 4718600 | tf_op jit(solution)/shard_map/ppermute | solution.py:191
  88.8 3.7 %copy-start.5 = (f32[1024,512]{1,0:T(8,128)S(1)}, f32[1024,512]{1,0:T(8,128)}, u32[]{:S(2)}) copy-start(f32[1024,512]{1,0:T(8,128)} %copy-done.4) | copy-start | bytes 6291460
  92.6 2.7 copy-start.14
  101.4 43.5 %collective-permute-start.12 = (f32[1024,384]{1,0:T(8,128)S(1)}, f32[1024,384]{1,0:T(8,128)S(1)}, u32[]{:S(2)}, u32[]{:S(2)}) collective-permute-start(f32[1024,384]{1,0:T(8,128)S(1)} %get-tuple-element.52), channel_id=1, source_target_pairs={{0,2},{2,1},{1,3},{3,5},{5,7},{7,4},{4,6},{6,8},{8,10},{10,9},{9,1... | collective-permute-start | bytes 4718600 | tf_op jit(solution)/shard_map/ppermute | solution.py:191
  114.1 30.8 %collective-permute-start.13 = (f32[1024,384]{1,0:T(8,128)S(1)}, f32[1024,384]{1,0:T(8,128)S(1)}, u32[]{:S(2)}, u32[]{:S(2)}) collective-permute-start(f32[1024,384]{1,0:T(8,128)S(1)} %get-tuple-element.53), channel_id=1, source_target_pairs={{2,0},{1,2},{3,1},{5,3},{7,5},{4,7},{6,4},{8,6},{10,8},{9,10},{11,... | collective-permute-start | bytes 4718600 | tf_op jit(solution)/shard_map/ppermute | solution.py:192
  141.4 79.9 %copy-start.16 = (f32[32,1,128]{2,1,0:T(1,128)}, f32[32,1,128]{2,1,0:T(1,128)S(1)}, u32[]{:S(2)}) copy-start(f32[32,1,128]{2,1,0:T(1,128)S(1)} %all_to_all.20.refs_0_) | copy-start | bytes 49156
  144.9 76.4 %copy-start.3 = (f32[1024,512]{1,0:T(8,128)}, f32[1024,512]{1,0:T(8,128)S(1)}, u32[]{:S(2)}) copy-start(f32[1024,512]{1,0:T(8,128)S(1)} %get-tuple-element.50.refs_2_.refs_4_.refs_3_.refs_5_) | copy-start | bytes 6291460
  152.7 30.2 %collective-permute-start.14 = (f32[1024,384]{1,0:T(8,128)S(1)}, f32[1024,384]{1,0:T(8,128)S(1)}, u32[]{:S(2)}, u32[]{:S(2)}) collective-permute-start(f32[1024,384]{1,0:T(8,128)S(1)} %get-tuple-element.58), channel_id=1, source_target_pairs={{0,2},{2,1},{1,3},{3,5},{5,7},{7,4},{4,6},{6,8},{8,10},{10,9},{9,1... | collective-permute-start | bytes 4718600 | tf_op jit(solution)/shard_map/ppermute | solution.py:191
  154.5 28.4 %collective-permute-start.15 = (f32[1024,384]{1,0:T(8,128)S(1)}, f32[1024,384]{1,0:T(8,128)S(1)}, u32[]{:S(2)}, u32[]{:S(2)}) collective-permute-start(f32[1024,384]{1,0:T(8,128)S(1)} %get-tuple-element.59), channel_id=1, source_target_pairs={{2,0},{1,2},{3,1},{5,3},{7,5},{4,7},{6,4},{8,6},{10,8},{9,10},{11,... | collective-permute-start | bytes 4718600 | tf_op jit(solution)/shard_map/ppermute | solution.py:192
  179.2 42.2 %copy-start.17 = (f32[32,1,128]{2,1,0:T(1,128)}, f32[32,1,128]{2,1,0:T(1,128)S(1)}, u32[]{:S(2)}) copy-start(f32[32,1,128]{2,1,0:T(1,128)S(1)} %all_to_all.21.refs_1_) | copy-start | bytes 49156
  182.9 38.4 %copy-start.6 = (f32[1024,512]{1,0:T(8,128)}, f32[1024,512]{1,0:T(8,128)S(1)}, u32[]{:S(2)}) copy-start(f32[1024,512]{1,0:T(8,128)S(1)} %get-tuple-element.56.refs_4_.refs_6_.refs_5_) | copy-start | bytes 6291460
  191.4 29.8 %collective-permute-start.16 = (f32[1024,384]{1,0:T(8,128)S(1)}, f32[1024,384]{1,0:T(8,128)S(1)}, u32[]{:S(2)}, u32[]{:S(2)}) collective-permute-start(f32[1024,384]{1,0:T(8,128)S(1)} %get-tuple-element.66), channel_id=1, source_target_pairs={{0,2},{2,1},{1,3},{3,5},{5,7},{7,4},{4,6},{6,8},{8,10},{10,9},{9,1... | collective-permute-start | bytes 4718600 | tf_op jit(solution)/shard_map/ppermute | solution.py:191
  193.3 28.0 %collective-permute-start.17 = (f32[1024,384]{1,0:T(8,128)S(1)}, f32[1024,384]{1,0:T(8,128)S(1)}, u32[]{:S(2)}, u32[]{:S(2)}) collective-permute-start(f32[1024,384]{1,0:T(8,128)S(1)} %get-tuple-element.67), channel_id=1, source_target_pairs={{2,0},{1,2},{3,1},{5,3},{7,5},{4,7},{6,4},{8,6},{10,8},{9,10},{11,... | collective-permute-start | bytes 4718600 | tf_op jit(solution)/shard_map/ppermute | solution.py:192
  217.3 4.1 %copy-start.18 = (f32[32,1,128]{2,1,0:T(1,128)}, f32[32,1,128]{2,1,0:T(1,128)S(1)}, u32[]{:S(2)}) copy-start(f32[32,1,128]{2,1,0:T(1,128)S(1)} %all_to_all.22.refs_2_) | copy-start | bytes 49156
  221.3 9.6 %copy-start.12 = (f32[1024,512]{1,0:T(8,128)}, f32[1024,512]{1,0:T(8,128)S(1)}, u32[]{:S(2)}) copy-start(f32[1024,512]{1,0:T(8,128)S(1)} %get-tuple-element.64.refs_6_.refs_7_) | copy-start | bytes 6291460
  232.2 9.8 %all-to-all-start.3 = ((f32[32,1,128]{2,1,0:T(1,128)}), f32[32,1,128]{2,1,0:T(1,128)S(1)}, u32[]{:S(2)}, u32[]{:S(2)}) async-start(f32[32,1,128]{2,1,0:T(1,128)} %get-tuple-element.70), calls=%async_computation.3 | async-start | bytes 32768 | tf_op jit(solution)/shard_map/all_to_all | solution.py:686
  252.1 6.6 %copy-start.23 = (f32[1024,512]{1,0:T(8,128)S(1)}, f32[1024,512]{1,0:T(8,128)}, u32[]{:S(2)}) copy-start(f32[1024,512]{1,0:T(8,128)} %get-tuple-element.73) | copy-start | bytes 6291460
  255.4 7.5 %collective-permute-start.18 = (f32[512,512]{1,0:T(8,128)}, f32[512,512]{1,0:T(8,128)}, u32[]{:S(2)}, u32[]{:S(2)}) collective-permute-start(f32[512,512]{1,0:T(8,128)} %get-tuple-element.77), channel_id=1, source_target_pairs={{2,1},{1,2},{7,4},{4,7},{10,9},{9,10},{15,12},{12,15},{18,17},{17,... | collective-permute-start | bytes 3145736 | tf_op jit(solution)/shard_map/ppermute | solution.py:153
  257.0 25.6 %collective-permute-start.19 = (f32[512,512]{1,0:T(8,128)}, f32[512,512]{1,0:T(8,128)}, u32[]{:S(2)}, u32[]{:S(2)}) collective-permute-start(f32[512,512]{1,0:T(8,128)} %get-tuple-element.76), channel_id=1, source_target_pairs={{2,0},{0,1},{3,2},{1,3},{7,5},{5,4},{6,7},{4,6},{10,8},{8,9},{11,1... | collective-permute-start | bytes 3145736 | tf_op jit(solution)/shard_map/ppermute | solution.py:152
  260.0 26.0 %collective-permute-start.20 = (f32[512,512]{1,0:T(8,128)}, f32[512,512]{1,0:T(8,128)}, u32[]{:S(2)}, u32[]{:S(2)}) collective-permute-start(f32[512,512]{1,0:T(8,128)} %get-tuple-element.75), channel_id=1, source_target_pairs={{2,1},{1,2},{7,4},{4,7},{10,9},{9,10},{15,12},{12,15},{18,17},{17,... | collective-permute-start | bytes 3145736 | tf_op jit(solution)/shard_map/ppermute | solution.py:153
  261.7 41.7 %collective-permute-start.21 = (f32[512,512]{1,0:T(8,128)S(1)}, f32[512,512]{1,0:T(8,128)}, u32[]{:S(2)}, u32[]{:S(2)}) collective-permute-start(f32[512,512]{1,0:T(8,128)S(1)} %get-tuple-element.74), channel_id=1, source_target_pairs={{2,0},{0,1},{3,2},{1,3},{7,5},{5,4},{6,7},{4,6},{10,8},{8,9},{11,1... | collective-permute-start | bytes 3145736 | tf_op jit(solution)/shard_map/ppermute | solution.py:152
  303.4 3.4 %copy-start.1 = (f32[3,4]{1,0:T(4,128)S(1)}, f32[3,4]{1,0:T(4,128)}, u32[]{:S(2)}) copy-start(f32[3,4]{1,0:T(4,128)} %param.17) | copy-start | bytes 148
  (4 other events, 4.5 us)
